TPU v7x, 8 devices: a whole 2x2x1 slice. The times are simulated.
8 devices in a mesh: tp: 2 (over z, y), dp: 4 (over x, core).
Axes of the slice: x: 2, y: 2, z: 1, core: 2. Of those that a mesh axis runs over, the one named last changes fastest.
Arguments:
- hidden: bfloat16 [4, 1024, 576], P('dp')
- norm_w: bfloat16 [576], replicated
- embed: bfloat16 [49152, 576], P('tp')
- targets: int32 [4, 1024], P('dp')
- loss_mask: int32 [4, 1024], P('dp')
- token_ids: int32 [4, 1024], P('dp')
- grad_embed: bfloat16 [4, 1024, 576], P('dp')
Outputs:
- output 1: float32 [], replicated
- output 2: bfloat16 [4, 1024, 576], P('dp')
- output 3: float32 [576], replicated
- output 4: float32 [49152, 576], P('tp', 'dp')
All inputs are finite; a program needn't handle non-finite values.
Results may differ from a plain program's by a relative error of at most 0.001.
Values sent between devices are 32-bit elements.
A program may use at most 1 GiB of HBM per device.

v0:
```python
import jax
import jax.numpy as jnp
from jax import lax
from jax.sharding import PartitionSpec as P

RMS_EPS = 1e-6


def solution(mesh):
    def local_step(hidden, norm_w, embed, targets, loss_mask, token_ids, grad_embed):
        batch_local, seq_len, d_model = hidden.shape
        vocab_local = embed.shape[0]
        tokens = batch_local * seq_len
        vocab_start = lax.axis_index("tp") * vocab_local
        hidden32 = hidden.reshape(tokens, d_model).astype(jnp.float32)
        inv_rms = lax.rsqrt(jnp.mean(hidden32 * hidden32, axis=-1, keepdims=True) + RMS_EPS)
        unit_rows = hidden32 * inv_rms
        norm_gain = norm_w.astype(jnp.float32)
        z_rows = (unit_rows * norm_gain).astype(jnp.bfloat16)
        logits = jnp.einsum("td,vd->tv", z_rows, embed, preferred_element_type=jnp.float32)
        row_max = lax.pmax(jnp.max(logits, axis=-1, keepdims=True), "tp")
        shifted = jnp.exp(logits - row_max)
        sum_exp = lax.psum(jnp.sum(shifted, axis=-1, keepdims=True), "tp")
        is_target = jnp.arange(vocab_local)[None, :] == (targets.reshape(tokens, 1) - vocab_start)
        target_logit = lax.psum(jnp.sum(jnp.where(is_target, logits, 0.0), axis=-1, keepdims=True), "tp")
        log_norm = row_max + jnp.log(sum_exp)
        mask_rows = loss_mask.reshape(tokens, 1).astype(jnp.float32)
        token_count = lax.psum(jnp.sum(mask_rows), "dp")
        loss_val = lax.psum(jnp.sum(mask_rows * (log_norm - target_logit)), "dp") / token_count
        soft_probs = shifted / sum_exp
        dlogits = (jnp.where(is_target, soft_probs - 1.0, soft_probs) * (mask_rows / token_count)).astype(jnp.bfloat16)
        grad_z = lax.psum(jnp.dot(dlogits, embed, preferred_element_type=jnp.float32), "tp")
        head_grad = jnp.einsum("tv,td->vd", dlogits, z_rows, preferred_element_type=jnp.float32)
        head_grad = lax.psum_scatter(head_grad, "dp", scatter_dimension=1, tiled=True)
        local_ids = token_ids.reshape(tokens) - vocab_start
        local_ids = jnp.where((local_ids >= 0) & (local_ids < vocab_local), local_ids, vocab_local)
        lookup_grad = jax.ops.segment_sum(grad_embed.reshape(tokens, d_model).astype(jnp.float32), local_ids, num_segments=vocab_local)
        lookup_grad = lax.psum_scatter(lookup_grad, "dp", scatter_dimension=1, tiled=True)
        grad_gain = lax.psum(jnp.sum(grad_z * unit_rows, axis=0), "dp")
        grad_unit = grad_z * norm_gain
        grad_hidden = inv_rms * (grad_unit - unit_rows * jnp.mean(grad_unit * unit_rows, axis=-1, keepdims=True))
        return (loss_val, grad_hidden.astype(jnp.bfloat16).reshape(batch_local, seq_len, d_model), grad_gain, head_grad + lookup_grad)

    return jax.shard_map(local_step, mesh=mesh, in_specs=(P("dp"), P(), P("tp"), P("dp"), P("dp"), P("dp"), P("dp")), out_specs=(P(), P("dp"), P(), P("tp", "dp")), check_vma=False)
```

profile of v0, /device:TPU:0, one launch (start us, length us, event | category | flops | bytes accessed | tf_op | source)
XLA Modules:
  0.0 875.8 jit_solution(4407244641180741639)
XLA Ops:
  8.0 1.5 fusion.13
  9.6 0.7 convert_element_type.46
  10.9 1.6 fusion.17.clone.4
  12.5 52.4 %fusion.19 = (f32[1024]{0:T(1024)S(1)}, f32[1024,24576]{1,0:T(8,128)}) fusion(bf16[24576,576]{0,1:T(8,128)(2,1)} %param.9, bf16[1024,576]{0,1:T(8,128)(2,1)S(1)} %fusion.17.clone.4), kind=kOutput, calls=%fused_computation.33 | convolution fusion | flops 29016195072 | bytes 130158592 | tf_op jit(solution)/shard_map/td,vd->tv/dot_general | solution.py:20
  64.9 6.2 pmax.7
  71.1 0.6 convert_reduce_fusion
  71.7 6.5 psum.45
  78.9 36.6 %fusion.2 = (f32[1024]{0:T(1024)S(1)}, f32[1024]{0:T(1024)S(1)}) fusion(f32[1024,24576]{1,0:T(8,128)} %get-tuple-element.13, f32[1024]{0:T(1024)S(1)} %bitcast.42, s32[1024]{0:T(1024)S(1)} %bitcast.44), kind=kLoop, calls=%fused_computation.7 | loop fusion | flops 125827072 | bytes 100679680 | tf_op jit(solution)/shard_map/reduce_sum | solution.py:23
  115.5 5.6 all-reduce.1
  121.1 49.3 %fusion.1 = bf16[1024,24576]{1,0:T(8,128)(2,1)} fusion(f32[1024,24576]{1,0:T(8,128)} %get-tuple-element.13, f32[1024]{0:T(1024)S(1)} %bitcast.46, f32[1024]{0:T(1024)S(1)} %bitcast.47, s32[1024]{0:T(1024)S(1)} %bitcast.45, f32[1024]{0:T(1024)S(1)} %bitcast.43), kind=kLoop, calls=%fused_computation.3 | loop fusion | flops 176160768 | bytes 151011328 | tf_op jit(solution)/shard_map/convert_element_type | solution.py:31
  170.4 38.4 %fusion.20 = f32[1024,576]{0,1:T(8,128)} fusion(bf16[1024,24576]{1,0:T(8,128)(2,1)} %fusion.1, bf16[24576,576]{0,1:T(8,128)(2,1)} %param.9), kind=kOutput, calls=%fused_computation.34 | convolution fusion | flops 28991029248 | bytes 81002496 | tf_op jit(solution)/shard_map/dot_general | solution.py:32
  209.2 0.9 copy-done.2
  210.1 1.7 bitcast_convert_fusion
  211.8 2.5 copy.11
  214.4 20.2 %broadcast_in_dim.28 = f32[24576,576]{1,0:T(8,128)} broadcast(f32[]{:T(128)} %constant.9.clone.1), dimensions={} | broadcast | bytes 56623108 | tf_op jit(solution)/shard_map/broadcast_in_dim | solution.py:37
  234.6 126.2 %scatter_fusion = f32[24576,576]{1,0:T(8,128)} fusion(f32[24576,576]{1,0:T(8,128)} %broadcast_in_dim.28, s32[1024]{0:T(1024)S(1)} %bitcast.48, f32[1024,576]{1,0:T(8,128)S(1)} %copy.11), kind=kCustom, calls=%fused_computation | custom fusion | flops 589824 | bytes 7081984 | tf_op jit(solution)/shard_map/scatter-add | solution.py:37
  360.8 58.7 %copy.12 = f32[24576,576]{0,1:T(8,128)} copy(f32[24576,576]{1,0:T(8,128)} %scatter_fusion) | data formatting | bytes 113246208 | tf_op jit(solution)/shard_map/scatter-add | solution.py:37
  419.5 64.5 %convolution_add_fusion = f32[24576,576]{0,1:T(8,128)} fusion(f32[24576,576]{0,1:T(8,128)} %copy.12, bf16[1024,24576]{1,0:T(8,128)(2,1)} %fusion.1, bf16[1,1024,576]{1,2,0:T(8,128)(2,1)S(1)} %copy-done, f32[576]{0:T(1024)S(1)} %copy-done.8, f32[1024]{0:T(1024)S(1)} %copy-done.6), kind=kOutput, calls=%fused_computation.8 | convolution fusion | flops 29007544320 | bytes 164763904 | tf_op jit(solution)/shard_map/tv,td->vd/dot_general | solution.py:33
  484.0 0.6 copy-done.4
  484.7 0.6 fusion.18
  485.3 2.6 fusion.12
  487.9 6.5 all-reduce
  495.7 1.5 fusion.14
  497.2 370.0 %reduce-scatter.2.cloned.1.call-done = f32[24576,144]{0,1:T(8,128)} async-done(((f32[24576,576]{0,1:T(8,128)}), f32[24576,144]{0,1:T(8,128)}) %reduce-scatter.2.cloned.1.call-update) | async-done | bytes 14155792 | tf_op jit(solution)/shard_map/reduce_scatter | solution.py:34
  (40 shorter events, 1.6 us)
Async XLA Ops:
  8.0 477.3 %all-reduce.4.cloned.1.call-start = ((), (), s32[]{:S(2)}) async-start(), calls=%async_computation.1 | async-start | bytes 4718592 | tf_op jit(solution)/shard_map/psum | solution.py:32
  9.6 0.7 copy-start.5
  10.3 0.6 copy-start.7
  12.5 58.7 %copy-start.9 = (s32[1,1024]{1,0:T(1,128)S(1)}, s32[1,1024]{1,0:T(1,128)}, u32[]{:S(2)}) copy-start(s32[1,1024]{1,0:T(1,128)} %param.11) | copy-start | bytes 12292
  12.5 66.4 %copy-start.13 = (s32[1,1024]{1,0:T(1,128)S(1)}, s32[1,1024]{1,0:T(1,128)}, u32[]{:S(2)}) copy-start(s32[1,1024]{1,0:T(1,128)} %param.10) | copy-start | bytes 12292
  71.1 50.0 %copy-start.3 = (f32[1024,1]{0,1:T(1,128)}, f32[1024,1]{0,1:T(1,128)S(1)}, u32[]{:S(2)}) copy-start(f32[1024,1]{0,1:T(1,128)S(1)} %pmax.7) | copy-start | bytes 12292
  121.1 49.3 %copy-start.11 = (f32[1024,1]{0,1:T(1,128)}, f32[1024,1]{0,1:T(1,128)S(1)}, u32[]{:S(2)}) copy-start(f32[1024,1]{0,1:T(1,128)S(1)} %get-tuple-element.11) | copy-start | bytes 12292
  170.4 38.8 %copy-start.14 = (s32[1,1024]{1,0:T(1,128)S(1)}, s32[1,1024]{1,0:T(1,128)}, u32[]{:S(2)}) copy-start(s32[1,1024]{1,0:T(1,128)} %param.12) | copy-start | bytes 12292
  208.9 1.3 copy-start.2
  208.9 658.3 %reduce-scatter.2.cloned.1.call-start = ((), (), s32[]{:S(2)}) async-start(), calls=%async_computation.2 | async-start | bytes 70778880 | tf_op jit(solution)/shard_map/reduce_scatter | solution.py:34
  360.7 58.7 %copy-start = (bf16[1,1024,576]{1,2,0:T(8,128)(2,1)S(1)}, bf16[1,1024,576]{1,2,0:T(8,128)(2,1)}, u32[]{:S(2)}) copy-start(bf16[1,1024,576]{1,2,0:T(8,128)(2,1)} %param.7) | copy-start | bytes 3538948
  360.7 58.7 %copy-start.6 = (f32[1024]{0:T(1024)S(1)}, f32[1024]{0:T(1024)}, u32[]{:S(2)}) copy-start(f32[1024]{0:T(1024)} %copy-done.5) | copy-start | bytes 12292
  360.8 58.7 %copy-start.8 = (f32[576]{0:T(1024)S(1)}, f32[576]{0:T(1024)}, u32[]{:S(2)}) copy-start(f32[576]{0:T(1024)} %copy-done.7) | copy-start | bytes 6916
  484.0 0.7 copy-start.4
  484.0 0.7 copy-start.10
  484.0 0.7 copy-start.12
  484.0 0.7 copy-start.15
  485.3 10.3 %copy-start.1 = (f32[1024,576]{0,1:T(8,128)S(1)}, f32[1024,576]{0,1:T(8,128)}, u32[]{:S(2)}) copy-start(f32[1024,576]{0,1:T(8,128)} %all-reduce.4.cloned.1.call-done) | copy-start | bytes 7077892
Sparse Core Ops, SparseCore 0:
  209.0 64.6 all-reduce.3
Sparse Core Ops, SparseCore 1:
  484.1 383.0 reduce-scatter.1
where the time goes:
time: 883 us; the launch traced here: 876 us
  waiting for transfers between devices  370 us (42%)
  other arithmetic  224 us (25%)
  matrix products  155 us (18%)
  local copies, waits for them, and re-layouts  83.7 us (9%)
  blocking collectives  24.8 us (3%)
  between operations  18 us (2%)
    reduce_scatter x1, waiting for transfers between devices, local_step(): lax.psum_scatter(head_grad, 'dp', scatter_dimension=1, tiled=True)  370 us
    scatter-add x1, other arithmetic, local_step(): jax.ops.segment_sum(grad_embed.reshape(tokens, d_model).astype(jnp.float3...  126 us
    dot_general x1, matrix products, local_step(): jnp.einsum('tv,td->vd', dlogits, z_rows, preferred_element_type=jnp.float32)  64.5 us
    scatter-add x1, local copies, waits for them, and re-layouts, local_step(): jax.ops.segment_sum(grad_embed.reshape(tokens, d_model).astype(jnp.float3...  58.7 us
    dot_general x1, matrix products, local_step(): jnp.einsum('td,vd->tv', z_rows, embed, preferred_element_type=jnp.float32)  52.4 us
    convert_element_type x1, other arithmetic, local_step(): (jnp.where(is_target, soft_probs - 1.0, soft_probs) * (mask_rows / token_...  49.3 us
    dot_general x1, matrix products, local_step(): jnp.dot(dlogits, embed, preferred_element_type=jnp.float32)  38.4 us
    reduce_sum x1, other arithmetic, local_step(): sum_exp = lax.psum(jnp.sum(shifted, axis=-1, keepdims=True), 'tp')  36.6 us
  transfers between devices with their start and end apart: 2, of which 1 were waited for; matrix products, arithmetic and copies ran while one was open for 32% of the time, Pallas kernels for 0%

commit v1 on v0

v1 whole, which is shorter than its diff:
```python
import functools

import jax
import jax.numpy as jnp
from jax import lax
from jax.experimental import pallas as pl
from jax.experimental.pallas import tpu as pltpu
from jax.sharding import PartitionSpec as P


RMS_EPS = 1e-6
LOG2E = 1.4426950408889634
LN2 = 0.6931471805599453
TB = 256
VB = 4096
SC = 512
LB = 1024
CH = 128
LANE = 128
ALL = Ellipsis
MIB = 2**20
SMALL = 2**28
F32 = jnp.float32
BF16 = jnp.bfloat16


def over_lanes(x):
    return jnp.sum(x, axis=1, keepdims=True)


def over_rows(x):
    return jnp.sum(x, axis=0, keepdims=True)


def mean_rows(x):
    return jnp.mean(x, axis=0, keepdims=True)


def cost(flops):
    return pl.CostEstimate(flops=int(flops), bytes_accessed=MIB, transcendentals=0)


def params(vmem_mib, n=2):
    return pltpu.CompilerParams(dimension_semantics=("arbitrary",) * n, vmem_limit_bytes=vmem_mib * MIB)


def stats_stage(l_ref, m_ref, s_ref, row, c):
    for r in range(TB // 8):
        rows = pl.ds(row + 8 * r, 8)
        old = m_ref[rows, :]
        total = s_ref[rows, :]
        parts = [l_ref[0, 0, 8 * r:8 * r + 8, c * SC + LANE * j:c * SC + LANE * j + LANE] for j in range(SC // LANE)]
        new = functools.reduce(jnp.maximum, parts, old)
        total = total * jnp.exp2(old - new)
        for part in parts:
            total = total + jnp.exp2(part - new)
        m_ref[rows, :] = new
        s_ref[rows, :] = total


def logits_kernel(sc, z_ref, e_ref, l_ref, m_ref, s_ref):
    v, t = pl.program_id(0), pl.program_id(1)
    row = pl.multiple_of(sc[0, t] * TB, TB)
    skip = sc[2, 3]

    @pl.when((v == 0) & (t >= skip))
    def _():
        m_ref[pl.ds(row, TB), :] = jnp.full((TB, LANE), -3e38, F32)
        s_ref[pl.ds(row, TB), :] = jnp.zeros((TB, LANE), F32)

    @pl.when(t >= skip)
    def _():
        n = VB // SC
        for c in range(n + 1):
            if c < n:
                q = slice(c * SC, (c + 1) * SC)
                l_ref[0, 0, :, q] = jnp.dot(z_ref[ALL], e_ref[:, q], preferred_element_type=F32) * LOG2E
            if c > 0:
                stats_stage(l_ref, m_ref, s_ref, row, c - 1)


def dlogits_stage(get, dl_ref, k_ref, scale, t_ref, tl_ref, row, base, c):
    for r in range(TB // 16):
        rows = pl.ds(row + 16 * r, 16)
        shift = k_ref[rows, :]
        target = t_ref[rows, :] - base
        if tl_ref is not None:
            found = tl_ref[rows, :]
        for j in range(SC // LANE):
            o = c * SC + LANE * j
            x = get(r, o)
            hit = target == o
            p = jnp.exp2(x - shift)
            if tl_ref is not None:
                found = jnp.where(hit, x, found)
            dl_ref[16 * r:16 * r + 16, o:o + LANE] = jnp.where(hit, p - scale, p).astype(BF16)
        if tl_ref is not None:
            tl_ref[rows, :] = found


def own_kernel(sc, l_ref, e_ref, za_ref, zb_ref, k_ref, t_ref, inv_ref, dz_ref, da_ref, db_ref, tl_ref, dl_ref):
    v, t = pl.program_id(0), pl.program_id(1)
    row = pl.multiple_of(sc[0, t] * TB, TB)
    skip = sc[2, 3]

    @pl.when((v == 0) & (t >= skip))
    def _():
        dz_ref[:, pl.ds(row, TB)] = jnp.zeros((dz_ref.shape[0], TB), F32)

    @pl.when((v == 0) & (t == 0))
    def _():
        tl_ref[ALL] = jnp.zeros_like(tl_ref)

    @pl.when(t == skip)
    def _():
        da_ref[ALL] = jnp.zeros_like(da_ref)
        db_ref[ALL] = jnp.zeros_like(db_ref)

    @pl.when(t >= skip)
    def _():
        zc = jnp.concatenate([za_ref[ALL], zb_ref[ALL]], axis=0)
        half = za_ref.shape[0]
        scale = jnp.concatenate([inv_ref[ALL], inv_ref[ALL]], axis=0)
        n = VB // SC
        get = lambda r, o: l_ref[0, 0, 16 * r:16 * r + 16, o:o + LANE]
        for c in range(n + 1):
            if c < n:
                dlogits_stage(get, dl_ref, k_ref, scale, t_ref, tl_ref, row, v * VB, c)
            if c > 0:
                q = slice((c - 1) * SC, c * SC)
                dl = dl_ref[:, q]
                dz_ref[:, pl.ds(row, TB)] += lax.dot_general(
                    e_ref[:, q], dl, (((1,), (1,)), ((), ())), preferred_element_type=F32)
                de = jnp.dot(zc, dl, preferred_element_type=F32)
                da_ref[:, q] += de[:half]
                db_ref[:, q] += de[half:]


def other_kernel(sc, z_ref, e_ref, za_ref, zb_ref, k_ref, t_ref, inv_ref, ia_ref, ib_ref, da_ref, db_ref, l_ref, dl_ref):
    v, t = pl.program_id(0), pl.program_id(1)
    row = pl.multiple_of(sc[1, t] * TB, TB)
    skip = sc[2, 4]

    @pl.when(t == skip)
    def _():
        da_ref[ALL] = ia_ref[ALL]
        db_ref[ALL] = ib_ref[ALL]

    @pl.when(t >= skip)
    def _():
        zc = jnp.concatenate([za_ref[ALL], zb_ref[ALL]], axis=0)
        half = za_ref.shape[0]
        scale = jnp.concatenate([inv_ref[ALL], inv_ref[ALL]], axis=0)
        n = VB // SC
        get = lambda r, o: l_ref[16 * r:16 * r + 16, o:o + LANE] * LOG2E
        for c in range(n + 2):
            if c < n:
                q = slice(c * SC, (c + 1) * SC)
                l_ref[:, q] = jnp.dot(z_ref[ALL], e_ref[:, q], preferred_element_type=F32)
            if 0 < c <= n:
                dlogits_stage(get, dl_ref, k_ref, scale, t_ref, None, row, v * VB, c - 1)
            if c > 1:
                q = slice((c - 2) * SC, (c - 1) * SC)
                de = jnp.dot(zc, dl_ref[:, q], preferred_element_type=F32)
                da_ref[:, q] += de[:half]
                db_ref[:, q] += de[half:]


def arrange_kernel(idx, a_ref, b_ref, zt_ref, z_ref):
    x = jnp.where(pl.program_id(0) == 0, a_ref[ALL], b_ref[ALL])
    zt_ref[ALL] = x.astype(BF16)
    z_ref[ALL] = x.T.astype(BF16)


def xor(i, k):
    return (i + 1 - 2 * lax.rem(i, 2), lax.rem(i + 2, 4), 3 - i)[k - 1]


def columns(row):
    return jnp.broadcast_to(row, (LANE, LANE)).T


def sort_kernel(t_ref, m_ref, i_ref, ge_ref, o1, o2, o3, o4, meta_ref, key_ref, perm_ref, sorted_ref):
    seq = i_ref.shape[1]
    nb = seq // LANE
    lane = lax.broadcasted_iota(jnp.int32, (1, LANE), 1)
    rows = [i_ref[:, LANE * j:LANE * j + LANE] * seq + lane + LANE * j for j in range(nb)]
    for j in range(nb):
        key_ref[LANE * j:LANE * j + LANE, :] = columns(rows[j])
    keys = key_ref[ALL]
    before = jnp.zeros((seq, LANE), F32)
    for j in range(nb):
        before = before + jnp.where(rows[j] < keys, 1.0, 0.0)
    rank = jnp.broadcast_to(over_lanes(before), (seq, LANE)).astype(jnp.int32)
    meta_ref[ALL] = jnp.zeros_like(meta_ref)
    meta_ref[0:1, :] = t_ref[ALL]
    meta_ref[1:2, :] = m_ref[ALL]
    for j in range(nb):
        hit = rank == lane + LANE * j
        perm_ref[:, LANE * j:LANE * j + LANE] = jnp.where(hit, 1.0, 0.0).astype(BF16)
        place = over_rows(jnp.where(hit, keys, 0))
        meta_ref[2:3, LANE * j:LANE * j + LANE] = lax.shift_right_logical(place, seq.bit_length() - 1)
    sorted_ref[ALL] = jnp.dot(ge_ref[ALL], perm_ref[ALL], preferred_element_type=F32)
    dp = lax.axis_index("dp")
    cols = o1.shape[0]
    for k, o in enumerate((o1, o2, o3, o4)):
        who = dp if k == 0 else xor(dp, k)
        o[ALL] = sorted_ref[pl.ds(pl.multiple_of(who * cols, 8), cols), :]


def greet(peers):
    barrier = pltpu.get_barrier_semaphore()
    for peer in peers:
        pl.semaphore_signal(barrier, inc=1, device_id=peer, device_id_type=pl.DeviceIdType.MESH)
    pl.semaphore_wait(barrier, len(peers))


def send(src, dst, sems, k, peer):
    copy = pltpu.make_async_remote_copy(
        src_ref=src, dst_ref=dst, send_sem=sems[0].at[k], recv_sem=sems[1].at[k],
        device_id=peer, device_id_type=pl.DeviceIdType.MESH)
    copy.start()
    return copy


def prep_kernel(h_ref, g_ref, meta_ref, z32_ref, zt_ref, z_ref, all_ref, table_ref, inv_ref, got_ref, box_ref, s_sem, r_sem):
    dp, tp = lax.axis_index("dp"), lax.axis_index("tp")
    core = lax.rem(dp, 2)
    chip = lax.div(dp, 2)
    _, seq = h_ref.shape
    at = lambda i: (tp, i)
    peers = [at(xor(dp, k)) for k in (1, 2, 3)]
    greet(peers)
    sems = (s_sem, r_sem)
    copies = [send(meta_ref, box_ref.at[k], sems, k, peers[k]) for k in range(3)]
    x = h_ref[ALL].astype(F32)
    inv = lax.rsqrt(mean_rows(x * x) + RMS_EPS)
    gain = jnp.concatenate([g_ref[ALL]] * (seq // LANE), axis=1)
    z = (x * inv * gain).astype(BF16)
    z32_ref[ALL] = z.astype(F32)
    z_ref[pl.ds(pl.multiple_of(core * seq, seq), seq), :] = z.T
    copies.append(send(z32_ref, got_ref, sems, 3, peers[0]))
    zt_ref[:, pl.ds(pl.multiple_of(core * seq, seq), seq)] = z
    for copy in copies[:3]:
        copy.wait()
    all_ref[dp] = meta_ref[ALL]
    for k in range(3):
        all_ref[xor(dp, k + 1)] = box_ref[k]

    tiles = []
    total = jnp.zeros((1, 1), F32)
    for q in range(4):
        length = over_lanes(all_ref[q, 1:2, :].astype(F32))
        total = total + length
        tiles.append(jnp.floor((length + (TB - 1)) * (1.0 / TB)).astype(jnp.int32))
    inv_ref[ALL] = jnp.broadcast_to(1.0 / total, inv_ref.shape)
    nt = 2 * seq // TB
    lane = lax.broadcasted_iota(jnp.int32, (1, LANE), 1)
    swap = chip == 1
    pairs = [(tiles[0], tiles[1]), (tiles[2], tiles[3])]
    out = []
    skips = []
    for c in range(2):
        na = jnp.where(swap, pairs[1 - c][0], pairs[c][0])
        nb = jnp.where(swap, pairs[1 - c][1], pairs[c][1])
        skip = nt - na - nb
        p = jnp.maximum(lane - skip, 0)
        lst = jnp.where(p < na, p, nt // 2 + p - na)
        out.append(jnp.minimum(lst, nt - 1))
        skips.append(skip)
    row = jnp.where(lane == 0, core, jnp.where(lane == 1, dp, jnp.where(lane == 2, xor(dp, 1), jnp.where(lane == 3, skips[0], skips[1]))))
    table_ref[ALL] = jnp.zeros_like(table_ref)
    table_ref[0:1, :] = out[0]
    table_ref[1:2, :] = out[1]
    table_ref[2:3, :] = row

    copies[3].wait()
    other = xor(dp, 1) - 2 * chip
    got = got_ref[ALL].astype(BF16)
    z_ref[pl.ds(pl.multiple_of(other * seq, seq), seq), :] = got.T
    zt_ref[:, pl.ds(pl.multiple_of(other * seq, seq), seq)] = got


def stats_kernel(vocab_local, m_ref, s_ref, all_ref, ko_ref, to_ref, kf_ref, tf_ref, lse_ref, look_ref, mine_ref, box_ref, s_sem, r_sem):
    dp, tp = lax.axis_index("dp"), lax.axis_index("tp")
    core = lax.rem(dp, 2)
    chip = lax.div(dp, 2)
    tokens = m_ref.shape[0]
    seq = all_ref.shape[2]
    nb = tokens // LANE
    dps = [dp, xor(dp, 1), xor(dp, 2), xor(dp, 3)]
    peers = [(t, i) for t in (tp, 1 - tp) for i in dps][1:]
    greet(peers)
    for j in range(nb):
        m = m_ref[LANE * j:LANE * j + LANE, :].T
        s = s_ref[LANE * j:LANE * j + LANE, :].T
        top = jnp.max(m, axis=0, keepdims=True)
        mine_ref[j:j + 1, :] = top
        mine_ref[nb + j:nb + j + 1, :] = over_rows(s * jnp.exp2(m - top))
    box_ref[0] = mine_ref[ALL]
    copies = [send(mine_ref, box_ref.at[k + 1], (s_sem, r_sem), k, peers[k]) for k in range(7)]

    lane = lax.broadcasted_iota(jnp.int32, (1, LANE), 1)
    edge = lane * LB + tp * vocab_local
    look_ref[ALL] = jnp.zeros_like(look_ref)
    steps = jnp.zeros((1, LANE), F32)
    for q in range(4):
        lo = jnp.zeros((1, LANE), F32)
        hi = jnp.zeros((1, LANE), F32)
        for j in range(seq // LANE):
            ids = columns(all_ref[dps[q], 2:3, LANE * j:LANE * j + LANE])
            lo = lo + over_rows(jnp.where(ids < edge, 1.0, 0.0))
            hi = hi + over_rows(jnp.where(ids < edge + LB, 1.0, 0.0))
        a = jnp.floor(lo * (1.0 / CH))
        b = jnp.floor((hi + (CH - 1)) * (1.0 / CH))
        look_ref[q:q + 1, :] = a.astype(jnp.int32)
        steps = jnp.maximum(steps, jnp.where(hi > lo, b - a, 0.0))
    look_ref[4:5, :] = steps.astype(jnp.int32)

    total = jnp.zeros((1, 1), F32)
    for q in range(4):
        total = total + over_lanes(all_ref[q, 1:2, :].astype(F32))
    shift = jnp.log(total) * LOG2E
    for copy in copies:
        copy.wait()

    def merged(slots):
        ms = [box_ref[k, 0:nb, :] for k in slots]
        ss = [box_ref[k, nb:2 * nb, :] for k in slots]
        top = functools.reduce(jnp.maximum, ms)
        w = [s * jnp.exp2(m - top) for s, m in zip(ss, ms)]
        return top + jnp.log((w[0] + w[1]) + (w[2] + w[3])) * LOG2E

    sets = [(merged((0, 1, 4, 5)), chip, ko_ref, to_ref), (merged((2, 3, 6, 7)), 1 - chip, kf_ref, tf_ref)]
    base = tp * vocab_local + core * (vocab_local // 2)
    sums = []
    for lse, c, k_out, t_out in sets:
        acc = jnp.zeros((1, LANE), F32)
        for j in range(nb):
            q, o = c * 2 + j // (nb // 2), LANE * (j % (nb // 2))
            on = all_ref[q, 1:2, o:o + LANE] > 0
            row = lse[j:j + 1, :]
            acc = acc + jnp.where(on, row, 0.0)
            k_out[LANE * j:LANE * j + LANE, :] = columns(jnp.where(on, row + shift, jnp.inf))
            t_out[LANE * j:LANE * j + LANE, :] = columns(jnp.where(on, all_ref[q, 0:1, o:o + LANE] - base, -MIB)) - lane
        sums.append(acc)
    lse_ref[ALL] = jnp.broadcast_to(sums[0] + sums[1], lse_ref.shape)


def final_kernel(a_ref, b_ref, h_ref, g_ref, on_ref, tl_ref, lse_ref, inv_ref, dh_ref, dg_ref, loss_ref, mine_ref, box_ref, s_sem, r_sem):
    dp, tp = lax.axis_index("dp"), lax.axis_index("tp")
    dps = [dp, xor(dp, 1), xor(dp, 2), xor(dp, 3)]
    peers = [(t, i) for t in (tp, 1 - tp) for i in dps][1:]
    greet(peers)
    d, seq = h_ref.shape
    x = h_ref[ALL].astype(F32)
    inv = lax.rsqrt(mean_rows(x * x) + RMS_EPS)
    u = x * inv
    dz = jnp.where(on_ref[ALL] > 0, a_ref[ALL] + b_ref[ALL], 0.0)
    prod = dz * u
    part = sum(prod[:, LANE * j:LANE * j + LANE] for j in range(seq // LANE))
    mine_ref[ALL] = jnp.zeros_like(mine_ref)
    mine_ref[0:1, 0:d] = over_rows(part.T)
    mine_ref[1:2, 0:LANE] = over_rows(tl_ref[ALL])
    gain = jnp.concatenate([g_ref[ALL]] * (seq // LANE), axis=1)
    w = dz * gain
    dh_ref[ALL] = (inv * (w - u * mean_rows(w * u))).astype(BF16)
    box_ref[0] = mine_ref[ALL]
    copies = [send(mine_ref, box_ref.at[k + 1], (s_sem, r_sem), k, peers[k]) for k in range(7)]
    for copy in copies:
        copy.wait()
    same = [jnp.zeros((1, d), F32)] * 4
    found = jnp.zeros((1, LANE), F32)
    for q in range(4):
        row = jnp.zeros((1, d), F32)
        hit = jnp.zeros((1, LANE), F32)
        low = jnp.zeros((1, LANE), F32)
        for k in range(4):
            row = jnp.where(dps[k] == q, box_ref[k, 0:1, 0:d], row)
            hit = jnp.where(dps[k] == q, box_ref[k, 1:2, 0:LANE], hit)
            low = jnp.where(dps[k] == q, box_ref[k + 4, 1:2, 0:LANE], low)
        same[q] = row
        found = found + (hit + low)
    dg_ref[ALL] = same[0] + same[1] + same[2] + same[3]
    loss = over_lanes(lse_ref[0:1, :] - found) * LN2
    loss_ref[ALL] = jnp.broadcast_to(loss, loss_ref.shape) * inv_ref[0:1, :]


def lookup_kernel(top, sc, look, from_ref, g1, g2, g3, g4, all_ref, *rest):
    out_ref, id_ref = rest[-2:]
    b = pl.program_id(0)
    nc = all_ref.shape[2] // CH

    @pl.when(b == 0)
    def _():
        for q in range(4):
            who = sc[2, 1] if q == 0 else xor(sc[2, 1], q)
            for j in range(nc):
                id_ref[q, j] = columns(all_ref[who, 2:3, CH * j:CH * j + CH])

    at = top(sc, b)
    out_ref[ALL] = from_ref[ALL]
    cols = lax.broadcasted_iota(jnp.int32, (CH, LB), 1) + (at * LB + sc[2, 5])

    def step(k, _):
        hots, rows = [], []
        for q, g in enumerate((g1, g2, g3, g4)):
            c = look[q, at] + k
            ok = c < nc
            c = jnp.minimum(c, nc - 1)
            ids = jnp.concatenate([id_ref[q, c]] * (LB // LANE), axis=1)
            hots.append(jnp.where(ids == jnp.where(ok, cols, -1), 1.0, 0.0).astype(BF16))
            rows.append(g[:, pl.ds(pl.multiple_of(c * CH, CH), CH)].astype(BF16))
        out_ref[ALL] += jnp.dot(jnp.concatenate(rows, axis=1), jnp.concatenate(hots, axis=0), preferred_element_type=F32)
        return 0

    lax.fori_loop(0, look[4, at], step, 0)


def solution(mesh):
    n_dp = mesh.shape["dp"]
    swap = {k: [(i, i ^ k) for i in range(n_dp)] for k in (1, 2, 3)}
    whole = pl.BlockSpec(memory_space=pltpu.VMEM)
    shape = jax.ShapeDtypeStruct
    dma = pltpu.SemaphoreType.DMA

    def local_step(hidden, norm_w, embed, targets, loss_mask, token_ids, grad_embed):
        _, seq, d = hidden.shape
        vocab_local = embed.shape[0]
        half = vocab_local // 2
        nv = half // VB
        cols = d // n_dp
        nt = 2 * seq // TB
        et = embed.T
        ht = hidden[0].T
        gain = jnp.broadcast_to(norm_w.astype(F32)[:, None], (d, LANE))
        talk = lambda i, mib: pltpu.CompilerParams(collective_id=i, has_side_effects=True, vmem_limit_bytes=mib * MIB)

        *give, meta = pl.pallas_call(
            sort_kernel, in_specs=[whole] * 4, out_specs=[whole] * 5,
            out_shape=[shape((cols, seq), F32)] * 4 + [shape((8, seq), jnp.int32)],
            scratch_shapes=[pltpu.VMEM((seq, LANE), jnp.int32), pltpu.VMEM((seq, seq), BF16), pltpu.VMEM((d, seq), F32)],
            compiler_params=pltpu.CompilerParams(vmem_limit_bytes=40 * MIB), name="sort",
            cost_estimate=cost(2 * d * seq * seq),
        )(targets, loss_mask, token_ids, grad_embed[0].T)

        zt32, zt_chip, z_chip, metas, table, inv_n = pl.pallas_call(
            prep_kernel, in_specs=[whole] * 3, out_specs=[whole] * 6,
            out_shape=[shape((d, seq), F32), shape((d, 2 * seq), BF16), shape((2 * seq, d), BF16),
                       shape((n_dp, 8, seq), jnp.int32), shape((8, LANE), jnp.int32), shape((8, LANE), F32)],
            scratch_shapes=[pltpu.VMEM((d, seq), F32), pltpu.VMEM((3, 8, seq), jnp.int32), dma((4,)), dma((4,))],
            compiler_params=talk(0, 48), name="prep",
            cost_estimate=cost(SMALL),
        )(ht, gain, meta)
        tp_base = lax.axis_index("tp") * vocab_local
        spot = (lax.broadcasted_iota(jnp.int32, (8, LANE), 0) == 2) & (lax.broadcasted_iota(jnp.int32, (8, LANE), 1) == 5)
        table = jnp.where(spot, tp_base, table)

        far = lax.ppermute(zt32, "dp", swap[2])
        far_near = lax.ppermute(far, "dp", swap[1])

        def arrange(a, b):
            w = 512
            n = seq // w
            place = lambda j, i, x: lax.bitwise_xor(j, x[2, 0]) * n + i
            return pl.pallas_call(
                arrange_kernel,
                grid_spec=pltpu.PrefetchScalarGridSpec(
                    num_scalar_prefetch=1, grid=(2, n),
                    in_specs=[
                        pl.BlockSpec((d, w), lambda j, i, x: (0, jnp.where(j == 0, i, n - 1))),
                        pl.BlockSpec((d, w), lambda j, i, x: (0, jnp.where(j == 1, i, 0)))],
                    out_specs=[
                        pl.BlockSpec((d, w), lambda j, i, x: (0, place(j, i, x))),
                        pl.BlockSpec((w, d), lambda j, i, x: (place(j, i, x), 0))]),
                out_shape=[shape((d, 2 * seq), BF16), shape((2 * seq, d), BF16)],
                compiler_params=params(40), name="arrange",
                cost_estimate=cost(SMALL),
            )(table, a, b)

        def specs(r):
            full = lambda v, t, x: (0, 0)
            return dict(
                e=pl.BlockSpec((d, VB), lambda v, t, x: (0, x[2, 0] * nv + v)),
                z=pl.BlockSpec((TB, d), lambda v, t, x: (x[r, t], 0)),
                l=pl.BlockSpec((1, 1, TB, VB), lambda v, t, x: (x[r, t], v, 0, 0)),
                vec=pl.BlockSpec((2 * seq, LANE), full),
                inv=pl.BlockSpec((8, LANE), full),
                dz=pl.BlockSpec((d, 2 * seq), full),
                za=pl.BlockSpec((cols, TB), lambda v, t, x: (x[2, 1], x[r, t])),
                zb=pl.BlockSpec((cols, TB), lambda v, t, x: (x[2, 2], x[r, t])),
                de=pl.BlockSpec((cols, VB), lambda v, t, x: (0, v)))

        pick = lambda sp, *names: [sp[k] for k in names]
        own, other = specs(0), specs(1)
        vec = shape((2 * seq, LANE), F32)
        ivec = shape((2 * seq, LANE), jnp.int32)
        de_shape = shape((cols, half), F32)
        flops = 2 * 2 * seq * half * d

        l_own, m_own, s_own = pl.pallas_call(
            logits_kernel,
            grid_spec=pltpu.PrefetchScalarGridSpec(
                num_scalar_prefetch=1, grid=(nv, nt), in_specs=pick(own, "z", "e"), out_specs=pick(own, "l", "vec", "vec")),
            out_shape=[shape((nt, nv, TB, VB), F32), vec, vec],
            compiler_params=params(56), name="logits",
            cost_estimate=cost(flops),
        )(table, z_chip, et)

        k_own, t_own, k_far, t_far, lse_sum, look = pl.pallas_call(
            functools.partial(stats_kernel, vocab_local),
            in_specs=[whole] * 3, out_specs=[whole] * 6,
            out_shape=[vec, ivec, vec, ivec, shape((8, LANE), F32), shape((8, LANE), jnp.int32)],
            scratch_shapes=[pltpu.VMEM((4 * seq // LANE, LANE), F32), pltpu.VMEM((8, 4 * seq // LANE, LANE), F32), dma((7,)), dma((7,))],
            compiler_params=talk(1, 32), name="stats",
            cost_estimate=cost(SMALL),
        )(m_own, s_own, metas)

        lists = [give[0]]
        for k in (1, 2, 3):
            lists.append(lax.ppermute(give[k], "dp", swap[k]))

        dz, da, db, tl = pl.pallas_call(
            own_kernel,
            grid_spec=pltpu.PrefetchScalarGridSpec(
                num_scalar_prefetch=1, grid=(nv, nt),
                in_specs=pick(own, "l", "e", "za", "zb", "vec", "vec", "inv"), out_specs=pick(own, "dz", "de", "de", "vec"),
                scratch_shapes=[pltpu.VMEM((TB, VB), BF16)]),
            out_shape=[shape((d, 2 * seq), F32), de_shape, de_shape, vec],
            compiler_params=params(60), name="own",
            cost_estimate=cost(flops + flops // 2),
        )(table, l_own, et, zt_chip, zt_chip, k_own, t_own, inv_n)

        core = lax.rem(lax.axis_index("dp"), 2)
        dz_own = lax.dynamic_slice_in_dim(dz, core * seq, seq, 1)
        dz_give = lax.dynamic_slice_in_dim(dz, (1 - core) * seq, seq, 1)
        dz_near = lax.ppermute(dz_give, "dp", swap[1])
        dz_half = dz_own + dz_near
        dz_tp = lax.ppermute(dz_half, "tp", [(0, 1), (1, 0)])

        zt_far, z_far = arrange(far, far_near)
        da, db = pl.pallas_call(
            other_kernel,
            grid_spec=pltpu.PrefetchScalarGridSpec(
                num_scalar_prefetch=1, grid=(nv, nt),
                in_specs=pick(other, "z", "e", "za", "zb", "vec", "vec", "inv", "de", "de"), out_specs=pick(other, "de", "de"),
                scratch_shapes=[pltpu.VMEM((TB, VB), F32), pltpu.VMEM((TB, VB), BF16)]),
            out_shape=[de_shape, de_shape],
            compiler_params=params(60), name="other",
            cost_estimate=cost(flops + flops // 2),
        )(table, z_far, et, zt_far, zt_far, k_far, t_far, inv_n, da, db)
        got = lax.ppermute(db, "dp", swap[1])

        nb = half // LB

        def lookup(top, source, *prior):
            zero = lambda b, x, k: (0, 0)
            return pl.pallas_call(
                functools.partial(lookup_kernel, top),
                grid_spec=pltpu.PrefetchScalarGridSpec(
                    num_scalar_prefetch=2, grid=(nb,),
                    in_specs=[pl.BlockSpec((cols, LB), lambda b, x, k: (0, b))] + [pl.BlockSpec((cols, seq), zero)] * 4
                    + [pl.BlockSpec((n_dp, 8, seq), lambda b, x, k: (0, 0, 0))] + [pl.BlockSpec(memory_space=pl.ANY)] * len(prior),
                    out_specs=pl.BlockSpec((cols, LB), lambda b, x, k: (0, top(x, b))),
                    scratch_shapes=[pltpu.VMEM((4, seq // CH, CH, LANE), jnp.int32)]),
                out_shape=shape((cols, vocab_local), F32),
                input_output_aliases={8: 0} if prior else {},
                compiler_params=params(40, 1), name="lookup",
                cost_estimate=cost(flops // 8),
            )(table, look, source, *lists, metas, *prior)

        de_t = lookup(lambda x, b: x[2, 0] * nb + b, da)

        dht, dg, loss = pl.pallas_call(
            final_kernel, in_specs=[whole] * 8, out_specs=[whole] * 3,
            out_shape=[shape((d, seq), BF16), shape((1, d), F32), shape((1, LANE), F32)],
            scratch_shapes=[pltpu.VMEM((8, 640), F32), pltpu.VMEM((8, 8, 640), F32), dma((7,)), dma((7,))],
            compiler_params=talk(2, 48), name="final",
            cost_estimate=cost(SMALL),
        )(dz_half, dz_tp, ht, gain, loss_mask, tl, lse_sum, inv_n)

        de_t = lookup(lambda x, b: (1 - x[2, 0]) * nb + b, got, de_t)
        return loss[0, 0], dht.T[None], dg[0], de_t.T

    return jax.shard_map(
        local_step, mesh=mesh,
        in_specs=(P("dp"), P(), P("tp"), P("dp"), P("dp"), P("dp"), P("dp")),
        out_specs=(P(), P("dp"), P(), P("tp", "dp")), check_vma=False)
```

time: 883 us -> 300 us (0.34)
  waiting for transfers between devices: 370 us -> 62.2 us
  other arithmetic: 224 us -> 4.11 us
  Pallas kernels: 0 us -> 205 us
  matrix products: 155 us -> 0 us
  local copies, waits for them, and re-layouts: 83.7 us -> 22.1 us
  blocking collectives: 24.8 us -> 0 us
  between operations: 18 us -> 1.98 us
    reduce_scatter x1 -> x0, waiting for transfers between devices: 370 us -> none  [local_step(): lax.psum_scatter(head_grad, 'dp', scatter_dimension=1, tiled=True)]
    pallas_call x0 -> x10, Pallas kernels: none -> 205 us  [the longest x1 49.5 us: local_step(): pl.pallas_call(other_kernel, grid_spec=pltpu.PrefetchScalarGridSpec(num_s...]
    dot_general x3 -> x0, matrix products: 155 us -> none  [the longest x1 64.5 us: local_step(): jnp.einsum('tv,td->vd', dlogits, z_rows, preferred_element_type=jnp.float32)]
    scatter-add x1 -> x0, other arithmetic: 126 us -> none  [local_step(): jax.ops.segment_sum(grad_embed.reshape(tokens, d_model).astype(jnp.float3...]
    ppermute x0 -> x8, waiting for transfers between devices: none -> 62.2 us  [the longest x1 51.1 us: local_step(): dz_tp = lax.ppermute(dz_half, 'tp', [(0, 1), (1, 0)])]
    scatter-add x1 -> x0, local copies, waits for them, and re-layouts: 58.7 us -> none  [local_step(): jax.ops.segment_sum(grad_embed.reshape(tokens, d_model).astype(jnp.float3...]
    convert_element_type x3 -> x0, other arithmetic: 51.7 us -> none  [the longest x1 49.3 us: local_step(): (jnp.where(is_target, soft_probs - 1.0, soft_probs) * (mask_rows / token_...]
    reduce_sum x5 -> x0, other arithmetic: 42 us -> none  [the longest x1 36.6 us: local_step(): sum_exp = lax.psum(jnp.sum(shifted, axis=-1, keepdims=True), 'tp')]
  transfers between devices with their start and end apart: 2 -> 8, of which waited for: 1 -> 2; matrix products, arithmetic and copies ran while one was open for 32% -> 3% of each run, Pallas kernels for 0% -> 41%
where the time goes in v1:
time: 300 us; the launch traced here: 299 us
  Pallas kernels  205 us (68%)
  waiting for transfers between devices  62.2 us (21%)
  local copies, waits for them, and re-layouts  22.1 us (7%)
  other arithmetic  4.11 us (1%)
  starting transfers between devices  3.37 us (1%)
    ppermute x1, waiting for transfers between devices, local_step(): dz_tp = lax.ppermute(dz_half, 'tp', [(0, 1), (1, 0)])  51.1 us
    pallas_call x1, Pallas kernels, local_step(): pl.pallas_call(other_kernel, grid_spec=pltpu.PrefetchScalarGridSpec(num_s...  49.5 us
    pallas_call x1, Pallas kernels, local_step(): pl.pallas_call(own_kernel, grid_spec=pltpu.PrefetchScalarGridSpec(num_sca...  47.4 us
    pallas_call x1, Pallas kernels, local_step(): pl.pallas_call(logits_kernel, grid_spec=pltpu.PrefetchScalarGridSpec(num_...  37.7 us
    pallas_call x2, Pallas kernels, lookup(): pl.pallas_call(functools.partial(lookup_kernel, top), grid_spec=pltpu.Pre...  25.7 us
    unnamed x49, local copies, waits for them, and re-layouts  18.6 us
    pallas_call x1, Pallas kernels, local_step(): pl.pallas_call(functools.partial(stats_kernel, vocab_local), in_specs=[wh...  16 us
    pallas_call x1, Pallas kernels, local_step(): pl.pallas_call(prep_kernel, in_specs=[whole] * 3, out_specs=[whole] * 6,...  11.1 us
  transfers between devices with their start and end apart: 8, of which 2 were waited for; matrix products, arithmetic and copies ran while one was open for 3% of the time, Pallas kernels for 41%

profile of v1, /device:TPU:0, one launch (start us, length us, event | category | flops | bytes accessed | tf_op | source)
XLA Modules:
  0.0 298.9 jit_solution(18316802447060108213)
XLA Ops:
  1.3 1.3 copy-done.15
  4.0 3.8 %sort.1 = (f32[144,1024]{1,0:T(8,128)S(1)}, f32[144,1024]{1,0:T(8,128)}, f32[144,1024]{1,0:T(8,128)}, f32[144,1024]{1,0:T(8,128)}, s32[8,1024]{1,0:T(8,128)S(1)}) custom-call(s32[1,1024]{1,0:T(1,128)S(1)} %copy-done.20, s32[1,1024]{1,0:T(1,128)S(1)} %copy-done.9, s32[1,1024]{1,0:T(1,128)S(1)} %copy-done.21, bf16[576,1024]{1,0:T(8,128)(2,1)S(1)} %bitcast.16), custom_call_target="tpu_custom_call" | custom-call | flops 1207959552 | bytes 1048576 | tf_op jit(solution)/shard_map/sort/pallas_call | solution.py:439
  7.9 11.1 %prep.1 = (f32[576,1024]{1,0:T(8,128)}, bf16[576,2048]{1,0:T(8,128)(2,1)}, bf16[2048,576]{1,0:T(8,128)(2,1)}, s32[4,8,1024]{2,1,0:T(8,128)S(1)}, s32[8,128]{1,0:T(8,128)S(1)}, /*index=5*/f32[8,128]{1,0:T(8,128)S(1)}) custom-call(bf16[576,1024]{1,0:T(8,128)(2,1)S(1)} %bitcast.13, f32[576,128]{1,0:T(8,128)S(1)} %broadcast_in_dim.14.g_ref, ...), custom_call_target="tpu_custom_call" | custom-call | flops 268435456 | bytes 1048576 | tf_op jit(solution)/shard_map/prep/pallas_call | solution.py:447
  20.7 37.7 %logits.1 = (f32[8,3,256,4096]{3,2,1,0:T(8,128)}, f32[2048,128]{1,0:T(8,128)}, f32[2048,128]{1,0:T(8,128)}) custom-call(s32[8,128]{1,0:T(8,128)} %and_select_fusion.sc.idx, bf16[2048,576]{1,0:T(8,128)(2,1)} %get-tuple-element.37.z_ref, bf16[576,24576]{1,0:T(8,128)(2,1)} %bitcast.19), custom_call_target="tpu_custom_call" | custom-call | flops 28991029248 | bytes 1048576 | tf_op jit(solution)/shard_map/logits/pallas_call | solution.py:501
  58.4 1.2 copy-done.4
  59.6 1.2 copy-done.5
  60.8 16.0 %stats.1 = (f32[2048,128]{1,0:T(8,128)S(1)}, s32[2048,128]{1,0:T(8,128)S(1)}, f32[2048,128]{1,0:T(8,128)S(1)}, s32[2048,128]{1,0:T(8,128)S(1)}, f32[8,128]{1,0:T(8,128)S(1)}, /*index=5*/s32[8,128]{1,0:T(8,128)S(1)}) custom-call(f32[2048,128]{1,0:T(8,128)S(1)} %copy-done.4, f32[2048,128]{1,0:T(8,128)S(1)} %copy-done.5, ...), custom_call_target="tpu_custom_call" | custom-call | flops 268435456 | bytes 1048576 | tf_op jit(solution)/shard_map/stats/pallas_call | solution.py:510
  79.9 47.4 %own.1 = (f32[576,2048]{1,0:T(8,128)}, f32[144,12288]{1,0:T(8,128)}, f32[144,12288]{1,0:T(8,128)}, f32[2048,128]{1,0:T(8,128)}) custom-call(s32[8,128]{1,0:T(8,128)} %and_select_fusion.sc.idx, f32[8,3,256,4096]{3,2,1,0:T(8,128)} %get-tuple-element.38.l_ref, bf16[576,24576]{1,0:T(8,128)(2,1)} %bitcast.20, bf16[576,2048]{1,0:T(8,128)(2,1)} %get-tuple-element.39.za_ref.zb_ref, ...), custom_call_target="tpu_custom_call" | custom-call | flops 43486543872 | bytes 1048576 | tf_op jit(solution)/shard_map/own/pallas_call | solution.py:523
  127.3 4.5 %arrange.1 = (bf16[576,2048]{1,0:T(8,128)(2,1)S(1)}, bf16[2048,576]{1,0:T(8,128)(2,1)S(1)}) custom-call(s32[8,128]{1,0:T(8,128)S(1)} %copy-done.7, f32[576,1024]{1,0:T(8,128)} %collective-permute-done.2.a_ref, f32[576,1024]{1,0:T(8,128)} %collective-permute-done.3.b_ref), custom_call_target="tpu_custom_call" | custom-call | flops 268435456 | bytes 1048576 | tf_op jit(solution)/shard_map/arrange/pallas_call | solution.py:466
  131.9 1.4 copy-done.13
  133.3 1.4 copy-done.14
  134.7 49.5 %other.1 = (f32[144,12288]{1,0:T(8,128)}, f32[144,12288]{1,0:T(8,128)}) custom-call(s32[8,128]{1,0:T(8,128)} %and_select_fusion.sc.idx, bf16[2048,576]{1,0:T(8,128)(2,1)} %copy-done.13, bf16[576,24576]{1,0:T(8,128)(2,1)} %bitcast.21, bf16[576,2048]{1,0:T(8,128)(2,1)} %copy-done.14, bf16[576,2048]{1,0:T(8,128)(2,1)} %copy-done.14, f32[2048,128]{1,0:T(8,128)} %copy-done.16, ...), custom_call_target="tpu_custom_call" | custom-call | flops 43486543872 | bytes 1048576 | tf_op jit(solution)/shard_map/other/pallas_call | solution.py:542
  184.6 3.4 %constant_dynamic-slice_fusion = f32[576,1024]{1,0:T(8,128)} fusion(f32[576,2048]{1,0:T(8,128)} %get-tuple-element.46, s32[]{:T(128)S(6)} %select_n.12), kind=kLoop, calls=%fused_computation.2 | loop fusion | bytes 4718596 | tf_op jit(solution)/shard_map/dynamic_slice | solution.py:536
  188.1 11.1 %collective-permute-done = f32[576,1024]{1,0:T(8,128)} collective-permute-done((f32[576,1024]{1,0:T(8,128)}, f32[576,1024]{1,0:T(8,128)}, u32[]{:S(2)}, u32[]{:S(2)}) %collective-permute-start) | collective-permute-done | bytes 2359328 | tf_op jit(solution)/shard_map/ppermute | solution.py:537
  199.3 2.8 dynamic-slice_add_fusion.a_ref
  203.0 1.5 collective-permute-start.7
  204.5 51.1 %collective-permute-done.1.b_ref = f32[576,1024]{1,0:T(8,128)S(1)} collective-permute-done((f32[576,1024]{1,0:T(8,128)S(1)}, f32[576,1024]{1,0:T(8,128)S(1)}, u32[]{:S(2)}, u32[]{:S(2)}) %collective-permute-start.1) | collective-permute-done | bytes 2359328 | tf_op jit(solution)/shard_map/ppermute | solution.py:539
  255.6 1.4 copy-done.22
  257.0 9.4 %final.1 = (bf16[576,1024]{1,0:T(8,128)(2,1)S(1)}, f32[1,576]{1,0:T(1,128)S(1)}, f32[1,128]{1,0:T(1,128)S(1)}) custom-call(f32[576,1024]{1,0:T(8,128)S(1)} %dynamic-slice_add_fusion.a_ref, f32[576,1024]{1,0:T(8,128)} %copy-done.22, bf16[576,1024]{1,0:T(8,128)(2,1)S(1)} %bitcast.14, f32[576,128]{1,0:T(8,128)S(1)} %broadcast_in_dim.14.g_ref, ...), custom_call_target="tpu_custom_call" | custom-call | flops 268435456 | bytes 1048576 | tf_op jit(solution)/shard_map/final/pallas_call | solution.py:574
  266.4 1.0 copy-done.2
  268.0 3.0 %copy-done = f32[144,12288]{1,0:T(8,128)S(1)} copy-done((f32[144,12288]{1,0:T(8,128)S(1)}, f32[144,12288]{1,0:T(8,128)}, u32[]{:S(2)}) %copy-start) | copy-done | bytes 7077912
  271.0 12.5 %lookup.2.rest_0_ = f32[144,24576]{1,0:T(8,128)} custom-call(s32[8,128]{1,0:T(8,128)S(1)} %copy-done.8, s32[8,128]{1,0:T(8,128)S(1)} %get-tuple-element.52.look, f32[144,12288]{1,0:T(8,128)S(1)} %copy-done, f32[144,1024]{1,0:T(8,128)S(1)} %get-tuple-element.61.g1, f32[144,1024]{1,0:T(8,128)S(1)} %collective-permute-done.5.g2, ...), custom_call_target="tpu_custom_call" | custom-call | flops 3623878656 | bytes 1048576 | tf_op jit(solution)/shard_map/lookup/pallas_call | solution.py:558
  283.6 13.2 %lookup.3 = f32[144,24576]{1,0:T(8,128)} custom-call(s32[8,128]{1,0:T(8,128)S(1)} %copy-done.8, s32[8,128]{1,0:T(8,128)S(1)} %get-tuple-element.52.look, f32[144,12288]{1,0:T(8,128)} %collective-permute-done.4.from_ref, f32[144,1024]{1,0:T(8,128)S(1)} %get-tuple-element.61.g1, ...), custom_call_target="tpu_custom_call", output_to_operand_aliasing={{}: (8, {})} | custom-call | flops 3623878656 | bytes 1048576 | tf_op jit(solution)/shard_map/lookup/pallas_call | solution.py:558
  296.8 1.0 copy.16
  (58 shorter events, 8.9 us)
Async XLA Ops:
  1.3 1.3 copy-start.15
  4.0 3.8 %copy-start.23 = (bf16[576]{0:T(1024)(128)(2,1)S(1)}, bf16[576]{0:T(1024)(128)(2,1)}, u32[]{:S(2)}) copy-start(bf16[576]{0:T(1024)(128)(2,1)} %param.8) | copy-start | bytes 3460
  4.0 3.9 %copy-start.1 = (bf16[1,1024,576]{1,2,0:T(8,128)(2,1)S(1)}, bf16[1,1024,576]{1,2,0:T(8,128)(2,1)}, u32[]{:S(2)}) copy-start(bf16[1,1024,576]{1,2,0:T(8,128)(2,1)} %param.7) | copy-start | bytes 3538948
  19.6 60.2 %collective-permute-start.2 = (f32[576,1024]{1,0:T(8,128)}, f32[576,1024]{1,0:T(8,128)}, u32[]{:S(2)}, u32[]{:S(2)}) collective-permute-start(f32[576,1024]{1,0:T(8,128)} %get-tuple-element.53), channel_id=1, source_target_pairs={{0,2},{1,3},{2,0},{3,1},{4,6},{5,7},{6,4},{7,5}} | collective-permute-start | bytes 7077896 | tf_op jit(solution)/shard_map/ppermute | solution.py:459
  58.4 1.2 copy-start.4
  59.6 1.2 copy-start.5
  79.8 47.5 %copy-start.17 = (s32[2048,128]{1,0:T(8,128)}, s32[2048,128]{1,0:T(8,128)S(1)}, u32[]{:S(2)}) copy-start(s32[2048,128]{1,0:T(8,128)S(1)} %get-tuple-element.57.t_ref) | copy-start | bytes 3145732
  79.8 47.5 %collective-permute-start.3 = (f32[576,1024]{1,0:T(8,128)}, f32[576,1024]{1,0:T(8,128)}, u32[]{:S(2)}, u32[]{:S(2)}) collective-permute-start(f32[576,1024]{1,0:T(8,128)} %collective-permute-done.2.a_ref), channel_id=1, source_target_pairs={{0,1},{1,0},{2,3},{3,2},{4,5},{5,4},{6,7},{7,6}} | collective-permute-start | bytes 7077896 | tf_op jit(solution)/shard_map/ppermute | solution.py:460
  79.9 47.4 %copy-start.7 = (s32[8,128]{1,0:T(8,128)S(1)}, s32[8,128]{1,0:T(8,128)}, u32[]{:S(2)}) copy-start(s32[8,128]{1,0:T(8,128)} %and_select_fusion.sc.idx) | copy-start | bytes 12292
  131.9 1.5 copy-start.13
  133.3 1.4 copy-start.14
  184.3 99.3 %collective-permute-start.4 = (f32[144,12288]{1,0:T(8,128)}, f32[144,12288]{1,0:T(8,128)}, u32[]{:S(2)}, u32[]{:S(2)}) collective-permute-start(f32[144,12288]{1,0:T(8,128)} %get-tuple-element.60), channel_id=1, source_target_pairs={{0,1},{1,0},{2,3},{3,2},{4,5},{5,4},{6,7},{7,6}} | collective-permute-start | bytes 21233672 | tf_op jit(solution)/shard_map/ppermute | solution.py:552
  187.9 11.3 %collective-permute-start = (f32[576,1024]{1,0:T(8,128)}, f32[576,1024]{1,0:T(8,128)}, u32[]{:S(2)}, u32[]{:S(2)}) collective-permute-start(f32[576,1024]{1,0:T(8,128)} %constant_dynamic-slice_fusion), channel_id=1, source_target_pairs={{0,1},{1,0},{2,3},{3,2},{4,5},{5,4},{6,7},{7,6}} | collective-permute-start | bytes 7077896 | tf_op jit(solution)/shard_map/ppermute | solution.py:537
  188.1 68.9 %copy-start.6 = (f32[2048,128]{1,0:T(8,128)S(1)}, f32[2048,128]{1,0:T(8,128)}, u32[]{:S(2)}) copy-start(f32[2048,128]{1,0:T(8,128)} %get-tuple-element.47.tl_ref) | copy-start | bytes 3145732
  188.1 68.9 %copy-start.10 = (s32[1,1024]{1,0:T(1,128)S(1)}, s32[1,1024]{1,0:T(1,128)}, u32[]{:S(2)}) copy-start(s32[1,1024]{1,0:T(1,128)} %on_ref.1) | copy-start | bytes 12292
  188.1 68.9 %copy-start.12 = (f32[8,128]{1,0:T(8,128)S(1)}, f32[8,128]{1,0:T(8,128)}, u32[]{:S(2)}) copy-start(f32[8,128]{1,0:T(8,128)} %copy-done.11) | copy-start | bytes 12292
  202.1 53.5 %collective-permute-start.1 = (f32[576,1024]{1,0:T(8,128)S(1)}, f32[576,1024]{1,0:T(8,128)S(1)}, u32[]{:S(2)}, u32[]{:S(2)}) collective-permute-start(f32[576,1024]{1,0:T(8,128)S(1)} %dynamic-slice_add_fusion.a_ref), channel_id=1, source_target_pairs={{0,4},{4,0},{1,5},{5,1},{2,6},{6,2},{3,7},{7,3}} | collective-permute-start | bytes 7077896 | tf_op jit(solution)/shard_map/ppermute | solution.py:539
  202.6 65.4 %collective-permute-start.5 = (f32[144,1024]{1,0:T(8,128)}, f32[144,1024]{1,0:T(8,128)S(1)}, u32[]{:S(2)}, u32[]{:S(2)}) collective-permute-start(f32[144,1024]{1,0:T(8,128)} %get-tuple-element.62), channel_id=1, source_target_pairs={{0,1},{1,0},{2,3},{3,2},{4,5},{5,4},{6,7},{7,6}} | collective-permute-start | bytes 1769480 | tf_op jit(solution)/shard_map/ppermute | solution.py:521
  202.7 65.3 %collective-permute-start.6 = (f32[144,1024]{1,0:T(8,128)}, f32[144,1024]{1,0:T(8,128)S(1)}, u32[]{:S(2)}, u32[]{:S(2)}) collective-permute-start(f32[144,1024]{1,0:T(8,128)} %get-tuple-element.63), channel_id=1, source_target_pairs={{0,2},{1,3},{2,0},{3,1},{4,6},{5,7},{6,4},{7,5}} | collective-permute-start | bytes 1769480 | tf_op jit(solution)/shard_map/ppermute | solution.py:521
  203.0 65.0 %collective-permute-start.7 = (f32[144,1024]{1,0:T(8,128)}, f32[144,1024]{1,0:T(8,128)}, u32[]{:S(2)}, u32[]{:S(2)}) collective-permute-start(f32[144,1024]{1,0:T(8,128)} %get-tuple-element.64), channel_id=1, source_target_pairs={{0,3},{1,2},{2,1},{3,0},{4,7},{5,6},{6,5},{7,4}} | collective-permute-start | bytes 1769480 | tf_op jit(solution)/shard_map/ppermute | solution.py:521
  255.6 1.4 copy-start.22
  257.0 11.0 %copy-start.8 = (s32[8,128]{1,0:T(8,128)S(1)}, s32[8,128]{1,0:T(8,128)}, u32[]{:S(2)}) copy-start(s32[8,128]{1,0:T(8,128)} %and_select_fusion.sc.idx) | copy-start | bytes 12292
  268.0 3.0 %copy-start = (f32[144,12288]{1,0:T(8,128)S(1)}, f32[144,12288]{1,0:T(8,128)}, u32[]{:S(2)}) copy-start(f32[144,12288]{1,0:T(8,128)} %get-tuple-element.65.from_ref) | copy-start | bytes 21233668
  283.6 13.2 %copy-start.3 = (bf16[576,1024]{1,0:T(8,128)(2,1)S(1)}, bf16[576,1024]{1,0:T(8,128)(2,1)}, u32[]{:S(2)}) copy-start(bf16[576,1024]{1,0:T(8,128)(2,1)} %copy-done.2) | copy-start | bytes 3538948
  (8 other events, 6.6 us)

commit v2 on v1

--- a/solution.py
+++ b/solution.py
@@ -98,14 +98,19 @@
             tl_ref[rows, :] = found
 
 
-def own_kernel(sc, l_ref, e_ref, za_ref, zb_ref, k_ref, t_ref, inv_ref, dz_ref, da_ref, db_ref, tl_ref, dl_ref):
+def own_kernel(sc, l_ref, e_ref, za_ref, zb_ref, k_ref, t_ref, inv_ref, dz_ref, gv_ref, da_ref, db_ref, tl_ref, dl_ref, kw_ref, tw_ref, acc_ref, sem):
     v, t = pl.program_id(0), pl.program_id(1)
     row = pl.multiple_of(sc[0, t] * TB, TB)
     skip = sc[2, 3]
 
+    expand(t, v, skip, sc[0, t], k_ref, t_ref, kw_ref, tw_ref)
+    seq = acc_ref.shape[2]
+    slot = lax.bitwise_xor(lax.div(row, seq), sc[2, 0])
+    place = pl.ds(pl.multiple_of(lax.rem(row, seq), TB), TB)
+
     @pl.when((v == 0) & (t >= skip))
     def _():
-        dz_ref[:, pl.ds(row, TB)] = jnp.zeros((dz_ref.shape[0], TB), F32)
+        acc_ref[slot, :, place] = jnp.zeros((acc_ref.shape[1], TB), F32)
 
     @pl.when((v == 0) & (t == 0))
     def _():
@@ -125,21 +130,30 @@
         get = lambda r, o: l_ref[0, 0, 16 * r:16 * r + 16, o:o + LANE]
         for c in range(n + 1):
             if c < n:
-                dlogits_stage(get, dl_ref, k_ref, scale, t_ref, tl_ref, row, v * VB, c)
+                dlogits_stage(get, dl_ref, kw_ref, scale, tw_ref, tl_ref, row, v * VB, c)
             if c > 0:
                 q = slice((c - 1) * SC, c * SC)
                 dl = dl_ref[:, q]
-                dz_ref[:, pl.ds(row, TB)] += lax.dot_general(
+                acc_ref[slot, :, place] += lax.dot_general(
                     e_ref[:, q], dl, (((1,), (1,)), ((), ())), preferred_element_type=F32)
                 de = jnp.dot(zc, dl, preferred_element_type=F32)
                 da_ref[:, q] += de[:half]
                 db_ref[:, q] += de[half:]
 
-
-def other_kernel(sc, z_ref, e_ref, za_ref, zb_ref, k_ref, t_ref, inv_ref, ia_ref, ib_ref, da_ref, db_ref, l_ref, dl_ref):
+    @pl.when((v == pl.num_programs(0) - 1) & (t == pl.num_programs(1) - 1))
+    def _():
+        copies = [pltpu.make_async_copy(acc_ref.at[k], out, sem.at[k]) for k, out in enumerate((dz_ref, gv_ref))]
+        for copy in copies:
+            copy.start()
+        for copy in copies:
+            copy.wait()
+
+
+def other_kernel(sc, z_ref, e_ref, za_ref, zb_ref, k_ref, t_ref, inv_ref, ia_ref, ib_ref, da_ref, db_ref, l_ref, dl_ref, kw_ref, tw_ref):
     v, t = pl.program_id(0), pl.program_id(1)
     row = pl.multiple_of(sc[1, t] * TB, TB)
     skip = sc[2, 4]
+    expand(t, v, skip, sc[1, t], k_ref, t_ref, kw_ref, tw_ref)
 
     @pl.when(t == skip)
     def _():
@@ -158,7 +172,7 @@
                 q = slice(c * SC, (c + 1) * SC)
                 l_ref[:, q] = jnp.dot(z_ref[ALL], e_ref[:, q], preferred_element_type=F32)
             if 0 < c <= n:
-                dlogits_stage(get, dl_ref, k_ref, scale, t_ref, None, row, v * VB, c - 1)
+                dlogits_stage(get, dl_ref, kw_ref, scale, tw_ref, None, row, v * VB, c - 1)
             if c > 1:
                 q = slice((c - 2) * SC, (c - 1) * SC)
                 de = jnp.dot(zc, dl_ref[:, q], preferred_element_type=F32)
@@ -174,6 +188,17 @@
 
 def xor(i, k):
     return (i + 1 - 2 * lax.rem(i, 2), lax.rem(i + 2, 4), 3 - i)[k - 1]
+
+
+def expand(t, v, skip, tile, k_ref, t_ref, kw_ref, tw_ref):
+    @pl.when((v == 0) & (t >= skip))
+    def _():
+        lane = lax.broadcasted_iota(jnp.int32, (1, LANE), 1)
+        for h in range(TB // LANE):
+            r = tile * (TB // LANE) + h
+            at = pl.ds(pl.multiple_of(r * LANE, LANE), LANE)
+            kw_ref[at, :] = columns(k_ref[pl.ds(r, 1), :])
+            tw_ref[at, :] = columns(t_ref[pl.ds(r, 1), :]) - lane
 
 
 def columns(row):
@@ -223,7 +248,7 @@
     return copy
 
 
-def prep_kernel(h_ref, g_ref, meta_ref, z32_ref, zt_ref, z_ref, all_ref, table_ref, inv_ref, got_ref, box_ref, s_sem, r_sem):
+def prep_kernel(vocab_local, h_ref, g_ref, meta_ref, z32_ref, zt_ref, z_ref, all_ref, table_ref, inv_ref, got_ref, box_ref, s_sem, r_sem):
     dp, tp = lax.axis_index("dp"), lax.axis_index("tp")
     core = lax.rem(dp, 2)
     chip = lax.div(dp, 2)
@@ -268,7 +293,7 @@
         lst = jnp.where(p < na, p, nt // 2 + p - na)
         out.append(jnp.minimum(lst, nt - 1))
         skips.append(skip)
-    row = jnp.where(lane == 0, core, jnp.where(lane == 1, dp, jnp.where(lane == 2, xor(dp, 1), jnp.where(lane == 3, skips[0], skips[1]))))
+    row = jnp.where(lane == 0, core, jnp.where(lane == 1, dp, jnp.where(lane == 2, xor(dp, 1), jnp.where(lane == 3, skips[0], jnp.where(lane == 4, skips[1], tp * vocab_local)))))
     table_ref[ALL] = jnp.zeros_like(table_ref)
     table_ref[0:1, :] = out[0]
     table_ref[1:2, :] = out[1]
@@ -281,15 +306,13 @@
     zt_ref[:, pl.ds(pl.multiple_of(other * seq, seq), seq)] = got
 
 
-def stats_kernel(vocab_local, m_ref, s_ref, all_ref, ko_ref, to_ref, kf_ref, tf_ref, lse_ref, look_ref, mine_ref, box_ref, s_sem, r_sem):
+def stats_kernel(vocab_local, m_ref, s_ref, all_ref, k_ref, t_ref, f_ref, lse_ref, look_ref, mine_ref, box_ref, s_sem, r_sem):
     dp, tp = lax.axis_index("dp"), lax.axis_index("tp")
     core = lax.rem(dp, 2)
     chip = lax.div(dp, 2)
-    tokens = m_ref.shape[0]
     seq = all_ref.shape[2]
-    nb = tokens // LANE
-    dps = [dp, xor(dp, 1), xor(dp, 2), xor(dp, 3)]
-    peers = [(t, i) for t in (tp, 1 - tp) for i in dps][1:]
+    nb = m_ref.shape[0] // LANE
+    peers = [(tp, xor(dp, 1)), (1 - tp, dp), (1 - tp, xor(dp, 1))]
     greet(peers)
     for j in range(nb):
         m = m_ref[LANE * j:LANE * j + LANE, :].T
@@ -297,8 +320,7 @@
         top = jnp.max(m, axis=0, keepdims=True)
         mine_ref[j:j + 1, :] = top
         mine_ref[nb + j:nb + j + 1, :] = over_rows(s * jnp.exp2(m - top))
-    box_ref[0] = mine_ref[ALL]
-    copies = [send(mine_ref, box_ref.at[k + 1], (s_sem, r_sem), k, peers[k]) for k in range(7)]
+    copies = [send(mine_ref, box_ref.at[k], (s_sem, r_sem), k, peers[k]) for k in range(3)]
 
     lane = lax.broadcasted_iota(jnp.int32, (1, LANE), 1)
     edge = lane * LB + tp * vocab_local
@@ -307,8 +329,9 @@
     for q in range(4):
         lo = jnp.zeros((1, LANE), F32)
         hi = jnp.zeros((1, LANE), F32)
+        who = dp if q == 0 else xor(dp, q)
         for j in range(seq // LANE):
-            ids = columns(all_ref[dps[q], 2:3, LANE * j:LANE * j + LANE])
+            ids = columns(all_ref[who, 2:3, LANE * j:LANE * j + LANE])
             lo = lo + over_rows(jnp.where(ids < edge, 1.0, 0.0))
             hi = hi + over_rows(jnp.where(ids < edge + LB, 1.0, 0.0))
         a = jnp.floor(lo * (1.0 / CH))
@@ -317,34 +340,25 @@
         steps = jnp.maximum(steps, jnp.where(hi > lo, b - a, 0.0))
     look_ref[4:5, :] = steps.astype(jnp.int32)
 
-    total = jnp.zeros((1, 1), F32)
-    for q in range(4):
-        total = total + over_lanes(all_ref[q, 1:2, :].astype(F32))
+    total = sum(over_lanes(all_ref[q, 1:2, :].astype(F32)) for q in range(4))
     shift = jnp.log(total) * LOG2E
+    base = tp * vocab_local + core * (vocab_local // 2)
+    half = nb // 2
+    for c, out in ((chip, t_ref), (1 - chip, f_ref)):
+        for j in range(nb):
+            q, o = c * 2 + j // half, LANE * (j % half)
+            on = all_ref[q, 1:2, o:o + LANE] > 0
+            out[j:j + 1, :] = jnp.where(on, all_ref[q, 0:1, o:o + LANE] - base, -MIB)
     for copy in copies:
         copy.wait()
-
-    def merged(slots):
-        ms = [box_ref[k, 0:nb, :] for k in slots]
-        ss = [box_ref[k, nb:2 * nb, :] for k in slots]
-        top = functools.reduce(jnp.maximum, ms)
-        w = [s * jnp.exp2(m - top) for s, m in zip(ss, ms)]
-        return top + jnp.log((w[0] + w[1]) + (w[2] + w[3])) * LOG2E
-
-    sets = [(merged((0, 1, 4, 5)), chip, ko_ref, to_ref), (merged((2, 3, 6, 7)), 1 - chip, kf_ref, tf_ref)]
-    base = tp * vocab_local + core * (vocab_local // 2)
-    sums = []
-    for lse, c, k_out, t_out in sets:
-        acc = jnp.zeros((1, LANE), F32)
-        for j in range(nb):
-            q, o = c * 2 + j // (nb // 2), LANE * (j % (nb // 2))
-            on = all_ref[q, 1:2, o:o + LANE] > 0
-            row = lse[j:j + 1, :]
-            acc = acc + jnp.where(on, row, 0.0)
-            k_out[LANE * j:LANE * j + LANE, :] = columns(jnp.where(on, row + shift, jnp.inf))
-            t_out[LANE * j:LANE * j + LANE, :] = columns(jnp.where(on, all_ref[q, 0:1, o:o + LANE] - base, -MIB)) - lane
-        sums.append(acc)
-    lse_ref[ALL] = jnp.broadcast_to(sums[0] + sums[1], lse_ref.shape)
+    parts = [mine_ref] + [box_ref.at[k] for k in range(3)]
+    ms = [p[0:nb, :] for p in parts]
+    top = functools.reduce(jnp.maximum, ms)
+    w = [p[nb:2 * nb, :] * jnp.exp2(m - top) for p, m in zip(parts, ms)]
+    lse = top + jnp.log((w[0] + w[1]) + (w[2] + w[3])) * LOG2E
+    live = t_ref[ALL] > 1 - MIB
+    k_ref[ALL] = jnp.where(live, lse + shift, jnp.inf)
+    lse_ref[ALL] = jnp.broadcast_to(over_rows(jnp.where(live, lse, 0.0)), lse_ref.shape)
 
 
 def final_kernel(a_ref, b_ref, h_ref, g_ref, on_ref, tl_ref, lse_ref, inv_ref, dh_ref, dg_ref, loss_ref, mine_ref, box_ref, s_sem, r_sem):
@@ -362,6 +376,7 @@
     mine_ref[ALL] = jnp.zeros_like(mine_ref)
     mine_ref[0:1, 0:d] = over_rows(part.T)
     mine_ref[1:2, 0:LANE] = over_rows(tl_ref[ALL])
+    mine_ref[2:3, 0:LANE] = lse_ref[0:1, :]
     gain = jnp.concatenate([g_ref[ALL]] * (seq // LANE), axis=1)
     w = dz * gain
     dh_ref[ALL] = (inv * (w - u * mean_rows(w * u))).astype(BF16)
@@ -382,7 +397,7 @@
         same[q] = row
         found = found + (hit + low)
     dg_ref[ALL] = same[0] + same[1] + same[2] + same[3]
-    loss = over_lanes(lse_ref[0:1, :] - found) * LN2
+    loss = over_lanes(box_ref[0, 2:3, 0:LANE] + box_ref[2, 2:3, 0:LANE] - found) * LN2
     loss_ref[ALL] = jnp.broadcast_to(loss, loss_ref.shape) * inv_ref[0:1, :]
 
 
@@ -420,8 +435,19 @@
 def solution(mesh):
     n_dp = mesh.shape["dp"]
     swap = {k: [(i, i ^ k) for i in range(n_dp)] for k in (1, 2, 3)}
-    whole = pl.BlockSpec(memory_space=pltpu.VMEM)
+
+    def blocks(*arrays):
+        return [pl.BlockSpec(a.shape, lambda i, n=len(a.shape): (0,) * n) for a in arrays]
+
     shape = jax.ShapeDtypeStruct
+
+    def single(kernel, args, outs, scratch, mib, ident=None):
+        talk = {} if ident is None else dict(collective_id=ident, has_side_effects=True)
+        return pl.pallas_call(
+            kernel, grid=(1,), in_specs=blocks(*args), out_specs=blocks(*outs), out_shape=outs, scratch_shapes=scratch,
+            compiler_params=pltpu.CompilerParams(dimension_semantics=("arbitrary",), vmem_limit_bytes=mib * MIB, **talk),
+            cost_estimate=cost(SMALL))(*args)
+
     dma = pltpu.SemaphoreType.DMA
 
     def local_step(hidden, norm_w, embed, targets, loss_mask, token_ids, grad_embed):
@@ -434,27 +460,17 @@
         et = embed.T
         ht = hidden[0].T
         gain = jnp.broadcast_to(norm_w.astype(F32)[:, None], (d, LANE))
-        talk = lambda i, mib: pltpu.CompilerParams(collective_id=i, has_side_effects=True, vmem_limit_bytes=mib * MIB)
-
-        *give, meta = pl.pallas_call(
-            sort_kernel, in_specs=[whole] * 4, out_specs=[whole] * 5,
-            out_shape=[shape((cols, seq), F32)] * 4 + [shape((8, seq), jnp.int32)],
-            scratch_shapes=[pltpu.VMEM((seq, LANE), jnp.int32), pltpu.VMEM((seq, seq), BF16), pltpu.VMEM((d, seq), F32)],
-            compiler_params=pltpu.CompilerParams(vmem_limit_bytes=40 * MIB), name="sort",
-            cost_estimate=cost(2 * d * seq * seq),
-        )(targets, loss_mask, token_ids, grad_embed[0].T)
-
-        zt32, zt_chip, z_chip, metas, table, inv_n = pl.pallas_call(
-            prep_kernel, in_specs=[whole] * 3, out_specs=[whole] * 6,
-            out_shape=[shape((d, seq), F32), shape((d, 2 * seq), BF16), shape((2 * seq, d), BF16),
-                       shape((n_dp, 8, seq), jnp.int32), shape((8, LANE), jnp.int32), shape((8, LANE), F32)],
-            scratch_shapes=[pltpu.VMEM((d, seq), F32), pltpu.VMEM((3, 8, seq), jnp.int32), dma((4,)), dma((4,))],
-            compiler_params=talk(0, 48), name="prep",
-            cost_estimate=cost(SMALL),
-        )(ht, gain, meta)
-        tp_base = lax.axis_index("tp") * vocab_local
-        spot = (lax.broadcasted_iota(jnp.int32, (8, LANE), 0) == 2) & (lax.broadcasted_iota(jnp.int32, (8, LANE), 1) == 5)
-        table = jnp.where(spot, tp_base, table)
+
+        *give, meta = single(
+            sort_kernel, (targets, loss_mask, token_ids, grad_embed[0].T),
+            [shape((cols, seq), F32)] * 4 + [shape((8, seq), jnp.int32)],
+            [pltpu.VMEM((seq, LANE), jnp.int32), pltpu.VMEM((seq, seq), BF16), pltpu.VMEM((d, seq), F32)], 48)
+
+        zt32, zt_chip, z_chip, metas, table, inv_n = single(
+            functools.partial(prep_kernel, vocab_local), (ht, gain, meta),
+            [shape((d, seq), F32), shape((d, 2 * seq), BF16), shape((2 * seq, d), BF16),
+             shape((n_dp, 8, seq), jnp.int32), shape((8, LANE), jnp.int32), shape((8, LANE), F32)],
+            [pltpu.VMEM((d, seq), F32), pltpu.VMEM((3, 8, seq), jnp.int32), dma((4,)), dma((4,))], 56, 0)
 
         far = lax.ppermute(zt32, "dp", swap[2])
         far_near = lax.ppermute(far, "dp", swap[1])
@@ -485,8 +501,9 @@
                 z=pl.BlockSpec((TB, d), lambda v, t, x: (x[r, t], 0)),
                 l=pl.BlockSpec((1, 1, TB, VB), lambda v, t, x: (x[r, t], v, 0, 0)),
                 vec=pl.BlockSpec((2 * seq, LANE), full),
+                row=pl.BlockSpec((2 * seq // LANE, LANE), full),
+                any=pl.BlockSpec(memory_space=pl.ANY),
                 inv=pl.BlockSpec((8, LANE), full),
-                dz=pl.BlockSpec((d, 2 * seq), full),
                 za=pl.BlockSpec((cols, TB), lambda v, t, x: (x[2, 1], x[r, t])),
                 zb=pl.BlockSpec((cols, TB), lambda v, t, x: (x[2, 2], x[r, t])),
                 de=pl.BlockSpec((cols, VB), lambda v, t, x: (0, v)))
@@ -494,7 +511,7 @@
         pick = lambda sp, *names: [sp[k] for k in names]
         own, other = specs(0), specs(1)
         vec = shape((2 * seq, LANE), F32)
-        ivec = shape((2 * seq, LANE), jnp.int32)
+        wide = [pltpu.VMEM((2 * seq, LANE), F32), pltpu.VMEM((2 * seq, LANE), jnp.int32)]
         de_shape = shape((cols, half), F32)
         flops = 2 * 2 * seq * half * d
 
@@ -507,33 +524,29 @@
             cost_estimate=cost(flops),
         )(table, z_chip, et)
 
-        k_own, t_own, k_far, t_far, lse_sum, look = pl.pallas_call(
-            functools.partial(stats_kernel, vocab_local),
-            in_specs=[whole] * 3, out_specs=[whole] * 6,
-            out_shape=[vec, ivec, vec, ivec, shape((8, LANE), F32), shape((8, LANE), jnp.int32)],
-            scratch_shapes=[pltpu.VMEM((4 * seq // LANE, LANE), F32), pltpu.VMEM((8, 4 * seq // LANE, LANE), F32), dma((7,)), dma((7,))],
-            compiler_params=talk(1, 32), name="stats",
-            cost_estimate=cost(SMALL),
-        )(m_own, s_own, metas)
+        rows = 2 * seq // LANE
+        k_own, t_own, t_far, lse_sum, look = single(
+            functools.partial(stats_kernel, vocab_local), (m_own, s_own, metas),
+            [shape((rows, LANE), F32), shape((rows, LANE), jnp.int32), shape((rows, LANE), jnp.int32),
+             shape((8, LANE), F32), shape((8, LANE), jnp.int32)],
+            [pltpu.VMEM((2 * rows, LANE), F32), pltpu.VMEM((3, 2 * rows, LANE), F32), dma((3,)), dma((3,))], 32, 1)
+        k_far = lax.ppermute(k_own, "dp", swap[2])
 
         lists = [give[0]]
         for k in (1, 2, 3):
             lists.append(lax.ppermute(give[k], "dp", swap[k]))
 
-        dz, da, db, tl = pl.pallas_call(
+        dz_own, dz_give, da, db, tl = pl.pallas_call(
             own_kernel,
             grid_spec=pltpu.PrefetchScalarGridSpec(
                 num_scalar_prefetch=1, grid=(nv, nt),
-                in_specs=pick(own, "l", "e", "za", "zb", "vec", "vec", "inv"), out_specs=pick(own, "dz", "de", "de", "vec"),
-                scratch_shapes=[pltpu.VMEM((TB, VB), BF16)]),
-            out_shape=[shape((d, 2 * seq), F32), de_shape, de_shape, vec],
+                in_specs=pick(own, "l", "e", "za", "zb", "row", "row", "inv"), out_specs=pick(own, "any", "any", "de", "de", "vec"),
+                scratch_shapes=[pltpu.VMEM((TB, VB), BF16), *wide, pltpu.VMEM((2, d, seq), F32), dma((2,))]),
+            out_shape=[shape((d, seq), F32), shape((d, seq), F32), de_shape, de_shape, vec],
             compiler_params=params(60), name="own",
             cost_estimate=cost(flops + flops // 2),
         )(table, l_own, et, zt_chip, zt_chip, k_own, t_own, inv_n)
 
-        core = lax.rem(lax.axis_index("dp"), 2)
-        dz_own = lax.dynamic_slice_in_dim(dz, core * seq, seq, 1)
-        dz_give = lax.dynamic_slice_in_dim(dz, (1 - core) * seq, seq, 1)
         dz_near = lax.ppermute(dz_give, "dp", swap[1])
         dz_half = dz_own + dz_near
         dz_tp = lax.ppermute(dz_half, "tp", [(0, 1), (1, 0)])
@@ -543,8 +556,8 @@
             other_kernel,
             grid_spec=pltpu.PrefetchScalarGridSpec(
                 num_scalar_prefetch=1, grid=(nv, nt),
-                in_specs=pick(other, "z", "e", "za", "zb", "vec", "vec", "inv", "de", "de"), out_specs=pick(other, "de", "de"),
-                scratch_shapes=[pltpu.VMEM((TB, VB), F32), pltpu.VMEM((TB, VB), BF16)]),
+                in_specs=pick(other, "z", "e", "za", "zb", "row", "row", "inv", "de", "de"), out_specs=pick(other, "de", "de"),
+                scratch_shapes=[pltpu.VMEM((TB, VB), F32), pltpu.VMEM((TB, VB), BF16), *wide]),
             out_shape=[de_shape, de_shape],
             compiler_params=params(60), name="other",
             cost_estimate=cost(flops + flops // 2),
@@ -571,13 +584,10 @@
 
         de_t = lookup(lambda x, b: x[2, 0] * nb + b, da)
 
-        dht, dg, loss = pl.pallas_call(
-            final_kernel, in_specs=[whole] * 8, out_specs=[whole] * 3,
-            out_shape=[shape((d, seq), BF16), shape((1, d), F32), shape((1, LANE), F32)],
-            scratch_shapes=[pltpu.VMEM((8, 640), F32), pltpu.VMEM((8, 8, 640), F32), dma((7,)), dma((7,))],
-            compiler_params=talk(2, 48), name="final",
-            cost_estimate=cost(SMALL),
-        )(dz_half, dz_tp, ht, gain, loss_mask, tl, lse_sum, inv_n)
+        dht, dg, loss = single(
+            final_kernel, (dz_half, dz_tp, ht, gain, loss_mask, tl, lse_sum, inv_n),
+            [shape((d, seq), BF16), shape((1, d), F32), shape((1, LANE), F32)],
+            [pltpu.VMEM((8, 640), F32), pltpu.VMEM((8, 8, 640), F32), dma((7,)), dma((7,))], 56, 2)
 
         de_t = lookup(lambda x, b: (1 - x[2, 0]) * nb + b, got, de_t)
         return loss[0, 0], dht.T[None], dg[0], de_t.T

time: 300 us -> 297 us (0.990)
  Pallas kernels: 205 us -> 196 us
  waiting for transfers between devices: 62.2 us -> 70.8 us
    pallas_call x4, Pallas kernels: 40.2 us -> 32.5 us  [single(): pl.pallas_call(kernel, grid=(1,), in_specs=blocks(*args), out_specs=block...]
    ppermute x1, waiting for transfers between devices: 0.01 us -> 6.15 us  [local_step(): far = lax.ppermute(zt32, 'dp', swap[2])]
    dynamic_slice x1 -> x0, local copies, waits for them, and re-layouts: 3.36 us -> none  [local_step(): dz_give = lax.dynamic_slice_in_dim(dz, (1 - core) * seq, seq, 1)]
    ppermute x1, waiting for transfers between devices: 11.1 us -> 14.5 us  [local_step(): dz_near = lax.ppermute(dz_give, 'dp', swap[1])]
    unnamed x49 -> x45, local copies, waits for them, and re-layouts: 18.6 us -> 17.9 us
  transfers between devices with their start and end apart: 8 -> 9, of which waited for: 2 -> 3; matrix products, arithmetic and copies ran while one was open for 3% -> 1% of each run, Pallas kernels for 41% -> 40%
where the time goes in v2:
time: 297 us; the launch traced here: 296 us
  Pallas kernels  196 us (66%)
  waiting for transfers between devices  70.8 us (24%)
  local copies, waits for them, and re-layouts  19.4 us (7%)
  starting transfers between devices  6.02 us (2%)
    ppermute x1, waiting for transfers between devices, local_step(): dz_tp = lax.ppermute(dz_half, 'tp', [(0, 1), (1, 0)])  50.2 us
    pallas_call x1, Pallas kernels, local_step(): pl.pallas_call(other_kernel, grid_spec=pltpu.PrefetchScalarGridSpec(num_s...  49.7 us
    pallas_call x1, Pallas kernels, local_step(): pl.pallas_call(own_kernel, grid_spec=pltpu.PrefetchScalarGridSpec(num_sca...  47.3 us
    pallas_call x1, Pallas kernels, local_step(): pl.pallas_call(logits_kernel, grid_spec=pltpu.PrefetchScalarGridSpec(num_...  37.5 us
    pallas_call x4, Pallas kernels, single(): pl.pallas_call(kernel, grid=(1,), in_specs=blocks(*args), out_specs=block...  32.5 us
    pallas_call x2, Pallas kernels, lookup(): pl.pallas_call(functools.partial(lookup_kernel, top), grid_spec=pltpu.Pre...  24.5 us
    unnamed x45, local copies, waits for them, and re-layouts  17.9 us
    ppermute x1, waiting for transfers between devices, local_step(): dz_near = lax.ppermute(dz_give, 'dp', swap[1])  14.5 us
  transfers between devices with their start and end apart: 9, of which 3 were waited for; matrix products, arithmetic and copies ran while one was open for 1% of the time, Pallas kernels for 40%

profile of v2, /device:TPU:0, one launch (start us, length us, event | category | flops | bytes accessed | tf_op | source)
XLA Modules:
  0.0 295.6 jit_solution(13716920144643156579)
XLA Ops:
  0.6 1.3 copy-done.1
  4.0 3.6 %shard_map.102 = (f32[144,1024]{1,0:T(8,128)S(1)}, f32[144,1024]{1,0:T(8,128)}, f32[144,1024]{1,0:T(8,128)}, f32[144,1024]{1,0:T(8,128)S(1)}, s32[8,1024]{1,0:T(8,128)S(1)}) custom-call(s32[1,1024]{1,0:T(1,128)S(1)} %copy-done.9, s32[1,1024]{1,0:T(1,128)S(1)} %copy-done.8, s32[1,1024]{1,0:T(1,128)S(1)} %copy-done.10, bf16[576,1024]{1,0:T(8,128)(2,1)S(1)} %bitcast.13), custom_call_target="tpu_custom_call" | custom-call | flops 268435456 | bytes 1048576 | tf_op jit(solution)/shard_map/pallas_call | solution.py:446
  8.1 1.5 broadcast_in_dim.4.g_ref
  9.7 12.7 %shard_map.103 = (f32[576,1024]{1,0:T(8,128)}, bf16[576,2048]{1,0:T(8,128)(2,1)}, bf16[2048,576]{1,0:T(8,128)(2,1)}, s32[4,8,1024]{2,1,0:T(8,128)}, s32[8,128]{1,0:T(8,128)}, /*index=5*/f32[8,128]{1,0:T(8,128)}) custom-call(bf16[576,1024]{1,0:T(8,128)(2,1)} %bitcast.15, f32[576,128]{1,0:T(8,128)} %broadcast_in_dim.4.g_ref, s32[8,1024]{1,0:T(8,128)} %copy-done.7), custom_call_target="tpu_custom_call" | custom-call | flops 268435456 | bytes 1048576 | tf_op jit(solution)/shard_map/pallas_call | solution.py:446
  22.7 37.5 %logits.1 = (f32[8,3,256,4096]{3,2,1,0:T(8,128)}, f32[2048,128]{1,0:T(8,128)}, f32[2048,128]{1,0:T(8,128)}) custom-call(s32[8,128]{1,0:T(8,128)} %get-tuple-element.36.sc.idx, bf16[2048,576]{1,0:T(8,128)(2,1)} %get-tuple-element.37.z_ref, bf16[576,24576]{1,0:T(8,128)(2,1)} %bitcast.18), custom_call_target="tpu_custom_call" | custom-call | flops 28991029248 | bytes 1048576 | tf_op jit(solution)/shard_map/logits/pallas_call | solution.py:518
  62.7 4.5 %shard_map.104 = (f32[16,128]{1,0:T(8,128)S(1)}, s32[16,128]{1,0:T(8,128)S(1)}, s32[16,128]{1,0:T(8,128)S(1)}, f32[8,128]{1,0:T(8,128)S(1)}, s32[8,128]{1,0:T(8,128)S(1)}) custom-call(f32[2048,128]{1,0:T(8,128)S(1)} %copy-done.3, f32[2048,128]{1,0:T(8,128)S(1)} %copy-done.4, s32[4,8,1024]{2,1,0:T(8,128)S(1)} %copy-done.2), custom_call_target="tpu_custom_call" | custom-call | flops 268435456 | bytes 1048576 | tf_op jit(solution)/shard_map/pallas_call | solution.py:446
  68.4 1.6 collective-permute-start.4
  70.0 6.1 %collective-permute-done.2.a_ref = f32[576,1024]{1,0:T(8,128)S(1)} collective-permute-done((f32[576,1024]{1,0:T(8,128)}, f32[576,1024]{1,0:T(8,128)S(1)}, u32[]{:S(2)}, u32[]{:S(2)}) %collective-permute-start.2) | collective-permute-done | bytes 2359328 | tf_op jit(solution)/shard_map/ppermute | solution.py:475
  76.2 47.3 %own.1 = (f32[576,1024]{1,0:T(8,128)}, f32[576,1024]{1,0:T(8,128)}, f32[144,12288]{1,0:T(8,128)}, f32[144,12288]{1,0:T(8,128)}, f32[2048,128]{1,0:T(8,128)}) custom-call(s32[8,128]{1,0:T(8,128)} %get-tuple-element.36.sc.idx, f32[8,3,256,4096]{3,2,1,0:T(8,128)} %get-tuple-element.38.l_ref, bf16[576,24576]{1,0:T(8,128)(2,1)} %bitcast.19, ...), custom_call_target="tpu_custom_call" | custom-call | flops 43486543872 | bytes 1048576 | tf_op jit(solution)/shard_map/own/pallas_call | solution.py:539
  123.5 4.2 %arrange.1 = (bf16[576,2048]{1,0:T(8,128)(2,1)S(1)}, bf16[2048,576]{1,0:T(8,128)(2,1)S(1)}) custom-call(s32[8,128]{1,0:T(8,128)S(1)} %copy-done.5, f32[576,1024]{1,0:T(8,128)S(1)} %collective-permute-done.2.a_ref, f32[576,1024]{1,0:T(8,128)} %collective-permute-done.3.b_ref), custom_call_target="tpu_custom_call" | custom-call | flops 268435456 | bytes 1048576 | tf_op jit(solution)/shard_map/arrange/pallas_call | solution.py:482
  127.8 1.5 copy-done.12
  129.2 1.4 copy-done.13
  131.2 49.7 %other.1 = (f32[144,12288]{1,0:T(8,128)}, f32[144,12288]{1,0:T(8,128)}) custom-call(s32[8,128]{1,0:T(8,128)} %get-tuple-element.36.sc.idx, bf16[2048,576]{1,0:T(8,128)(2,1)} %copy-done.12, bf16[576,24576]{1,0:T(8,128)(2,1)} %bitcast.20, bf16[576,2048]{1,0:T(8,128)(2,1)} %copy-done.13, bf16[576,2048]{1,0:T(8,128)(2,1)} %copy-done.13, f32[16,128]{1,0:T(8,128)} %copy-done.20, ...), custom_call_target="tpu_custom_call" | custom-call | flops 43486543872 | bytes 1048576 | tf_op jit(solution)/shard_map/other/pallas_call | solution.py:555
  181.6 14.5 %collective-permute-done = f32[576,1024]{1,0:T(8,128)S(1)} collective-permute-done((f32[576,1024]{1,0:T(8,128)}, f32[576,1024]{1,0:T(8,128)S(1)}, u32[]{:S(2)}, u32[]{:S(2)}) %collective-permute-start) | collective-permute-done | bytes 2359328 | tf_op jit(solution)/shard_map/ppermute | solution.py:550
  196.5 1.5 collective-permute-start.1
  198.7 1.2 collective-permute-start.8
  199.9 50.2 %collective-permute-done.1.b_ref = f32[576,1024]{1,0:T(8,128)S(1)} collective-permute-done((f32[576,1024]{1,0:T(8,128)S(1)}, f32[576,1024]{1,0:T(8,128)S(1)}, u32[]{:S(2)}, u32[]{:S(2)}) %collective-permute-start.1) | collective-permute-done | bytes 2359328 | tf_op jit(solution)/shard_map/ppermute | solution.py:552
  250.1 1.4 copy-done.19
  251.5 11.7 %shard_map.105 = (bf16[576,1024]{1,0:T(8,128)(2,1)}, f32[1,576]{1,0:T(1,128)}, f32[1,128]{1,0:T(1,128)}) custom-call(f32[576,1024]{1,0:T(8,128)} %copy-done.17, f32[576,1024]{1,0:T(8,128)} %copy-done.19, bf16[576,1024]{1,0:T(8,128)(2,1)} %bitcast.16, f32[576,128]{1,0:T(8,128)} %broadcast_in_dim.4.g_ref, s32[1,1024]{1,0:T(1,128)} %on_ref.1, ...), custom_call_target="tpu_custom_call" | custom-call | flops 268435456 | bytes 1048576 | tf_op jit(solution)/shard_map/pallas_call | solution.py:446
  263.3 1.3 reduce
  264.6 3.0 %copy-done = f32[144,12288]{1,0:T(8,128)S(1)} copy-done((f32[144,12288]{1,0:T(8,128)S(1)}, f32[144,12288]{1,0:T(8,128)}, u32[]{:S(2)}) %copy-start) | copy-done | bytes 7077912
  267.6 11.5 %lookup.2.rest_0_ = f32[144,24576]{1,0:T(8,128)} custom-call(s32[8,128]{1,0:T(8,128)S(1)} %copy-done.6, s32[8,128]{1,0:T(8,128)S(1)} %get-tuple-element.53.look, f32[144,12288]{1,0:T(8,128)S(1)} %copy-done, f32[144,1024]{1,0:T(8,128)S(1)} %get-tuple-element.61.g1, f32[144,1024]{1,0:T(8,128)S(1)} %collective-permute-done.6.g2, ...), custom_call_target="tpu_custom_call" | custom-call | flops 3623878656 | bytes 1048576 | tf_op jit(solution)/shard_map/lookup/pallas_call | solution.py:571
  279.1 13.0 %lookup.3 = f32[144,24576]{1,0:T(8,128)} custom-call(s32[8,128]{1,0:T(8,128)S(1)} %copy-done.6, s32[8,128]{1,0:T(8,128)S(1)} %get-tuple-element.53.look, f32[144,12288]{1,0:T(8,128)} %collective-permute-done.5.from_ref, f32[144,1024]{1,0:T(8,128)S(1)} %get-tuple-element.61.g1, ...), custom_call_target="tpu_custom_call", output_to_operand_aliasing={{}: (8, {})} | custom-call | flops 3623878656 | bytes 1048576 | tf_op jit(solution)/shard_map/lookup/pallas_call | solution.py:571
  292.1 2.4 copy.16
  (52 shorter events, 9.0 us)
Async XLA Ops:
  0.6 1.3 copy-start.1
  22.3 53.8 %collective-permute-start.2 = (f32[576,1024]{1,0:T(8,128)}, f32[576,1024]{1,0:T(8,128)S(1)}, u32[]{:S(2)}, u32[]{:S(2)}) collective-permute-start(f32[576,1024]{1,0:T(8,128)} %get-tuple-element.54), channel_id=1, source_target_pairs={{0,2},{1,3},{2,0},{3,1},{4,6},{5,7},{6,4},{7,5}} | collective-permute-start | bytes 7077896 | tf_op jit(solution)/shard_map/ppermute | solution.py:475
  22.7 37.5 %copy-start.2 = (s32[4,8,1024]{2,1,0:T(8,128)S(1)}, s32[4,8,1024]{2,1,0:T(8,128)}, u32[]{:S(2)}) copy-start(s32[4,8,1024]{2,1,0:T(8,128)} %get-tuple-element.42.all_ref) | copy-start | bytes 393220
  60.3 1.2 copy-start.3
  61.5 1.2 copy-start.4
  68.4 7.8 %copy-start.11 = (f32[8,128]{1,0:T(8,128)}, f32[8,128]{1,0:T(8,128)S(1)}, u32[]{:S(2)}) copy-start(f32[8,128]{1,0:T(8,128)S(1)} %get-tuple-element.49.lse_ref) | copy-start | bytes 12292
  68.4 7.8 %copy-start.15 = (f32[16,128]{1,0:T(8,128)}, f32[16,128]{1,0:T(8,128)S(1)}, u32[]{:S(2)}) copy-start(f32[16,128]{1,0:T(8,128)S(1)} %get-tuple-element.43.k_ref) | copy-start | bytes 24580
  68.4 62.3 %collective-permute-start.4 = (f32[16,128]{1,0:T(8,128)S(1)}, f32[16,128]{1,0:T(8,128)S(1)}, u32[]{:S(2)}, u32[]{:S(2)}) collective-permute-start(f32[16,128]{1,0:T(8,128)S(1)} %get-tuple-element.43.k_ref), channel_id=1, source_target_pairs={{0,2},{1,3},{2,0},{3,1},{4,6},{5,7},{6,4},{7,5}} | collective-permute-start | bytes 24584 | tf_op jit(solution)/shard_map/ppermute | solution.py:533
  76.2 47.3 %collective-permute-start.3 = (f32[576,1024]{1,0:T(8,128)S(1)}, f32[576,1024]{1,0:T(8,128)}, u32[]{:S(2)}, u32[]{:S(2)}) collective-permute-start(f32[576,1024]{1,0:T(8,128)S(1)} %collective-permute-done.2.a_ref), channel_id=1, source_target_pairs={{0,1},{1,0},{2,3},{3,2},{4,5},{5,4},{6,7},{7,6}} | collective-permute-start | bytes 7077896 | tf_op jit(solution)/shard_map/ppermute | solution.py:476
  76.2 47.3 %copy-start.5 = (s32[8,128]{1,0:T(8,128)S(1)}, s32[8,128]{1,0:T(8,128)}, u32[]{:S(2)}) copy-start(s32[8,128]{1,0:T(8,128)} %get-tuple-element.36.sc.idx) | copy-start | bytes 12292
  127.8 1.5 copy-start.12
  129.2 1.4 copy-start.13
  131.2 64.8 %copy-start.18 = (f32[576,1024]{1,0:T(8,128)S(1)}, f32[576,1024]{1,0:T(8,128)}, u32[]{:S(2)}) copy-start(f32[576,1024]{1,0:T(8,128)} %get-tuple-element.46) | copy-start | bytes 7077892
  181.0 98.1 %collective-permute-start.5 = (f32[144,12288]{1,0:T(8,128)}, f32[144,12288]{1,0:T(8,128)}, u32[]{:S(2)}, u32[]{:S(2)}) collective-permute-start(f32[144,12288]{1,0:T(8,128)} %get-tuple-element.60), channel_id=1, source_target_pairs={{0,1},{1,0},{2,3},{3,2},{4,5},{5,4},{6,7},{7,6}} | collective-permute-start | bytes 21233672 | tf_op jit(solution)/shard_map/ppermute | solution.py:565
  181.5 14.5 %collective-permute-start = (f32[576,1024]{1,0:T(8,128)}, f32[576,1024]{1,0:T(8,128)S(1)}, u32[]{:S(2)}, u32[]{:S(2)}) collective-permute-start(f32[576,1024]{1,0:T(8,128)} %get-tuple-element.47), channel_id=1, source_target_pairs={{0,1},{1,0},{2,3},{3,2},{4,5},{5,4},{6,7},{7,6}} | collective-permute-start | bytes 7077896 | tf_op jit(solution)/shard_map/ppermute | solution.py:550
  196.5 53.6 %copy-start.17 = (f32[576,1024]{1,0:T(8,128)}, f32[576,1024]{1,0:T(8,128)S(1)}, u32[]{:S(2)}) copy-start(f32[576,1024]{1,0:T(8,128)S(1)} %add.3.a_ref) | copy-start | bytes 7077892
  196.5 53.5 %collective-permute-start.1 = (f32[576,1024]{1,0:T(8,128)S(1)}, f32[576,1024]{1,0:T(8,128)S(1)}, u32[]{:S(2)}, u32[]{:S(2)}) collective-permute-start(f32[576,1024]{1,0:T(8,128)S(1)} %add.3.a_ref), channel_id=1, source_target_pairs={{0,4},{4,0},{1,5},{5,1},{2,6},{6,2},{3,7},{7,3}} | collective-permute-start | bytes 7077896 | tf_op jit(solution)/shard_map/ppermute | solution.py:552
  198.0 66.5 %collective-permute-start.6 = (f32[144,1024]{1,0:T(8,128)}, f32[144,1024]{1,0:T(8,128)S(1)}, u32[]{:S(2)}, u32[]{:S(2)}) collective-permute-start(f32[144,1024]{1,0:T(8,128)} %get-tuple-element.62), channel_id=1, source_target_pairs={{0,1},{1,0},{2,3},{3,2},{4,5},{5,4},{6,7},{7,6}} | collective-permute-start | bytes 1769480 | tf_op jit(solution)/shard_map/ppermute | solution.py:537
  198.1 66.4 %collective-permute-start.7 = (f32[144,1024]{1,0:T(8,128)}, f32[144,1024]{1,0:T(8,128)S(1)}, u32[]{:S(2)}, u32[]{:S(2)}) collective-permute-start(f32[144,1024]{1,0:T(8,128)} %get-tuple-element.63), channel_id=1, source_target_pairs={{0,2},{1,3},{2,0},{3,1},{4,6},{5,7},{6,4},{7,5}} | collective-permute-start | bytes 1769480 | tf_op jit(solution)/shard_map/ppermute | solution.py:537
  198.7 65.9 %collective-permute-start.8 = (f32[144,1024]{1,0:T(8,128)S(1)}, f32[144,1024]{1,0:T(8,128)S(1)}, u32[]{:S(2)}, u32[]{:S(2)}) collective-permute-start(f32[144,1024]{1,0:T(8,128)S(1)} %get-tuple-element.64), channel_id=1, source_target_pairs={{0,3},{1,2},{2,1},{3,0},{4,7},{5,6},{6,5},{7,4}} | collective-permute-start | bytes 1769480 | tf_op jit(solution)/shard_map/ppermute | solution.py:537
  250.0 1.5 copy-start.19
  251.5 13.0 %copy-start.6 = (s32[8,128]{1,0:T(8,128)S(1)}, s32[8,128]{1,0:T(8,128)}, u32[]{:S(2)}) copy-start(s32[8,128]{1,0:T(8,128)} %get-tuple-element.36.sc.idx) | copy-start | bytes 12292
  264.5 3.0 %copy-start = (f32[144,12288]{1,0:T(8,128)S(1)}, f32[144,12288]{1,0:T(8,128)}, u32[]{:S(2)}) copy-start(f32[144,12288]{1,0:T(8,128)} %get-tuple-element.65.from_ref) | copy-start | bytes 21233668
  279.1 13.0 %copy-start.21 = (f32[1,128]{1,0:T(1,128)S(1)}, f32[1,128]{1,0:T(1,128)}, u32[]{:S(2)}) copy-start(f32[1,128]{1,0:T(1,128)} %get-tuple-element.50) | copy-start | bytes 1540
  (7 other events, 4.5 us)

commit v3 on v2

--- a/solution.py
+++ b/solution.py
@@ -12,14 +12,18 @@
 LOG2E = 1.4426950408889634
 LN2 = 0.6931471805599453
 TB = 256
-VB = 4096
+VB = 6144
 SC = 512
+SF = 1024
+LW = 2048
 LB = 1024
 CH = 128
+ST = 16
 LANE = 128
 ALL = Ellipsis
 MIB = 2**20
 SMALL = 2**28
+GRANT = 60 * 1024 * 1024
 F32 = jnp.float32
 BF16 = jnp.bfloat16
 
@@ -40,8 +44,8 @@
     return pl.CostEstimate(flops=int(flops), bytes_accessed=MIB, transcendentals=0)
 
 
-def params(vmem_mib, n=2):
-    return pltpu.CompilerParams(dimension_semantics=("arbitrary",) * n, vmem_limit_bytes=vmem_mib * MIB)
+def params(n=2):
+    return pltpu.CompilerParams(dimension_semantics=("arbitrary",) * n, vmem_limit_bytes=GRANT)
 
 
 def stats_stage(l_ref, m_ref, s_ref, row, c):
@@ -79,15 +83,15 @@
                 stats_stage(l_ref, m_ref, s_ref, row, c - 1)
 
 
-def dlogits_stage(get, dl_ref, k_ref, scale, t_ref, tl_ref, row, base, c):
+def dlogits_stage(get, dl_ref, k_ref, scale, t_ref, tl_ref, row, base, c, width):
     for r in range(TB // 16):
         rows = pl.ds(row + 16 * r, 16)
         shift = k_ref[rows, :]
         target = t_ref[rows, :] - base
         if tl_ref is not None:
             found = tl_ref[rows, :]
-        for j in range(SC // LANE):
-            o = c * SC + LANE * j
+        for j in range(width // LANE):
+            o = c * width + LANE * j
             x = get(r, o)
             hit = target == o
             p = jnp.exp2(x - shift)
@@ -130,7 +134,7 @@
         get = lambda r, o: l_ref[0, 0, 16 * r:16 * r + 16, o:o + LANE]
         for c in range(n + 1):
             if c < n:
-                dlogits_stage(get, dl_ref, kw_ref, scale, tw_ref, tl_ref, row, v * VB, c)
+                dlogits_stage(get, dl_ref, kw_ref, scale, tw_ref, tl_ref, row, v * VB, c, SC)
             if c > 0:
                 q = slice((c - 1) * SC, c * SC)
                 dl = dl_ref[:, q]
@@ -165,25 +169,40 @@
         zc = jnp.concatenate([za_ref[ALL], zb_ref[ALL]], axis=0)
         half = za_ref.shape[0]
         scale = jnp.concatenate([inv_ref[ALL], inv_ref[ALL]], axis=0)
-        n = VB // SC
+        n = VB // SF
         get = lambda r, o: l_ref[16 * r:16 * r + 16, o:o + LANE] * LOG2E
         for c in range(n + 2):
             if c < n:
-                q = slice(c * SC, (c + 1) * SC)
+                q = slice(c * SF, (c + 1) * SF)
                 l_ref[:, q] = jnp.dot(z_ref[ALL], e_ref[:, q], preferred_element_type=F32)
             if 0 < c <= n:
-                dlogits_stage(get, dl_ref, kw_ref, scale, tw_ref, None, row, v * VB, c - 1)
+                dlogits_stage(get, dl_ref, kw_ref, scale, tw_ref, None, row, v * VB, c - 1, SF)
             if c > 1:
-                q = slice((c - 2) * SC, (c - 1) * SC)
+                q = slice((c - 2) * SF, (c - 1) * SF)
                 de = jnp.dot(zc, dl_ref[:, q], preferred_element_type=F32)
                 da_ref[:, q] += de[:half]
                 db_ref[:, q] += de[half:]
 
 
-def arrange_kernel(idx, a_ref, b_ref, zt_ref, z_ref):
-    x = jnp.where(pl.program_id(0) == 0, a_ref[ALL], b_ref[ALL])
-    zt_ref[ALL] = x.astype(BF16)
-    z_ref[ALL] = x.T.astype(BF16)
+def swap_kernel(own_ref, give_ref, a_ref, b_ref, zt_ref, z_ref, dz_ref, got_ref, s_sem, r_sem):
+    dp, tp = lax.axis_index("dp"), lax.axis_index("tp")
+    i, n = pl.program_id(0), pl.num_programs(0)
+    peer = (tp, xor(dp, 1))
+    copy = link(give_ref, got_ref, (s_sem, r_sem), 0, peer)
+
+    @pl.when(i == 0)
+    def _():
+        greet([peer])
+        copy.start()
+
+    z = jnp.where(i < 4, a_ref[ALL], b_ref[ALL]).astype(BF16)
+    zt_ref[ALL] = z
+    z_ref[ALL] = z.T
+
+    @pl.when(i == n - 1)
+    def _():
+        copy.wait()
+        dz_ref[ALL] = own_ref[ALL] + got_ref[ALL]
 
 
 def xor(i, k):
@@ -205,7 +224,7 @@
     return jnp.broadcast_to(row, (LANE, LANE)).T
 
 
-def sort_kernel(t_ref, m_ref, i_ref, ge_ref, o1, o2, o3, o4, meta_ref, key_ref, perm_ref, sorted_ref):
+def sort_lists(i_ref, ge_ref, outs, ids_ref, key_ref, perm_ref, sorted_ref):
     seq = i_ref.shape[1]
     nb = seq // LANE
     lane = lax.broadcasted_iota(jnp.int32, (1, LANE), 1)
@@ -217,18 +236,16 @@
     for j in range(nb):
         before = before + jnp.where(rows[j] < keys, 1.0, 0.0)
     rank = jnp.broadcast_to(over_lanes(before), (seq, LANE)).astype(jnp.int32)
-    meta_ref[ALL] = jnp.zeros_like(meta_ref)
-    meta_ref[0:1, :] = t_ref[ALL]
-    meta_ref[1:2, :] = m_ref[ALL]
+    ids_ref[ALL] = jnp.zeros_like(ids_ref)
     for j in range(nb):
         hit = rank == lane + LANE * j
         perm_ref[:, LANE * j:LANE * j + LANE] = jnp.where(hit, 1.0, 0.0).astype(BF16)
         place = over_rows(jnp.where(hit, keys, 0))
-        meta_ref[2:3, LANE * j:LANE * j + LANE] = lax.shift_right_logical(place, seq.bit_length() - 1)
+        ids_ref[0:1, LANE * j:LANE * j + LANE] = lax.shift_right_logical(place, seq.bit_length() - 1)
     sorted_ref[ALL] = jnp.dot(ge_ref[ALL], perm_ref[ALL], preferred_element_type=F32)
     dp = lax.axis_index("dp")
-    cols = o1.shape[0]
-    for k, o in enumerate((o1, o2, o3, o4)):
+    cols = outs[0].shape[0]
+    for k, o in enumerate(outs):
         who = dp if k == 0 else xor(dp, k)
         o[ALL] = sorted_ref[pl.ds(pl.multiple_of(who * cols, 8), cols), :]
 
@@ -241,31 +258,41 @@
 
 
 def send(src, dst, sems, k, peer):
-    copy = pltpu.make_async_remote_copy(
+    copy = link(src, dst, sems, k, peer)
+    copy.start()
+    return copy
+
+
+def link(src, dst, sems, k, peer):
+    return pltpu.make_async_remote_copy(
         src_ref=src, dst_ref=dst, send_sem=sems[0].at[k], recv_sem=sems[1].at[k],
         device_id=peer, device_id_type=pl.DeviceIdType.MESH)
-    copy.start()
-    return copy
-
-
-def prep_kernel(vocab_local, h_ref, g_ref, meta_ref, z32_ref, zt_ref, z_ref, all_ref, table_ref, inv_ref, got_ref, box_ref, s_sem, r_sem):
+
+
+def prep_kernel(vocab_local, h_ref, g_ref, t_ref, m_ref, i_ref, ge_ref, z32_ref, zt_ref, z_ref, all_ref, table_ref, inv_ref, o1, o2, o3, o4,
+                meta_ref, ids_ref, key_ref, perm_ref, sorted_ref, got_ref, box_ref, id_box_ref, s_sem, r_sem):
     dp, tp = lax.axis_index("dp"), lax.axis_index("tp")
     core = lax.rem(dp, 2)
     chip = lax.div(dp, 2)
-    _, seq = h_ref.shape
+    d, seq = h_ref.shape
     at = lambda i: (tp, i)
     peers = [at(xor(dp, k)) for k in (1, 2, 3)]
+    meta_ref[ALL] = jnp.zeros_like(meta_ref)
+    meta_ref[0:1, :] = t_ref[ALL]
+    meta_ref[1:2, :] = m_ref[ALL]
     greet(peers)
     sems = (s_sem, r_sem)
     copies = [send(meta_ref, box_ref.at[k], sems, k, peers[k]) for k in range(3)]
     x = h_ref[ALL].astype(F32)
     inv = lax.rsqrt(mean_rows(x * x) + RMS_EPS)
-    gain = jnp.concatenate([g_ref[ALL]] * (seq // LANE), axis=1)
+    gain = jnp.concatenate([jnp.broadcast_to(g_ref[ALL].astype(F32)[None], (LANE, d)).T] * (seq // LANE), axis=1)
     z = (x * inv * gain).astype(BF16)
     z32_ref[ALL] = z.astype(F32)
     z_ref[pl.ds(pl.multiple_of(core * seq, seq), seq), :] = z.T
     copies.append(send(z32_ref, got_ref, sems, 3, peers[0]))
     zt_ref[:, pl.ds(pl.multiple_of(core * seq, seq), seq)] = z
+    sort_lists(i_ref, ge_ref, (o1, o2, o3, o4), ids_ref, key_ref, perm_ref, sorted_ref)
+    id_copies = [send(ids_ref, id_box_ref.at[k], sems, k + 4, peers[k]) for k in range(3)]
     for copy in copies[:3]:
         copy.wait()
     all_ref[dp] = meta_ref[ALL]
@@ -304,6 +331,11 @@
     got = got_ref[ALL].astype(BF16)
     z_ref[pl.ds(pl.multiple_of(other * seq, seq), seq), :] = got.T
     zt_ref[:, pl.ds(pl.multiple_of(other * seq, seq), seq)] = got
+    for copy in id_copies:
+        copy.wait()
+    all_ref[dp, 2:3, :] = ids_ref[0:1, :]
+    for k in range(3):
+        all_ref[xor(dp, k + 1), 2:3, :] = id_box_ref[k, 0:1, :]
 
 
 def stats_kernel(vocab_local, m_ref, s_ref, all_ref, k_ref, t_ref, f_ref, lse_ref, look_ref, mine_ref, box_ref, s_sem, r_sem):
@@ -334,10 +366,9 @@
             ids = columns(all_ref[who, 2:3, LANE * j:LANE * j + LANE])
             lo = lo + over_rows(jnp.where(ids < edge, 1.0, 0.0))
             hi = hi + over_rows(jnp.where(ids < edge + LB, 1.0, 0.0))
-        a = jnp.floor(lo * (1.0 / CH))
-        b = jnp.floor((hi + (CH - 1)) * (1.0 / CH))
+        a = jnp.floor(lo * (1.0 / ST)) * ST
         look_ref[q:q + 1, :] = a.astype(jnp.int32)
-        steps = jnp.maximum(steps, jnp.where(hi > lo, b - a, 0.0))
+        steps = jnp.maximum(steps, jnp.floor((hi - a + (CH - 1)) * (1.0 / CH)))
     look_ref[4:5, :] = steps.astype(jnp.int32)
 
     total = sum(over_lanes(all_ref[q, 1:2, :].astype(F32)) for q in range(4))
@@ -377,11 +408,11 @@
     mine_ref[0:1, 0:d] = over_rows(part.T)
     mine_ref[1:2, 0:LANE] = over_rows(tl_ref[ALL])
     mine_ref[2:3, 0:LANE] = lse_ref[0:1, :]
-    gain = jnp.concatenate([g_ref[ALL]] * (seq // LANE), axis=1)
+    box_ref[0] = mine_ref[ALL]
+    copies = [send(mine_ref, box_ref.at[k + 1], (s_sem, r_sem), k, peers[k]) for k in range(7)]
+    gain = jnp.concatenate([jnp.broadcast_to(g_ref[ALL].astype(F32)[None], (LANE, d)).T] * (seq // LANE), axis=1)
     w = dz * gain
     dh_ref[ALL] = (inv * (w - u * mean_rows(w * u))).astype(BF16)
-    box_ref[0] = mine_ref[ALL]
-    copies = [send(mine_ref, box_ref.at[k + 1], (s_sem, r_sem), k, peers[k]) for k in range(7)]
     for copy in copies:
         copy.wait()
     same = [jnp.zeros((1, d), F32)] * 4
@@ -396,40 +427,52 @@
             low = jnp.where(dps[k] == q, box_ref[k + 4, 1:2, 0:LANE], low)
         same[q] = row
         found = found + (hit + low)
-    dg_ref[ALL] = same[0] + same[1] + same[2] + same[3]
+    dg_ref[ALL] = (same[0] + same[1] + same[2] + same[3])[0]
     loss = over_lanes(box_ref[0, 2:3, 0:LANE] + box_ref[2, 2:3, 0:LANE] - found) * LN2
     loss_ref[ALL] = jnp.broadcast_to(loss, loss_ref.shape) * inv_ref[0:1, :]
 
 
 def lookup_kernel(top, sc, look, from_ref, g1, g2, g3, g4, all_ref, *rest):
-    out_ref, id_ref = rest[-2:]
+    out_ref, id_ref, row_ref = rest[-3:]
     b = pl.program_id(0)
-    nc = all_ref.shape[2] // CH
+    seq = all_ref.shape[2]
+    lists = (g1, g2, g3, g4)
 
     @pl.when(b == 0)
     def _():
-        for q in range(4):
+        for q, g in enumerate(lists):
             who = sc[2, 1] if q == 0 else xor(sc[2, 1], q)
-            for j in range(nc):
-                id_ref[q, j] = columns(all_ref[who, 2:3, CH * j:CH * j + CH])
-
-    at = top(sc, b)
-    out_ref[ALL] = from_ref[ALL]
-    cols = lax.broadcasted_iota(jnp.int32, (CH, LB), 1) + (at * LB + sc[2, 5])
-
-    def step(k, _):
+            for j in range(seq // LANE):
+                id_ref[q, LANE * j:LANE * j + LANE, :] = columns(all_ref[who, 2:3, LANE * j:LANE * j + LANE]) - sc[2, 5]
+            row_ref[q, 0:seq, :] = g[ALL].astype(BF16).T
+            id_ref[q, seq:, :] = jnp.full((CH, LANE), -MIB, jnp.int32)
+            row_ref[q, seq:, :] = jnp.zeros((CH, row_ref.shape[2]), BF16)
+
+    lane = lax.broadcasted_iota(jnp.int32, (CH, LB), 1)
+    subs = from_ref.shape[1] // LB
+
+    def part(at, k):
         hots, rows = [], []
-        for q, g in enumerate((g1, g2, g3, g4)):
-            c = look[q, at] + k
-            ok = c < nc
-            c = jnp.minimum(c, nc - 1)
-            ids = jnp.concatenate([id_ref[q, c]] * (LB // LANE), axis=1)
-            hots.append(jnp.where(ids == jnp.where(ok, cols, -1), 1.0, 0.0).astype(BF16))
-            rows.append(g[:, pl.ds(pl.multiple_of(c * CH, CH), CH)].astype(BF16))
-        out_ref[ALL] += jnp.dot(jnp.concatenate(rows, axis=1), jnp.concatenate(hots, axis=0), preferred_element_type=F32)
-        return 0
-
-    lax.fori_loop(0, look[4, at], step, 0)
+        for q in range(len(lists)):
+            c = pl.ds(pl.multiple_of(jnp.minimum(look[q, at] + k * CH, seq), ST), CH)
+            ids = jnp.concatenate([id_ref[q, c, :] - at * LB] * (LB // LANE), axis=1)
+            hots.append(jnp.where(ids == lane, 1.0, 0.0).astype(BF16))
+            rows.append(row_ref[q, c, :])
+        return lax.dot_general(
+            jnp.concatenate(rows, axis=0), jnp.concatenate(hots, axis=0), (((0,), (0,)), ((), ())), preferred_element_type=F32)
+
+    for u in range(subs):
+        q = slice(u * LB, (u + 1) * LB)
+        out_ref[:, q] = from_ref[:, q] + part(top(sc, b) * subs + u, 0)
+    for u in range(subs):
+        at = top(sc, b) * subs + u
+        q = slice(u * LB, (u + 1) * LB)
+
+        def step(k, _, at=at, q=q):
+            out_ref[:, q] += part(at, k)
+            return 0
+
+        lax.fori_loop(1, look[4, at], step, 0)
 
 
 def solution(mesh):
@@ -441,11 +484,11 @@
 
     shape = jax.ShapeDtypeStruct
 
-    def single(kernel, args, outs, scratch, mib, ident=None):
+    def single(kernel, args, outs, scratch, ident=None):
         talk = {} if ident is None else dict(collective_id=ident, has_side_effects=True)
         return pl.pallas_call(
             kernel, grid=(1,), in_specs=blocks(*args), out_specs=blocks(*outs), out_shape=outs, scratch_shapes=scratch,
-            compiler_params=pltpu.CompilerParams(dimension_semantics=("arbitrary",), vmem_limit_bytes=mib * MIB, **talk),
+            compiler_params=pltpu.CompilerParams(dimension_semantics=("arbitrary",), vmem_limit_bytes=GRANT, **talk),
             cost_estimate=cost(SMALL))(*args)
 
     dma = pltpu.SemaphoreType.DMA
@@ -459,53 +502,46 @@
         nt = 2 * seq // TB
         et = embed.T
         ht = hidden[0].T
-        gain = jnp.broadcast_to(norm_w.astype(F32)[:, None], (d, LANE))
-
-        *give, meta = single(
-            sort_kernel, (targets, loss_mask, token_ids, grad_embed[0].T),
-            [shape((cols, seq), F32)] * 4 + [shape((8, seq), jnp.int32)],
-            [pltpu.VMEM((seq, LANE), jnp.int32), pltpu.VMEM((seq, seq), BF16), pltpu.VMEM((d, seq), F32)], 48)
-
-        zt32, zt_chip, z_chip, metas, table, inv_n = single(
-            functools.partial(prep_kernel, vocab_local), (ht, gain, meta),
+
+        zt32, zt_chip, z_chip, metas, table, inv_n, *give = single(
+            functools.partial(prep_kernel, vocab_local),
+            (ht, norm_w, targets, loss_mask, token_ids, grad_embed[0].T),
             [shape((d, seq), F32), shape((d, 2 * seq), BF16), shape((2 * seq, d), BF16),
-             shape((n_dp, 8, seq), jnp.int32), shape((8, LANE), jnp.int32), shape((8, LANE), F32)],
-            [pltpu.VMEM((d, seq), F32), pltpu.VMEM((3, 8, seq), jnp.int32), dma((4,)), dma((4,))], 56, 0)
+             shape((n_dp, 8, seq), jnp.int32), shape((8, LANE), jnp.int32), shape((8, LANE), F32)] + [shape((cols, seq), F32)] * 4,
+            [pltpu.VMEM((8, seq), jnp.int32), pltpu.VMEM((8, seq), jnp.int32),
+             pltpu.VMEM((seq, LANE), jnp.int32), pltpu.VMEM((seq, seq), BF16), pltpu.VMEM((d, seq), F32),
+             pltpu.VMEM((d, seq), F32), pltpu.VMEM((3, 8, seq), jnp.int32), pltpu.VMEM((3, 8, seq), jnp.int32),
+             dma((7,)), dma((7,))], 0)
 
         far = lax.ppermute(zt32, "dp", swap[2])
         far_near = lax.ppermute(far, "dp", swap[1])
 
-        def arrange(a, b):
-            w = 512
-            n = seq // w
-            place = lambda j, i, x: lax.bitwise_xor(j, x[2, 0]) * n + i
+        def swap_call(own, give, a, b):
+            w = 2 * seq // 8
             return pl.pallas_call(
-                arrange_kernel,
-                grid_spec=pltpu.PrefetchScalarGridSpec(
-                    num_scalar_prefetch=1, grid=(2, n),
-                    in_specs=[
-                        pl.BlockSpec((d, w), lambda j, i, x: (0, jnp.where(j == 0, i, n - 1))),
-                        pl.BlockSpec((d, w), lambda j, i, x: (0, jnp.where(j == 1, i, 0)))],
-                    out_specs=[
-                        pl.BlockSpec((d, w), lambda j, i, x: (0, place(j, i, x))),
-                        pl.BlockSpec((w, d), lambda j, i, x: (place(j, i, x), 0))]),
-                out_shape=[shape((d, 2 * seq), BF16), shape((2 * seq, d), BF16)],
-                compiler_params=params(40), name="arrange",
-                cost_estimate=cost(SMALL),
-            )(table, a, b)
+                swap_kernel, grid=(8,),
+                in_specs=[pl.BlockSpec((d, seq), lambda i: (0, 0)), pl.BlockSpec(memory_space=pl.ANY),
+                          pl.BlockSpec((d, w), lambda i: (0, jnp.minimum(i, 3))), pl.BlockSpec((d, w), lambda i: (0, jnp.maximum(i - 4, 0)))],
+                out_specs=[pl.BlockSpec((d, w), lambda i: (0, i)), pl.BlockSpec((w, d), lambda i: (i, 0)), pl.BlockSpec((d, seq), lambda i: (0, 0))],
+                out_shape=[shape((d, 2 * seq), BF16), shape((2 * seq, d), BF16), shape((d, seq), F32)],
+                scratch_shapes=[pltpu.VMEM((d, seq), F32), dma((1,)), dma((1,))],
+                compiler_params=pltpu.CompilerParams(
+                    dimension_semantics=("arbitrary",), vmem_limit_bytes=GRANT, collective_id=3, has_side_effects=True),
+                name="swap", cost_estimate=cost(SMALL))(own, give, a, b)
 
         def specs(r):
+            at = lambda x, t: lax.bitwise_xor(x[r, t], x[2, 0] * (nt // 2)) if r else x[r, t]
             full = lambda v, t, x: (0, 0)
             return dict(
                 e=pl.BlockSpec((d, VB), lambda v, t, x: (0, x[2, 0] * nv + v)),
-                z=pl.BlockSpec((TB, d), lambda v, t, x: (x[r, t], 0)),
+                z=pl.BlockSpec((TB, d), lambda v, t, x: (at(x, t), 0)),
                 l=pl.BlockSpec((1, 1, TB, VB), lambda v, t, x: (x[r, t], v, 0, 0)),
                 vec=pl.BlockSpec((2 * seq, LANE), full),
                 row=pl.BlockSpec((2 * seq // LANE, LANE), full),
                 any=pl.BlockSpec(memory_space=pl.ANY),
                 inv=pl.BlockSpec((8, LANE), full),
-                za=pl.BlockSpec((cols, TB), lambda v, t, x: (x[2, 1], x[r, t])),
-                zb=pl.BlockSpec((cols, TB), lambda v, t, x: (x[2, 2], x[r, t])),
+                za=pl.BlockSpec((cols, TB), lambda v, t, x: (x[2, 1], at(x, t))),
+                zb=pl.BlockSpec((cols, TB), lambda v, t, x: (x[2, 2], at(x, t))),
                 de=pl.BlockSpec((cols, VB), lambda v, t, x: (0, v)))
 
         pick = lambda sp, *names: [sp[k] for k in names]
@@ -520,7 +556,7 @@
             grid_spec=pltpu.PrefetchScalarGridSpec(
                 num_scalar_prefetch=1, grid=(nv, nt), in_specs=pick(own, "z", "e"), out_specs=pick(own, "l", "vec", "vec")),
             out_shape=[shape((nt, nv, TB, VB), F32), vec, vec],
-            compiler_params=params(56), name="logits",
+            compiler_params=params(), name="logits",
             cost_estimate=cost(flops),
         )(table, z_chip, et)
 
@@ -529,7 +565,7 @@
             functools.partial(stats_kernel, vocab_local), (m_own, s_own, metas),
             [shape((rows, LANE), F32), shape((rows, LANE), jnp.int32), shape((rows, LANE), jnp.int32),
              shape((8, LANE), F32), shape((8, LANE), jnp.int32)],
-            [pltpu.VMEM((2 * rows, LANE), F32), pltpu.VMEM((3, 2 * rows, LANE), F32), dma((3,)), dma((3,))], 32, 1)
+            [pltpu.VMEM((2 * rows, LANE), F32), pltpu.VMEM((3, 2 * rows, LANE), F32), dma((3,)), dma((3,))], 1)
         k_far = lax.ppermute(k_own, "dp", swap[2])
 
         lists = [give[0]]
@@ -543,15 +579,13 @@
                 in_specs=pick(own, "l", "e", "za", "zb", "row", "row", "inv"), out_specs=pick(own, "any", "any", "de", "de", "vec"),
                 scratch_shapes=[pltpu.VMEM((TB, VB), BF16), *wide, pltpu.VMEM((2, d, seq), F32), dma((2,))]),
             out_shape=[shape((d, seq), F32), shape((d, seq), F32), de_shape, de_shape, vec],
-            compiler_params=params(60), name="own",
+            compiler_params=params(), name="own",
             cost_estimate=cost(flops + flops // 2),
         )(table, l_own, et, zt_chip, zt_chip, k_own, t_own, inv_n)
 
-        dz_near = lax.ppermute(dz_give, "dp", swap[1])
-        dz_half = dz_own + dz_near
+        zt_far, z_far, dz_half = swap_call(dz_own, dz_give, far, far_near)
         dz_tp = lax.ppermute(dz_half, "tp", [(0, 1), (1, 0)])
 
-        zt_far, z_far = arrange(far, far_near)
         da, db = pl.pallas_call(
             other_kernel,
             grid_spec=pltpu.PrefetchScalarGridSpec(
@@ -559,12 +593,12 @@
                 in_specs=pick(other, "z", "e", "za", "zb", "row", "row", "inv", "de", "de"), out_specs=pick(other, "de", "de"),
                 scratch_shapes=[pltpu.VMEM((TB, VB), F32), pltpu.VMEM((TB, VB), BF16), *wide]),
             out_shape=[de_shape, de_shape],
-            compiler_params=params(60), name="other",
+            compiler_params=params(), name="other",
             cost_estimate=cost(flops + flops // 2),
         )(table, z_far, et, zt_far, zt_far, k_far, t_far, inv_n, da, db)
         got = lax.ppermute(db, "dp", swap[1])
 
-        nb = half // LB
+        nb = half // LW
 
         def lookup(top, source, *prior):
             zero = lambda b, x, k: (0, 0)
@@ -572,25 +606,25 @@
                 functools.partial(lookup_kernel, top),
                 grid_spec=pltpu.PrefetchScalarGridSpec(
                     num_scalar_prefetch=2, grid=(nb,),
-                    in_specs=[pl.BlockSpec((cols, LB), lambda b, x, k: (0, b))] + [pl.BlockSpec((cols, seq), zero)] * 4
+                    in_specs=[pl.BlockSpec((cols, LW), lambda b, x, k: (0, b))] + [pl.BlockSpec((cols, seq), zero)] * 4
                     + [pl.BlockSpec((n_dp, 8, seq), lambda b, x, k: (0, 0, 0))] + [pl.BlockSpec(memory_space=pl.ANY)] * len(prior),
-                    out_specs=pl.BlockSpec((cols, LB), lambda b, x, k: (0, top(x, b))),
-                    scratch_shapes=[pltpu.VMEM((4, seq // CH, CH, LANE), jnp.int32)]),
+                    out_specs=pl.BlockSpec((cols, LW), lambda b, x, k: (0, top(x, b))),
+                    scratch_shapes=[pltpu.VMEM((4, seq + CH, LANE), jnp.int32), pltpu.VMEM((4, seq + CH, cols), BF16)]),
                 out_shape=shape((cols, vocab_local), F32),
                 input_output_aliases={8: 0} if prior else {},
-                compiler_params=params(40, 1), name="lookup",
+                compiler_params=params(1), name="lookup",
                 cost_estimate=cost(flops // 8),
             )(table, look, source, *lists, metas, *prior)
 
         de_t = lookup(lambda x, b: x[2, 0] * nb + b, da)
 
         dht, dg, loss = single(
-            final_kernel, (dz_half, dz_tp, ht, gain, loss_mask, tl, lse_sum, inv_n),
-            [shape((d, seq), BF16), shape((1, d), F32), shape((1, LANE), F32)],
-            [pltpu.VMEM((8, 640), F32), pltpu.VMEM((8, 8, 640), F32), dma((7,)), dma((7,))], 56, 2)
+            final_kernel, (dz_half, dz_tp, ht, norm_w, loss_mask, tl, lse_sum, inv_n),
+            [shape((d, seq), BF16), shape((d,), F32), shape((1, LANE), F32)],
+            [pltpu.VMEM((8, 640), F32), pltpu.VMEM((8, 8, 640), F32), dma((7,)), dma((7,))], 2)
 
         de_t = lookup(lambda x, b: (1 - x[2, 0]) * nb + b, got, de_t)
-        return loss[0, 0], dht.T[None], dg[0], de_t.T
+        return loss[0, 0], dht.T[None], dg, de_t.T
 
     return jax.shard_map(
         local_step, mesh=mesh,

time: 297 us -> 253 us (0.85)
  waiting for transfers between devices: 70.8 us -> 46.2 us
  local copies, waits for them, and re-layouts: 19.4 us -> 3.02 us
    ppermute x1, waiting for transfers between devices: 50.2 us -> 10.7 us  [local_step(): dz_tp = lax.ppermute(dz_half, 'tp', [(0, 1), (1, 0)])]
    ppermute x3, waiting for transfers between devices: 0.01 us -> 26.1 us  [local_step(): lists.append(lax.ppermute(give[k], 'dp', swap[k]))]
    unnamed x45 -> x20, local copies, waits for them, and re-layouts: 17.9 us -> 3.02 us
    ppermute x1 -> x0, waiting for transfers between devices: 14.5 us -> none  [local_step(): dz_near = lax.ppermute(dz_give, 'dp', swap[1])]
    pallas_call x1, Pallas kernels: 4.21 us -> 9.99 us  [swap_call(): pl.pallas_call(swap_kernel, grid=(8,), in_specs=[pl.BlockSpec((d, seq), l...]
    ppermute x1, waiting for transfers between devices: 6.15 us -> 9.33 us  [local_step(): far = lax.ppermute(zt32, 'dp', swap[2])]
    pallas_call x4 -> x3, Pallas kernels: 32.5 us -> 32.2 us  [single(): pl.pallas_call(kernel, grid=(1,), in_specs=blocks(*args), out_specs=block...]
  transfers between devices with their start and end apart: 9 -> 8, of which waited for: 3 -> 5; matrix products, arithmetic and copies ran while one was open for 1% -> 0% of each run, Pallas kernels for 40% -> 48%
where the time goes in v3:
time: 253 us; the launch traced here: 252 us
  Pallas kernels  195 us (77%)
  waiting for transfers between devices  46.2 us (18%)
  starting transfers between devices  5.53 us (2%)
  local copies, waits for them, and re-layouts  3.02 us (1%)
    pallas_call x1, Pallas kernels, local_step(): pl.pallas_call(other_kernel, grid_spec=pltpu.PrefetchScalarGridSpec(num_s...  47 us
    pallas_call x1, Pallas kernels, local_step(): pl.pallas_call(own_kernel, grid_spec=pltpu.PrefetchScalarGridSpec(num_sca...  46.2 us
    pallas_call x1, Pallas kernels, local_step(): pl.pallas_call(logits_kernel, grid_spec=pltpu.PrefetchScalarGridSpec(num_...  35.6 us
    pallas_call x3, Pallas kernels, single(): pl.pallas_call(kernel, grid=(1,), in_specs=blocks(*args), out_specs=block...  32.2 us
    ppermute x3, waiting for transfers between devices, local_step(): lists.append(lax.ppermute(give[k], 'dp', swap[k]))  26.1 us
    pallas_call x2, Pallas kernels, lookup(): pl.pallas_call(functools.partial(lookup_kernel, top), grid_spec=pltpu.Pre...  24.3 us
    ppermute x1, waiting for transfers between devices, local_step(): dz_tp = lax.ppermute(dz_half, 'tp', [(0, 1), (1, 0)])  10.7 us
    pallas_call x1, Pallas kernels, swap_call(): pl.pallas_call(swap_kernel, grid=(8,), in_specs=[pl.BlockSpec((d, seq), l...  9.99 us
  transfers between devices with their start and end apart: 8, of which 5 were waited for; matrix products, arithmetic and copies ran while one was open for 0% of the time, Pallas kernels for 48%

profile of v3, /device:TPU:0, one launch (start us, length us, event | category | flops | bytes accessed | tf_op | source)
XLA Modules:
  0.0 252.0 jit_solution(12335880972640919526)
XLA Ops:
  0.6 14.9 %shard_map.102 = (f32[576,1024]{1,0:T(8,128)}, bf16[576,2048]{1,0:T(8,128)(2,1)}, bf16[2048,576]{1,0:T(8,128)(2,1)}, s32[4,8,1024]{2,1,0:T(8,128)}, s32[8,128]{1...) custom-call(bf16[576,1024]{1,0:T(8,128)(2,1)} %bitcast.14, ...), custom_call_target="tpu_custom_call" | custom-call | flops 268435456 | bytes 1048576 | tf_op jit(solution)/shard_map/pallas_call | solution.py:489
  15.5 1.5 collective-permute-start
  17.0 35.6 %logits.1 = (f32[8,2,256,6144]{3,2,1,0:T(8,128)}, f32[2048,128]{1,0:T(8,128)}, f32[2048,128]{1,0:T(8,128)}) custom-call(s32[8,128]{1,0:T(8,128)} %get-tuple-element.35.sc, bf16[2048,576]{1,0:T(8,128)(2,1)} %get-tuple-element.36.z_ref, bf16[576,24576]{1,0:T(8,128)(2,1)} %bitcast.18), custom_call_target="tpu_custom_call" | custom-call | flops 28991029248 | bytes 1048576 | tf_op jit(solution)/shard_map/logits/pallas_call | solution.py:554
  52.6 6.6 %shard_map.103 = (f32[16,128]{1,0:T(8,128)}, s32[16,128]{1,0:T(8,128)}, s32[16,128]{1,0:T(8,128)}, f32[8,128]{1,0:T(8,128)}, s32[8,128]{1,0:T(8,128)}) custom-call(f32[2048,128]{1,0:T(8,128)} %get-tuple-element.39.m_ref, f32[2048,128]{1,0:T(8,128)} %get-tuple-element.40.s_ref, s32[4,8,1024]{2,1,0:T(8,128)} %get-tuple-element.41.all_ref), custom_call_target="tpu_custom_call" | custom-call | flops 268435456 | bytes 1048576 | tf_op jit(solution)/shard_map/pallas_call | solution.py:489
  59.2 0.6 collective-permute-start.3
  59.8 9.3 %collective-permute-done.a_ref = f32[576,1024]{1,0:T(8,128)S(1)} collective-permute-done((f32[576,1024]{1,0:T(8,128)}, f32[576,1024]{1,0:T(8,128)S(1)}, u32[]{:S(2)}, u32[]{:S(2)}) %collective-permute-start) | collective-permute-done | bytes 2359328 | tf_op jit(solution)/shard_map/ppermute | solution.py:516
  69.1 46.2 %own.1 = (f32[576,1024]{1,0:T(8,128)}, f32[576,1024]{1,0:T(8,128)}, f32[144,12288]{1,0:T(8,128)}, f32[144,12288]{1,0:T(8,128)}, f32[2048,128]{1,0:T(8,128)}) custom-call(s32[8,128]{1,0:T(8,128)} %get-tuple-element.35.sc, f32[8,2,256,6144]{3,2,1,0:T(8,128)} %get-tuple-element.37.l_ref, bf16[576,24576]{1,0:T(8,128)(2,1)} %bitcast.19, ...), custom_call_target="tpu_custom_call" | custom-call | flops 43486543872 | bytes 1048576 | tf_op jit(solution)/shard_map/own/pallas_call | solution.py:575
  115.4 10.0 %swap.1 = (bf16[576,2048]{1,0:T(8,128)(2,1)}, bf16[2048,576]{1,0:T(8,128)(2,1)}, f32[576,1024]{1,0:T(8,128)}) custom-call(f32[576,1024]{1,0:T(8,128)} %get-tuple-element.45.own_ref, f32[576,1024]{1,0:T(8,128)} %get-tuple-element.46.give_ref, f32[576,1024]{1,0:T(8,128)} %copy-done.1, f32[576,1024]{1,0:T(8,128)} %collective-permute-done.1.b_ref), custom_call_target="tpu_custom_call" | custom-call | flops 268435456 | bytes 1048576 | tf_op jit(solution)/shard_map/swap/pallas_call | solution.py:521
  125.4 0.6 copy-done.7
  126.0 47.0 %other.1 = (f32[144,12288]{1,0:T(8,128)}, f32[144,12288]{1,0:T(8,128)}) custom-call(s32[8,128]{1,0:T(8,128)} %get-tuple-element.35.sc, bf16[2048,576]{1,0:T(8,128)(2,1)} %get-tuple-element.55.z_ref, bf16[576,24576]{1,0:T(8,128)(2,1)} %bitcast.20, bf16[576,2048]{1,0:T(8,128)(2,1)} %get-tuple-element.56.za_ref.zb_ref, ...), custom_call_target="tpu_custom_call" | custom-call | flops 43486543872 | bytes 1048576 | tf_op jit(solution)/shard_map/other/pallas_call | solution.py:589
  173.0 1.6 collective-permute-start.2
  174.6 0.2 collective-permute-start.5
  174.8 1.5 collective-permute-start.6
  176.3 0.1 collective-permute-start.7
  176.5 8.9 %collective-permute-done.5.g2 = f32[144,1024]{1,0:T(8,128)S(1)} collective-permute-done((f32[144,1024]{1,0:T(8,128)}, f32[144,1024]{1,0:T(8,128)S(1)}, u32[]{:S(2)}, u32[]{:S(2)}) %collective-permute-start.5) | collective-permute-done | bytes 589856 | tf_op jit(solution)/shard_map/ppermute | solution.py:573
  185.3 5.9 %collective-permute-done.6.g3 = f32[144,1024]{1,0:T(8,128)S(1)} collective-permute-done((f32[144,1024]{1,0:T(8,128)}, f32[144,1024]{1,0:T(8,128)S(1)}, u32[]{:S(2)}, u32[]{:S(2)}) %collective-permute-start.6) | collective-permute-done | bytes 589856 | tf_op jit(solution)/shard_map/ppermute | solution.py:573
  191.2 11.3 %collective-permute-done.7.g4 = f32[144,1024]{1,0:T(8,128)S(1)} collective-permute-done((f32[144,1024]{1,0:T(8,128)}, f32[144,1024]{1,0:T(8,128)S(1)}, u32[]{:S(2)}, u32[]{:S(2)}) %collective-permute-start.7) | collective-permute-done | bytes 589856 | tf_op jit(solution)/shard_map/ppermute | solution.py:573
  202.5 0.8 copy-done.4
  203.3 12.7 %lookup.2.rest_0_ = f32[144,24576]{1,0:T(8,128)} custom-call(s32[8,128]{1,0:T(8,128)} %get-tuple-element.35.sc, s32[8,128]{1,0:T(8,128)} %get-tuple-element.54.look, f32[144,12288]{1,0:T(8,128)} %get-tuple-element.65.from_ref, f32[144,1024]{1,0:T(8,128)} %get-tuple-element.61.g1, f32[144,1024]{1,0:T(8,128)} %copy-done.2, f32[144,1024]{1,0:T(8,128)} %copy-done.3, ...), custom_call_target="tpu_custom_call" | custom-call | flops 3623878656 | bytes 1048576 | tf_op jit(solution)/shard_map/lookup/pallas_call | solution.py:605
  216.0 10.7 %collective-permute-done.2.b_ref = f32[576,1024]{1,0:T(8,128)} collective-permute-done((f32[576,1024]{1,0:T(8,128)S(1)}, f32[576,1024]{1,0:T(8,128)}, u32[]{:S(2)}, u32[]{:S(2)}) %collective-permute-start.2) | collective-permute-done | bytes 2359328 | tf_op jit(solution)/shard_map/ppermute | solution.py:587
  226.8 10.7 %shard_map.104 = (bf16[576,1024]{1,0:T(8,128)(2,1)}, f32[576]{0:T(1024)}, f32[1,128]{1,0:T(1,128)}) custom-call(f32[576,1024]{1,0:T(8,128)} %get-tuple-element.48.a_ref, f32[576,1024]{1,0:T(8,128)} %collective-permute-done.2.b_ref, bf16[576,1024]{1,0:T(8,128)(2,1)} %bitcast.15, bf16[576]{0:T(1024)(128)(2,1)} %g_ref.3, s32[1,1024]{1,0:T(1,128)} %on_ref.1, ...), custom_call_target="tpu_custom_call" | custom-call | flops 268435456 | bytes 1048576 | tf_op jit(solution)/shard_map/pallas_call | solution.py:489
  237.5 11.7 %lookup.3 = f32[144,24576]{1,0:T(8,128)} custom-call(s32[8,128]{1,0:T(8,128)} %get-tuple-element.35.sc, s32[8,128]{1,0:T(8,128)} %get-tuple-element.54.look, f32[144,12288]{1,0:T(8,128)} %collective-permute-done.4.from_ref, f32[144,1024]{1,0:T(8,128)} %get-tuple-element.61.g1, f32[144,1024]{1,0:T(8,128)} %copy-done.2, ...), custom_call_target="tpu_custom_call", output_to_operand_aliasing={{}: (8, {})} | custom-call | flops 3623878656 | bytes 1048576 | tf_op jit(solution)/shard_map/lookup/pallas_call | solution.py:605
  249.2 1.0 copy.17
  250.2 0.6 copy.18
  (21 shorter events, 0.1 us)
Async XLA Ops:
  15.5 53.6 %collective-permute-start = (f32[576,1024]{1,0:T(8,128)}, f32[576,1024]{1,0:T(8,128)S(1)}, u32[]{:S(2)}, u32[]{:S(2)}) collective-permute-start(f32[576,1024]{1,0:T(8,128)} %get-tuple-element.47), channel_id=1, source_target_pairs={{0,2},{1,3},{2,0},{3,1},{4,6},{5,7},{6,4},{7,5}} | collective-permute-start | bytes 7077896 | tf_op jit(solution)/shard_map/ppermute | solution.py:516
  59.2 66.2 %collective-permute-start.3 = (f32[16,128]{1,0:T(8,128)}, f32[16,128]{1,0:T(8,128)S(1)}, u32[]{:S(2)}, u32[]{:S(2)}) collective-permute-start(f32[16,128]{1,0:T(8,128)} %get-tuple-element.42.k_ref), channel_id=1, source_target_pairs={{0,2},{1,3},{2,0},{3,1},{4,6},{5,7},{6,4},{7,5}} | collective-permute-start | bytes 24584 | tf_op jit(solution)/shard_map/ppermute | solution.py:569
  69.1 46.2 %copy-start.1 = (f32[576,1024]{1,0:T(8,128)}, f32[576,1024]{1,0:T(8,128)S(1)}, u32[]{:S(2)}) copy-start(f32[576,1024]{1,0:T(8,128)S(1)} %collective-permute-done.a_ref) | copy-start | bytes 7077892
  69.1 46.3 %collective-permute-start.1 = (f32[576,1024]{1,0:T(8,128)S(1)}, f32[576,1024]{1,0:T(8,128)}, u32[]{:S(2)}, u32[]{:S(2)}) collective-permute-start(f32[576,1024]{1,0:T(8,128)S(1)} %collective-permute-done.a_ref), channel_id=1, source_target_pairs={{0,1},{1,0},{2,3},{3,2},{4,5},{5,4},{6,7},{7,6}} | collective-permute-start | bytes 7077896 | tf_op jit(solution)/shard_map/ppermute | solution.py:517
  125.4 0.6 copy-start.7
  126.0 47.0 %copy-start = (f32[576,1024]{1,0:T(8,128)S(1)}, f32[576,1024]{1,0:T(8,128)}, u32[]{:S(2)}) copy-start(f32[576,1024]{1,0:T(8,128)} %get-tuple-element.48.a_ref) | copy-start | bytes 7077892
  173.0 64.5 %collective-permute-start.4 = (f32[144,12288]{1,0:T(8,128)}, f32[144,12288]{1,0:T(8,128)}, u32[]{:S(2)}, u32[]{:S(2)}) collective-permute-start(f32[144,12288]{1,0:T(8,128)} %get-tuple-element.60), channel_id=1, source_target_pairs={{0,1},{1,0},{2,3},{3,2},{4,5},{5,4},{6,7},{7,6}} | collective-permute-start | bytes 21233672 | tf_op jit(solution)/shard_map/ppermute | solution.py:599
  173.0 53.8 %collective-permute-start.2 = (f32[576,1024]{1,0:T(8,128)S(1)}, f32[576,1024]{1,0:T(8,128)}, u32[]{:S(2)}, u32[]{:S(2)}) collective-permute-start(f32[576,1024]{1,0:T(8,128)S(1)} %copy-done), channel_id=1, source_target_pairs={{0,4},{4,0},{1,5},{5,1},{2,6},{6,2},{3,7},{7,3}} | collective-permute-start | bytes 7077896 | tf_op jit(solution)/shard_map/ppermute | solution.py:587
  174.6 10.7 %collective-permute-start.5 = (f32[144,1024]{1,0:T(8,128)}, f32[144,1024]{1,0:T(8,128)S(1)}, u32[]{:S(2)}, u32[]{:S(2)}) collective-permute-start(f32[144,1024]{1,0:T(8,128)} %get-tuple-element.62), channel_id=1, source_target_pairs={{0,1},{1,0},{2,3},{3,2},{4,5},{5,4},{6,7},{7,6}} | collective-permute-start | bytes 1769480 | tf_op jit(solution)/shard_map/ppermute | solution.py:573
  174.8 16.4 %collective-permute-start.6 = (f32[144,1024]{1,0:T(8,128)}, f32[144,1024]{1,0:T(8,128)S(1)}, u32[]{:S(2)}, u32[]{:S(2)}) collective-permute-start(f32[144,1024]{1,0:T(8,128)} %get-tuple-element.63), channel_id=1, source_target_pairs={{0,2},{1,3},{2,0},{3,1},{4,6},{5,7},{6,4},{7,5}} | collective-permute-start | bytes 1769480 | tf_op jit(solution)/shard_map/ppermute | solution.py:573
  176.3 26.2 %collective-permute-start.7 = (f32[144,1024]{1,0:T(8,128)}, f32[144,1024]{1,0:T(8,128)S(1)}, u32[]{:S(2)}, u32[]{:S(2)}) collective-permute-start(f32[144,1024]{1,0:T(8,128)} %get-tuple-element.64), channel_id=1, source_target_pairs={{0,3},{1,2},{2,1},{3,0},{4,7},{5,6},{6,5},{7,4}} | collective-permute-start | bytes 1769480 | tf_op jit(solution)/shard_map/ppermute | solution.py:573
  185.3 17.2 %copy-start.2 = (f32[144,1024]{1,0:T(8,128)}, f32[144,1024]{1,0:T(8,128)S(1)}, u32[]{:S(2)}) copy-start(f32[144,1024]{1,0:T(8,128)S(1)} %collective-permute-done.5.g2) | copy-start | bytes 1769476
  191.2 11.3 %copy-start.3 = (f32[144,1024]{1,0:T(8,128)}, f32[144,1024]{1,0:T(8,128)S(1)}, u32[]{:S(2)}) copy-start(f32[144,1024]{1,0:T(8,128)S(1)} %collective-permute-done.6.g3) | copy-start | bytes 1769476
  202.5 0.8 copy-start.4
  237.5 11.7 %copy-start.8 = (f32[1,128]{1,0:T(1,128)S(1)}, f32[1,128]{1,0:T(1,128)}, u32[]{:S(2)}) copy-start(f32[1,128]{1,0:T(1,128)} %get-tuple-element.51) | copy-start | bytes 1540
  237.5 11.7 %copy-start.5 = (bf16[576,1024]{1,0:T(8,128)(2,1)S(1)}, bf16[576,1024]{1,0:T(8,128)(2,1)}, u32[]{:S(2)}) copy-start(bf16[576,1024]{1,0:T(8,128)(2,1)} %get-tuple-element.52) | copy-start | bytes 3538948
  249.2 1.1 copy-start.6

commit v4 on v3

--- a/solution.py
+++ b/solution.py
@@ -15,7 +15,7 @@
 VB = 6144
 SC = 512
 SF = 1024
-LW = 2048
+LW = 6144
 LB = 1024
 CH = 128
 ST = 16
@@ -48,9 +48,10 @@
     return pltpu.CompilerParams(dimension_semantics=("arbitrary",) * n, vmem_limit_bytes=GRANT)
 
 
-def stats_stage(l_ref, m_ref, s_ref, row, c):
+def stats_stage(l_ref, m_ref, s_ref, bases, c):
     for r in range(TB // 8):
-        rows = pl.ds(row + 8 * r, 8)
+        h, o = divmod(8 * r, LANE)
+        rows = pl.ds(bases[h] + o, 8)
         old = m_ref[rows, :]
         total = s_ref[rows, :]
         parts = [l_ref[0, 0, 8 * r:8 * r + 8, c * SC + LANE * j:c * SC + LANE * j + LANE] for j in range(SC // LANE)]
@@ -62,30 +63,38 @@
         s_ref[rows, :] = total
 
 
-def logits_kernel(sc, z_ref, e_ref, l_ref, m_ref, s_ref):
+def spots(sc, i):
+    t = pl.program_id(1)
+    return [pl.multiple_of(sc[i + h, t] * LANE, LANE) for h in range(TB // LANE)]
+
+
+def logits_kernel(sc, z0, z1, e_ref, l_ref, m_ref, s_ref):
     v, t = pl.program_id(0), pl.program_id(1)
-    row = pl.multiple_of(sc[0, t] * TB, TB)
-    skip = sc[2, 3]
+    bases = spots(sc, 0)
+    skip = sc[4, 3]
 
     @pl.when((v == 0) & (t >= skip))
     def _():
-        m_ref[pl.ds(row, TB), :] = jnp.full((TB, LANE), -3e38, F32)
-        s_ref[pl.ds(row, TB), :] = jnp.zeros((TB, LANE), F32)
+        for base in bases:
+            m_ref[pl.ds(base, LANE), :] = jnp.full((LANE, LANE), -3e38, F32)
+            s_ref[pl.ds(base, LANE), :] = jnp.zeros((LANE, LANE), F32)
 
     @pl.when(t >= skip)
     def _():
+        z = jnp.concatenate([z0[ALL], z1[ALL]], axis=0)
         n = VB // SC
         for c in range(n + 1):
             if c < n:
                 q = slice(c * SC, (c + 1) * SC)
-                l_ref[0, 0, :, q] = jnp.dot(z_ref[ALL], e_ref[:, q], preferred_element_type=F32) * LOG2E
+                l_ref[0, 0, :, q] = jnp.dot(z, e_ref[:, q], preferred_element_type=F32) * LOG2E
             if c > 0:
-                stats_stage(l_ref, m_ref, s_ref, row, c - 1)
-
-
-def dlogits_stage(get, dl_ref, k_ref, scale, t_ref, tl_ref, row, base, c, width):
+                stats_stage(l_ref, m_ref, s_ref, bases, c - 1)
+
+
+def dlogits_stage(get, dl_ref, k_ref, scale, t_ref, tl_ref, bases, base, c, width):
     for r in range(TB // 16):
-        rows = pl.ds(row + 16 * r, 16)
+        h, o = divmod(16 * r, LANE)
+        rows = pl.ds(bases[h] + o, 16)
         shift = k_ref[rows, :]
         target = t_ref[rows, :] - base
         if tl_ref is not None:
@@ -102,19 +111,24 @@
             tl_ref[rows, :] = found
 
 
-def own_kernel(sc, l_ref, e_ref, za_ref, zb_ref, k_ref, t_ref, inv_ref, dz_ref, gv_ref, da_ref, db_ref, tl_ref, dl_ref, kw_ref, tw_ref, acc_ref, sem):
+def pair_columns(a, b, c, d):
+    return jnp.concatenate([jnp.concatenate([a[ALL], b[ALL]], axis=1), jnp.concatenate([c[ALL], d[ALL]], axis=1)], axis=0)
+
+
+def own_kernel(sc, l_ref, e_ref, za0, za1, zb0, zb1, k_ref, t_ref, inv_ref, dz_ref, gv_ref, da_ref, db_ref, tl_ref, dl_ref, kw_ref, tw_ref, part_ref, acc_ref, sem):
     v, t = pl.program_id(0), pl.program_id(1)
-    row = pl.multiple_of(sc[0, t] * TB, TB)
-    skip = sc[2, 3]
-
-    expand(t, v, skip, sc[0, t], k_ref, t_ref, kw_ref, tw_ref)
+    bases = spots(sc, 0)
+    skip = sc[4, 3]
+
+    expand(t, v, skip, bases, k_ref, t_ref, kw_ref, tw_ref)
     seq = acc_ref.shape[2]
-    slot = lax.bitwise_xor(lax.div(row, seq), sc[2, 0])
-    place = pl.ds(pl.multiple_of(lax.rem(row, seq), TB), TB)
+    slots = [lax.bitwise_xor(lax.div(base, seq), sc[4, 0]) for base in bases]
+    places = [pl.ds(pl.multiple_of(lax.rem(base, seq), LANE), LANE) for base in bases]
 
     @pl.when((v == 0) & (t >= skip))
     def _():
-        acc_ref[slot, :, place] = jnp.zeros((acc_ref.shape[1], TB), F32)
+        for slot, place in zip(slots, places):
+            acc_ref[slot, :, place] = jnp.zeros((acc_ref.shape[1], LANE), F32)
 
     @pl.when((v == 0) & (t == 0))
     def _():
@@ -127,22 +141,24 @@
 
     @pl.when(t >= skip)
     def _():
-        zc = jnp.concatenate([za_ref[ALL], zb_ref[ALL]], axis=0)
-        half = za_ref.shape[0]
+        zc = pair_columns(za0, za1, zb0, zb1)
+        half = za0.shape[0]
         scale = jnp.concatenate([inv_ref[ALL], inv_ref[ALL]], axis=0)
         n = VB // SC
         get = lambda r, o: l_ref[0, 0, 16 * r:16 * r + 16, o:o + LANE]
         for c in range(n + 1):
             if c < n:
-                dlogits_stage(get, dl_ref, kw_ref, scale, tw_ref, tl_ref, row, v * VB, c, SC)
+                dlogits_stage(get, dl_ref, kw_ref, scale, tw_ref, tl_ref, bases, v * VB, c, SC)
             if c > 0:
                 q = slice((c - 1) * SC, c * SC)
                 dl = dl_ref[:, q]
-                acc_ref[slot, :, place] += lax.dot_general(
-                    e_ref[:, q], dl, (((1,), (1,)), ((), ())), preferred_element_type=F32)
+                dz = lax.dot_general(e_ref[:, q], dl, (((1,), (1,)), ((), ())), preferred_element_type=F32)
+                part_ref[ALL] = dz if c == 1 else part_ref[ALL] + dz
                 de = jnp.dot(zc, dl, preferred_element_type=F32)
                 da_ref[:, q] += de[:half]
                 db_ref[:, q] += de[half:]
+        for h, (slot, place) in enumerate(zip(slots, places)):
+            acc_ref[slot, :, place] += part_ref[:, LANE * h:LANE * h + LANE]
 
     @pl.when((v == pl.num_programs(0) - 1) & (t == pl.num_programs(1) - 1))
     def _():
@@ -153,11 +169,11 @@
             copy.wait()
 
 
-def other_kernel(sc, z_ref, e_ref, za_ref, zb_ref, k_ref, t_ref, inv_ref, ia_ref, ib_ref, da_ref, db_ref, l_ref, dl_ref, kw_ref, tw_ref):
+def other_kernel(sc, z0, z1, e_ref, za0, za1, zb0, zb1, k_ref, t_ref, inv_ref, ia_ref, ib_ref, da_ref, db_ref, l_ref, dl_ref, kw_ref, tw_ref):
     v, t = pl.program_id(0), pl.program_id(1)
-    row = pl.multiple_of(sc[1, t] * TB, TB)
-    skip = sc[2, 4]
-    expand(t, v, skip, sc[1, t], k_ref, t_ref, kw_ref, tw_ref)
+    bases = spots(sc, 2)
+    skip = sc[4, 4]
+    expand(t, v, skip, bases, k_ref, t_ref, kw_ref, tw_ref)
 
     @pl.when(t == skip)
     def _():
@@ -166,17 +182,18 @@
 
     @pl.when(t >= skip)
     def _():
-        zc = jnp.concatenate([za_ref[ALL], zb_ref[ALL]], axis=0)
-        half = za_ref.shape[0]
+        zc = pair_columns(za0, za1, zb0, zb1)
+        half = za0.shape[0]
+        z = jnp.concatenate([z0[ALL], z1[ALL]], axis=0)
         scale = jnp.concatenate([inv_ref[ALL], inv_ref[ALL]], axis=0)
         n = VB // SF
         get = lambda r, o: l_ref[16 * r:16 * r + 16, o:o + LANE] * LOG2E
         for c in range(n + 2):
             if c < n:
                 q = slice(c * SF, (c + 1) * SF)
-                l_ref[:, q] = jnp.dot(z_ref[ALL], e_ref[:, q], preferred_element_type=F32)
+                l_ref[:, q] = jnp.dot(z, e_ref[:, q], preferred_element_type=F32)
             if 0 < c <= n:
-                dlogits_stage(get, dl_ref, kw_ref, scale, tw_ref, None, row, v * VB, c - 1, SF)
+                dlogits_stage(get, dl_ref, kw_ref, scale, tw_ref, None, bases, v * VB, c - 1, SF)
             if c > 1:
                 q = slice((c - 2) * SF, (c - 1) * SF)
                 de = jnp.dot(zc, dl_ref[:, q], preferred_element_type=F32)
@@ -209,15 +226,14 @@
     return (i + 1 - 2 * lax.rem(i, 2), lax.rem(i + 2, 4), 3 - i)[k - 1]
 
 
-def expand(t, v, skip, tile, k_ref, t_ref, kw_ref, tw_ref):
+def expand(t, v, skip, bases, k_ref, t_ref, kw_ref, tw_ref):
     @pl.when((v == 0) & (t >= skip))
     def _():
         lane = lax.broadcasted_iota(jnp.int32, (1, LANE), 1)
-        for h in range(TB // LANE):
-            r = tile * (TB // LANE) + h
-            at = pl.ds(pl.multiple_of(r * LANE, LANE), LANE)
-            kw_ref[at, :] = columns(k_ref[pl.ds(r, 1), :])
-            tw_ref[at, :] = columns(t_ref[pl.ds(r, 1), :]) - lane
+        for base in bases:
+            r = pl.ds(lax.div(base, LANE), 1)
+            kw_ref[pl.ds(base, LANE), :] = columns(k_ref[r, :])
+            tw_ref[pl.ds(base, LANE), :] = columns(t_ref[r, :]) - lane
 
 
 def columns(row):
@@ -304,7 +320,7 @@
     for q in range(4):
         length = over_lanes(all_ref[q, 1:2, :].astype(F32))
         total = total + length
-        tiles.append(jnp.floor((length + (TB - 1)) * (1.0 / TB)).astype(jnp.int32))
+        tiles.append(jnp.floor((length + (LANE - 1)) * (1.0 / LANE)).astype(jnp.int32))
     inv_ref[ALL] = jnp.broadcast_to(1.0 / total, inv_ref.shape)
     nt = 2 * seq // TB
     lane = lax.broadcasted_iota(jnp.int32, (1, LANE), 1)
@@ -315,16 +331,17 @@
     for c in range(2):
         na = jnp.where(swap, pairs[1 - c][0], pairs[c][0])
         nb = jnp.where(swap, pairs[1 - c][1], pairs[c][1])
-        skip = nt - na - nb
-        p = jnp.maximum(lane - skip, 0)
-        lst = jnp.where(p < na, p, nt // 2 + p - na)
-        out.append(jnp.minimum(lst, nt - 1))
+        skip = nt - lax.shift_right_logical(na + nb + 1, 1)
+        full = seq // LANE
+        spare = jnp.minimum(jnp.where(na < full, na, full + nb), 2 * full - 1)
+        for h in range(TB // LANE):
+            p = 2 * jnp.maximum(lane - skip, 0) + h
+            out.append(jnp.where(p < na, p, jnp.where(p < na + nb, full + p - na, spare)))
         skips.append(skip)
     row = jnp.where(lane == 0, core, jnp.where(lane == 1, dp, jnp.where(lane == 2, xor(dp, 1), jnp.where(lane == 3, skips[0], jnp.where(lane == 4, skips[1], tp * vocab_local)))))
     table_ref[ALL] = jnp.zeros_like(table_ref)
-    table_ref[0:1, :] = out[0]
-    table_ref[1:2, :] = out[1]
-    table_ref[2:3, :] = row
+    for k, line in enumerate(out + [row]):
+        table_ref[k:k + 1, :] = line
 
     copies[3].wait()
     other = xor(dp, 1) - 2 * chip
@@ -441,9 +458,9 @@
     @pl.when(b == 0)
     def _():
         for q, g in enumerate(lists):
-            who = sc[2, 1] if q == 0 else xor(sc[2, 1], q)
+            who = sc[4, 1] if q == 0 else xor(sc[4, 1], q)
             for j in range(seq // LANE):
-                id_ref[q, LANE * j:LANE * j + LANE, :] = columns(all_ref[who, 2:3, LANE * j:LANE * j + LANE]) - sc[2, 5]
+                id_ref[q, LANE * j:LANE * j + LANE, :] = columns(all_ref[who, 2:3, LANE * j:LANE * j + LANE]) - sc[4, 5]
             row_ref[q, 0:seq, :] = g[ALL].astype(BF16).T
             id_ref[q, seq:, :] = jnp.full((CH, LANE), -MIB, jnp.int32)
             row_ref[q, seq:, :] = jnp.zeros((CH, row_ref.shape[2]), BF16)
@@ -530,22 +547,22 @@
                 name="swap", cost_estimate=cost(SMALL))(own, give, a, b)
 
         def specs(r):
-            at = lambda x, t: lax.bitwise_xor(x[r, t], x[2, 0] * (nt // 2)) if r else x[r, t]
+            at = lambda x, t, h: lax.bitwise_xor(x[r + h, t], x[4, 0] * (seq // LANE)) if r else x[h, t]
             full = lambda v, t, x: (0, 0)
+            halves = range(TB // LANE)
             return dict(
-                e=pl.BlockSpec((d, VB), lambda v, t, x: (0, x[2, 0] * nv + v)),
-                z=pl.BlockSpec((TB, d), lambda v, t, x: (at(x, t), 0)),
-                l=pl.BlockSpec((1, 1, TB, VB), lambda v, t, x: (x[r, t], v, 0, 0)),
-                vec=pl.BlockSpec((2 * seq, LANE), full),
-                row=pl.BlockSpec((2 * seq // LANE, LANE), full),
-                any=pl.BlockSpec(memory_space=pl.ANY),
-                inv=pl.BlockSpec((8, LANE), full),
-                za=pl.BlockSpec((cols, TB), lambda v, t, x: (x[2, 1], at(x, t))),
-                zb=pl.BlockSpec((cols, TB), lambda v, t, x: (x[2, 2], at(x, t))),
-                de=pl.BlockSpec((cols, VB), lambda v, t, x: (0, v)))
-
-        pick = lambda sp, *names: [sp[k] for k in names]
-        own, other = specs(0), specs(1)
+                e=[pl.BlockSpec((d, VB), lambda v, t, x: (0, x[4, 0] * nv + v))],
+                z=[pl.BlockSpec((LANE, d), lambda v, t, x, h=h: (at(x, t, h), 0)) for h in halves],
+                l=[pl.BlockSpec((1, 1, TB, VB), lambda v, t, x: (jnp.maximum(t, x[4, 3]), v, 0, 0))],
+                vec=[pl.BlockSpec((2 * seq, LANE), full)],
+                row=[pl.BlockSpec((2 * seq // LANE, LANE), full)],
+                any=[pl.BlockSpec(memory_space=pl.ANY)],
+                inv=[pl.BlockSpec((8, LANE), full)],
+                zc=[pl.BlockSpec((cols, LANE), lambda v, t, x, h=h, k=k: (x[4, k], at(x, t, h))) for k in (1, 2) for h in halves],
+                de=[pl.BlockSpec((cols, VB), lambda v, t, x: (0, v))])
+
+        pick = lambda sp, *names: [b for k in names for b in sp[k]]
+        own, other = specs(0), specs(2)
         vec = shape((2 * seq, LANE), F32)
         wide = [pltpu.VMEM((2 * seq, LANE), F32), pltpu.VMEM((2 * seq, LANE), jnp.int32)]
         de_shape = shape((cols, half), F32)
@@ -558,7 +575,7 @@
             out_shape=[shape((nt, nv, TB, VB), F32), vec, vec],
             compiler_params=params(), name="logits",
             cost_estimate=cost(flops),
-        )(table, z_chip, et)
+        )(table, z_chip, z_chip, et)
 
         rows = 2 * seq // LANE
         k_own, t_own, t_far, lse_sum, look = single(
@@ -576,12 +593,12 @@
             own_kernel,
             grid_spec=pltpu.PrefetchScalarGridSpec(
                 num_scalar_prefetch=1, grid=(nv, nt),
-                in_specs=pick(own, "l", "e", "za", "zb", "row", "row", "inv"), out_specs=pick(own, "any", "any", "de", "de", "vec"),
-                scratch_shapes=[pltpu.VMEM((TB, VB), BF16), *wide, pltpu.VMEM((2, d, seq), F32), dma((2,))]),
+                in_specs=pick(own, "l", "e", "zc", "row", "row", "inv"), out_specs=pick(own, "any", "any", "de", "de", "vec"),
+                scratch_shapes=[pltpu.VMEM((TB, VB), BF16), *wide, pltpu.VMEM((d, TB), F32), pltpu.VMEM((2, d, seq), F32), dma((2,))]),
             out_shape=[shape((d, seq), F32), shape((d, seq), F32), de_shape, de_shape, vec],
             compiler_params=params(), name="own",
             cost_estimate=cost(flops + flops // 2),
-        )(table, l_own, et, zt_chip, zt_chip, k_own, t_own, inv_n)
+        )(table, l_own, et, *[zt_chip] * 4, k_own, t_own, inv_n)
 
         zt_far, z_far, dz_half = swap_call(dz_own, dz_give, far, far_near)
         dz_tp = lax.ppermute(dz_half, "tp", [(0, 1), (1, 0)])
@@ -590,12 +607,12 @@
             other_kernel,
             grid_spec=pltpu.PrefetchScalarGridSpec(
                 num_scalar_prefetch=1, grid=(nv, nt),
-                in_specs=pick(other, "z", "e", "za", "zb", "row", "row", "inv", "de", "de"), out_specs=pick(other, "de", "de"),
+                in_specs=pick(other, "z", "e", "zc", "row", "row", "inv", "de", "de"), out_specs=pick(other, "de", "de"),
                 scratch_shapes=[pltpu.VMEM((TB, VB), F32), pltpu.VMEM((TB, VB), BF16), *wide]),
             out_shape=[de_shape, de_shape],
             compiler_params=params(), name="other",
             cost_estimate=cost(flops + flops // 2),
-        )(table, z_far, et, zt_far, zt_far, k_far, t_far, inv_n, da, db)
+        )(table, z_far, z_far, et, *[zt_far] * 4, k_far, t_far, inv_n, da, db)
         got = lax.ppermute(db, "dp", swap[1])
 
         nb = half // LW
@@ -616,14 +633,14 @@
                 cost_estimate=cost(flops // 8),
             )(table, look, source, *lists, metas, *prior)
 
-        de_t = lookup(lambda x, b: x[2, 0] * nb + b, da)
+        de_t = lookup(lambda x, b: x[4, 0] * nb + b, da)
 
         dht, dg, loss = single(
             final_kernel, (dz_half, dz_tp, ht, norm_w, loss_mask, tl, lse_sum, inv_n),
             [shape((d, seq), BF16), shape((d,), F32), shape((1, LANE), F32)],
             [pltpu.VMEM((8, 640), F32), pltpu.VMEM((8, 8, 640), F32), dma((7,)), dma((7,))], 2)
 
-        de_t = lookup(lambda x, b: (1 - x[2, 0]) * nb + b, got, de_t)
+        de_t = lookup(lambda x, b: (1 - x[4, 0]) * nb + b, got, de_t)
         return loss[0, 0], dht.T[None], dg, de_t.T
 
     return jax.shard_map(

time: 253 us -> 245 us (0.968)
  Pallas kernels: 195 us -> 181 us
  starting transfers between devices: 5.53 us -> 11.7 us
    pallas_call x1, Pallas kernels: 46.2 us -> 39.5 us  [local_step(): pl.pallas_call(own_kernel, grid_spec=pltpu.PrefetchScalarGridSpec(num_sca...]
    ppermute x1, starting transfers between devices: 0.58 us -> 6.73 us  [local_step(): k_far = lax.ppermute(k_own, 'dp', swap[2])]
    pallas_call x1, Pallas kernels: 35.6 us -> 30.4 us  [local_step(): pl.pallas_call(logits_kernel, grid_spec=pltpu.PrefetchScalarGridSpec(num_...]
    pallas_call x2, Pallas kernels: 24.3 us -> 21.6 us  [lookup(): pl.pallas_call(functools.partial(lookup_kernel, top), grid_spec=pltpu.Pre...]
  transfers between devices with their start and end apart: 8 -> 8, of which waited for: 5 -> 5; matrix products, arithmetic and copies ran while one was open for 0% -> 0% of each run, Pallas kernels for 48% -> 44%
where the time goes in v4:
time: 245 us
  Pallas kernels  181 us (74%)
  waiting for transfers between devices  46.6 us (19%)
  starting transfers between devices  11.7 us (5%)
  local copies, waits for them, and re-layouts  3.02 us (1%)
    pallas_call x1, Pallas kernels, local_step(): pl.pallas_call(other_kernel, grid_spec=pltpu.PrefetchScalarGridSpec(num_s...  47.5 us
    pallas_call x1, Pallas kernels, local_step(): pl.pallas_call(own_kernel, grid_spec=pltpu.PrefetchScalarGridSpec(num_sca...  39.5 us
    pallas_call x3, Pallas kernels, single(): pl.pallas_call(kernel, grid=(1,), in_specs=blocks(*args), out_specs=block...  32.2 us
    pallas_call x1, Pallas kernels, local_step(): pl.pallas_call(logits_kernel, grid_spec=pltpu.PrefetchScalarGridSpec(num_...  30.4 us
    ppermute x3, waiting for transfers between devices, local_step(): lists.append(lax.ppermute(give[k], 'dp', swap[k]))  26.1 us
    pallas_call x2, Pallas kernels, lookup(): pl.pallas_call(functools.partial(lookup_kernel, top), grid_spec=pltpu.Pre...  21.6 us
    ppermute x1, waiting for transfers between devices, local_step(): dz_tp = lax.ppermute(dz_half, 'tp', [(0, 1), (1, 0)])  12.2 us
    pallas_call x1, Pallas kernels, swap_call(): pl.pallas_call(swap_kernel, grid=(8,), in_specs=[pl.BlockSpec((d, seq), l...  10 us
  transfers between devices with their start and end apart: 8, of which 5 were waited for; matrix products, arithmetic and copies ran while one was open for 0% of the time, Pallas kernels for 44%

profile of v4, /device:TPU:0, one launch (start us, length us, event | category | flops | bytes accessed | tf_op | source)
XLA Modules:
  0.0 244.5 jit_solution(2804550914313643034)
XLA Ops:
  0.6 14.9 %shard_map.102 = (f32[576,1024]{1,0:T(8,128)}, bf16[576,2048]{1,0:T(8,128)(2,1)}, bf16[2048,576]{1,0:T(8,128)(2,1)}, s32[4,8,1024]{2,1,0:T(8,128)}, s32[8,128]{1...) custom-call(bf16[576,1024]{1,0:T(8,128)(2,1)} %bitcast.14, ...), custom_call_target="tpu_custom_call" | custom-call | flops 268435456 | bytes 1048576 | tf_op jit(solution)/shard_map/pallas_call | solution.py:506
  15.5 1.5 collective-permute-start
  17.0 30.4 %logits.1 = (f32[8,2,256,6144]{3,2,1,0:T(8,128)}, f32[2048,128]{1,0:T(8,128)}, f32[2048,128]{1,0:T(8,128)}) custom-call(s32[8,128]{1,0:T(8,128)} %get-tuple-element.35.sc, bf16[2048,576]{1,0:T(8,128)(2,1)} %get-tuple-element.36.z0.z1, bf16[2048,576]{1,0:T(8,128)(2,1)} %get-tuple-element.36.z0.z1, bf16[576,24576]{1,0:T(8,128)(2,1)} %bitcast.18), custom_call_target="tpu_custom_call" | custom-call | flops 28991029248 | bytes 1048576 | tf_op jit(solution)/shard_map/logits/pallas_call | solution.py:571
  47.4 6.6 %shard_map.103 = (f32[16,128]{1,0:T(8,128)}, s32[16,128]{1,0:T(8,128)}, s32[16,128]{1,0:T(8,128)}, f32[8,128]{1,0:T(8,128)}, s32[8,128]{1,0:T(8,128)}) custom-call(f32[2048,128]{1,0:T(8,128)} %get-tuple-element.39.m_ref, f32[2048,128]{1,0:T(8,128)} %get-tuple-element.40.s_ref, s32[4,8,1024]{2,1,0:T(8,128)} %get-tuple-element.41.all_ref), custom_call_target="tpu_custom_call" | custom-call | flops 268435456 | bytes 1048576 | tf_op jit(solution)/shard_map/pallas_call | solution.py:506
  54.1 6.7 %collective-permute-start.3 = (f32[16,128]{1,0:T(8,128)}, f32[16,128]{1,0:T(8,128)S(1)}, u32[]{:S(2)}, u32[]{:S(2)}) collective-permute-start(f32[16,128]{1,0:T(8,128)} %get-tuple-element.42.k_ref), channel_id=1, source_target_pairs={{0,2},{1,3},{2,0},{3,1},{4,6},{5,7},{6,4},{7,5}} | collective-permute-start | bytes 24584 | tf_op jit(solution)/shard_map/ppermute | solution.py:586
  60.8 8.3 %collective-permute-done.a_ref = f32[576,1024]{1,0:T(8,128)S(1)} collective-permute-done((f32[576,1024]{1,0:T(8,128)}, f32[576,1024]{1,0:T(8,128)S(1)}, u32[]{:S(2)}, u32[]{:S(2)}) %collective-permute-start) | collective-permute-done | bytes 2359328 | tf_op jit(solution)/shard_map/ppermute | solution.py:533
  69.1 39.5 %own.1 = (f32[576,1024]{1,0:T(8,128)}, f32[576,1024]{1,0:T(8,128)}, f32[144,12288]{1,0:T(8,128)}, f32[144,12288]{1,0:T(8,128)}, f32[2048,128]{1,0:T(8,128)}) custom-call(s32[8,128]{1,0:T(8,128)} %get-tuple-element.35.sc, f32[8,2,256,6144]{3,2,1,0:T(8,128)} %get-tuple-element.37.l_ref, bf16[576,24576]{1,0:T(8,128)(2,1)} %bitcast.19, ...), custom_call_target="tpu_custom_call" | custom-call | flops 43486543872 | bytes 1048576 | tf_op jit(solution)/shard_map/own/pallas_call | solution.py:592
  108.7 10.0 %swap.1 = (bf16[576,2048]{1,0:T(8,128)(2,1)}, bf16[2048,576]{1,0:T(8,128)(2,1)}, f32[576,1024]{1,0:T(8,128)}) custom-call(f32[576,1024]{1,0:T(8,128)} %get-tuple-element.45.own_ref, f32[576,1024]{1,0:T(8,128)} %get-tuple-element.46.give_ref, f32[576,1024]{1,0:T(8,128)} %copy-done.1, f32[576,1024]{1,0:T(8,128)} %collective-permute-done.1.b_ref), custom_call_target="tpu_custom_call" | custom-call | flops 268435456 | bytes 1048576 | tf_op jit(solution)/shard_map/swap/pallas_call | solution.py:538
  118.7 0.6 copy-done.7
  119.3 47.5 %other.1 = (f32[144,12288]{1,0:T(8,128)}, f32[144,12288]{1,0:T(8,128)}) custom-call(s32[8,128]{1,0:T(8,128)} %get-tuple-element.35.sc, bf16[2048,576]{1,0:T(8,128)(2,1)} %get-tuple-element.55.z0.z1, bf16[2048,576]{1,0:T(8,128)(2,1)} %get-tuple-element.55.z0.z1, bf16[576,24576]{1,0:T(8,128)(2,1)} %bitcast.20, ...), custom_call_target="tpu_custom_call" | custom-call | flops 43486543872 | bytes 1048576 | tf_op jit(solution)/shard_map/other/pallas_call | solution.py:606
  166.8 1.6 collective-permute-start.2
  168.4 0.2 collective-permute-start.5
  168.6 0.6 collective-permute-start.6
  169.2 1.1 collective-permute-start.7
  170.3 8.9 %collective-permute-done.5.g2 = f32[144,1024]{1,0:T(8,128)S(1)} collective-permute-done((f32[144,1024]{1,0:T(8,128)}, f32[144,1024]{1,0:T(8,128)S(1)}, u32[]{:S(2)}, u32[]{:S(2)}) %collective-permute-start.5) | collective-permute-done | bytes 589856 | tf_op jit(solution)/shard_map/ppermute | solution.py:590
  179.1 5.9 %collective-permute-done.6.g3 = f32[144,1024]{1,0:T(8,128)S(1)} collective-permute-done((f32[144,1024]{1,0:T(8,128)}, f32[144,1024]{1,0:T(8,128)S(1)}, u32[]{:S(2)}, u32[]{:S(2)}) %collective-permute-start.6) | collective-permute-done | bytes 589856 | tf_op jit(solution)/shard_map/ppermute | solution.py:590
  185.0 11.3 %collective-permute-done.7.g4 = f32[144,1024]{1,0:T(8,128)S(1)} collective-permute-done((f32[144,1024]{1,0:T(8,128)}, f32[144,1024]{1,0:T(8,128)S(1)}, u32[]{:S(2)}, u32[]{:S(2)}) %collective-permute-start.7) | collective-permute-done | bytes 589856 | tf_op jit(solution)/shard_map/ppermute | solution.py:590
  196.3 0.8 copy-done.4
  197.1 11.2 %lookup.2.rest_0_ = f32[144,24576]{1,0:T(8,128)} custom-call(s32[8,128]{1,0:T(8,128)} %get-tuple-element.35.sc, s32[8,128]{1,0:T(8,128)} %get-tuple-element.54.look, f32[144,12288]{1,0:T(8,128)} %get-tuple-element.65.from_ref, f32[144,1024]{1,0:T(8,128)} %get-tuple-element.61.g1, f32[144,1024]{1,0:T(8,128)} %copy-done.2, f32[144,1024]{1,0:T(8,128)} %copy-done.3, ...), custom_call_target="tpu_custom_call" | custom-call | flops 3623878656 | bytes 1048576 | tf_op jit(solution)/shard_map/lookup/pallas_call | solution.py:622
  208.3 12.2 %collective-permute-done.2.b_ref = f32[576,1024]{1,0:T(8,128)} collective-permute-done((f32[576,1024]{1,0:T(8,128)S(1)}, f32[576,1024]{1,0:T(8,128)}, u32[]{:S(2)}, u32[]{:S(2)}) %collective-permute-start.2) | collective-permute-done | bytes 2359328 | tf_op jit(solution)/shard_map/ppermute | solution.py:604
  220.6 10.7 %shard_map.104 = (bf16[576,1024]{1,0:T(8,128)(2,1)}, f32[576]{0:T(1024)}, f32[1,128]{1,0:T(1,128)}) custom-call(f32[576,1024]{1,0:T(8,128)} %get-tuple-element.48.a_ref, f32[576,1024]{1,0:T(8,128)} %collective-permute-done.2.b_ref, bf16[576,1024]{1,0:T(8,128)(2,1)} %bitcast.15, bf16[576]{0:T(1024)(128)(2,1)} %g_ref.3, s32[1,1024]{1,0:T(1,128)} %on_ref.1, ...), custom_call_target="tpu_custom_call" | custom-call | flops 268435456 | bytes 1048576 | tf_op jit(solution)/shard_map/pallas_call | solution.py:506
  231.3 10.5 %lookup.3 = f32[144,24576]{1,0:T(8,128)} custom-call(s32[8,128]{1,0:T(8,128)} %get-tuple-element.35.sc, s32[8,128]{1,0:T(8,128)} %get-tuple-element.54.look, f32[144,12288]{1,0:T(8,128)} %collective-permute-done.4.from_ref, f32[144,1024]{1,0:T(8,128)} %get-tuple-element.61.g1, f32[144,1024]{1,0:T(8,128)} %copy-done.2, ...), custom_call_target="tpu_custom_call", output_to_operand_aliasing={{}: (8, {})} | custom-call | flops 3623878656 | bytes 1048576 | tf_op jit(solution)/shard_map/lookup/pallas_call | solution.py:622
  241.8 1.0 copy.17
  242.8 0.6 copy.18
  (21 shorter events, 0.1 us)
Async XLA Ops:
  15.5 53.6 %collective-permute-start = (f32[576,1024]{1,0:T(8,128)}, f32[576,1024]{1,0:T(8,128)S(1)}, u32[]{:S(2)}, u32[]{:S(2)}) collective-permute-start(f32[576,1024]{1,0:T(8,128)} %get-tuple-element.47), channel_id=1, source_target_pairs={{0,2},{1,3},{2,0},{3,1},{4,6},{5,7},{6,4},{7,5}} | collective-permute-start | bytes 7077896 | tf_op jit(solution)/shard_map/ppermute | solution.py:533
  54.1 64.6 %collective-permute-start.3 = (f32[16,128]{1,0:T(8,128)}, f32[16,128]{1,0:T(8,128)S(1)}, u32[]{:S(2)}, u32[]{:S(2)}) collective-permute-start(f32[16,128]{1,0:T(8,128)} %get-tuple-element.42.k_ref), channel_id=1, source_target_pairs={{0,2},{1,3},{2,0},{3,1},{4,6},{5,7},{6,4},{7,5}} | collective-permute-start | bytes 24584 | tf_op jit(solution)/shard_map/ppermute | solution.py:586
  69.1 39.6 %copy-start.1 = (f32[576,1024]{1,0:T(8,128)}, f32[576,1024]{1,0:T(8,128)S(1)}, u32[]{:S(2)}) copy-start(f32[576,1024]{1,0:T(8,128)S(1)} %collective-permute-done.a_ref) | copy-start | bytes 7077892
  69.1 39.6 %collective-permute-start.1 = (f32[576,1024]{1,0:T(8,128)S(1)}, f32[576,1024]{1,0:T(8,128)}, u32[]{:S(2)}, u32[]{:S(2)}) collective-permute-start(f32[576,1024]{1,0:T(8,128)S(1)} %collective-permute-done.a_ref), channel_id=1, source_target_pairs={{0,1},{1,0},{2,3},{3,2},{4,5},{5,4},{6,7},{7,6}} | collective-permute-start | bytes 7077896 | tf_op jit(solution)/shard_map/ppermute | solution.py:534
  118.7 0.6 copy-start.7
  119.3 47.5 %copy-start = (f32[576,1024]{1,0:T(8,128)S(1)}, f32[576,1024]{1,0:T(8,128)}, u32[]{:S(2)}) copy-start(f32[576,1024]{1,0:T(8,128)} %get-tuple-element.48.a_ref) | copy-start | bytes 7077892
  166.8 64.5 %collective-permute-start.4 = (f32[144,12288]{1,0:T(8,128)}, f32[144,12288]{1,0:T(8,128)}, u32[]{:S(2)}, u32[]{:S(2)}) collective-permute-start(f32[144,12288]{1,0:T(8,128)} %get-tuple-element.60), channel_id=1, source_target_pairs={{0,1},{1,0},{2,3},{3,2},{4,5},{5,4},{6,7},{7,6}} | collective-permute-start | bytes 21233672 | tf_op jit(solution)/shard_map/ppermute | solution.py:616
  166.8 53.7 %collective-permute-start.2 = (f32[576,1024]{1,0:T(8,128)S(1)}, f32[576,1024]{1,0:T(8,128)}, u32[]{:S(2)}, u32[]{:S(2)}) collective-permute-start(f32[576,1024]{1,0:T(8,128)S(1)} %copy-done), channel_id=1, source_target_pairs={{0,4},{4,0},{1,5},{5,1},{2,6},{6,2},{3,7},{7,3}} | collective-permute-start | bytes 7077896 | tf_op jit(solution)/shard_map/ppermute | solution.py:604
  168.4 10.7 %collective-permute-start.5 = (f32[144,1024]{1,0:T(8,128)}, f32[144,1024]{1,0:T(8,128)S(1)}, u32[]{:S(2)}, u32[]{:S(2)}) collective-permute-start(f32[144,1024]{1,0:T(8,128)} %get-tuple-element.62), channel_id=1, source_target_pairs={{0,1},{1,0},{2,3},{3,2},{4,5},{5,4},{6,7},{7,6}} | collective-permute-start | bytes 1769480 | tf_op jit(solution)/shard_map/ppermute | solution.py:590
  168.6 16.4 %collective-permute-start.6 = (f32[144,1024]{1,0:T(8,128)}, f32[144,1024]{1,0:T(8,128)S(1)}, u32[]{:S(2)}, u32[]{:S(2)}) collective-permute-start(f32[144,1024]{1,0:T(8,128)} %get-tuple-element.63), channel_id=1, source_target_pairs={{0,2},{1,3},{2,0},{3,1},{4,6},{5,7},{6,4},{7,5}} | collective-permute-start | bytes 1769480 | tf_op jit(solution)/shard_map/ppermute | solution.py:590
  169.2 27.2 %collective-permute-start.7 = (f32[144,1024]{1,0:T(8,128)}, f32[144,1024]{1,0:T(8,128)S(1)}, u32[]{:S(2)}, u32[]{:S(2)}) collective-permute-start(f32[144,1024]{1,0:T(8,128)} %get-tuple-element.64), channel_id=1, source_target_pairs={{0,3},{1,2},{2,1},{3,0},{4,7},{5,6},{6,5},{7,4}} | collective-permute-start | bytes 1769480 | tf_op jit(solution)/shard_map/ppermute | solution.py:590
  179.1 17.2 %copy-start.2 = (f32[144,1024]{1,0:T(8,128)}, f32[144,1024]{1,0:T(8,128)S(1)}, u32[]{:S(2)}) copy-start(f32[144,1024]{1,0:T(8,128)S(1)} %collective-permute-done.5.g2) | copy-start | bytes 1769476
  185.0 11.3 %copy-start.3 = (f32[144,1024]{1,0:T(8,128)}, f32[144,1024]{1,0:T(8,128)S(1)}, u32[]{:S(2)}) copy-start(f32[144,1024]{1,0:T(8,128)S(1)} %collective-permute-done.6.g3) | copy-start | bytes 1769476
  196.3 0.8 copy-start.4
  231.2 10.5 %copy-start.8 = (f32[1,128]{1,0:T(1,128)S(1)}, f32[1,128]{1,0:T(1,128)}, u32[]{:S(2)}) copy-start(f32[1,128]{1,0:T(1,128)} %get-tuple-element.51) | copy-start | bytes 1540
  231.2 10.5 %copy-start.5 = (bf16[576,1024]{1,0:T(8,128)(2,1)S(1)}, bf16[576,1024]{1,0:T(8,128)(2,1)}, u32[]{:S(2)}) copy-start(bf16[576,1024]{1,0:T(8,128)(2,1)} %get-tuple-element.52) | copy-start | bytes 3538948
  241.7 1.1 copy-start.6

commit v5 on v4

--- a/solution.py
+++ b/solution.py
@@ -16,7 +16,7 @@
 SC = 512
 SF = 1024
 LW = 6144
-LB = 1024
+LB = 512
 CH = 128
 ST = 16
 LANE = 128
@@ -212,7 +212,7 @@
         greet([peer])
         copy.start()
 
-    z = jnp.where(i < 4, a_ref[ALL], b_ref[ALL]).astype(BF16)
+    z = jnp.where(i < 2, a_ref[ALL], b_ref[ALL]).astype(BF16)
     zt_ref[ALL] = z
     z_ref[ALL] = z.T
 
@@ -534,11 +534,11 @@
         far_near = lax.ppermute(far, "dp", swap[1])
 
         def swap_call(own, give, a, b):
-            w = 2 * seq // 8
+            w = seq // 2
             return pl.pallas_call(
-                swap_kernel, grid=(8,),
+                swap_kernel, grid=(4,),
                 in_specs=[pl.BlockSpec((d, seq), lambda i: (0, 0)), pl.BlockSpec(memory_space=pl.ANY),
-                          pl.BlockSpec((d, w), lambda i: (0, jnp.minimum(i, 3))), pl.BlockSpec((d, w), lambda i: (0, jnp.maximum(i - 4, 0)))],
+                          pl.BlockSpec((d, w), lambda i: (0, jnp.minimum(i, 1))), pl.BlockSpec((d, w), lambda i: (0, jnp.maximum(i - 2, 0)))],
                 out_specs=[pl.BlockSpec((d, w), lambda i: (0, i)), pl.BlockSpec((w, d), lambda i: (i, 0)), pl.BlockSpec((d, seq), lambda i: (0, 0))],
                 out_shape=[shape((d, 2 * seq), BF16), shape((2 * seq, d), BF16), shape((d, seq), F32)],
                 scratch_shapes=[pltpu.VMEM((d, seq), F32), dma((1,)), dma((1,))],

time: 245 us -> 244 us (level)
  no operation moved by 1% of the time
where the time goes in v5:
time: 244 us; the launch traced here: 243 us
  Pallas kernels  179 us (73%)
  waiting for transfers between devices  47.6 us (20%)
  starting transfers between devices  12 us (5%)
  local copies, waits for them, and re-layouts  3.02 us (1%)
    pallas_call x1, Pallas kernels, local_step(): pl.pallas_call(other_kernel, grid_spec=pltpu.PrefetchScalarGridSpec(num_s...  47.5 us
    pallas_call x1, Pallas kernels, local_step(): pl.pallas_call(own_kernel, grid_spec=pltpu.PrefetchScalarGridSpec(num_sca...  39.5 us
    pallas_call x3, Pallas kernels, single(): pl.pallas_call(kernel, grid=(1,), in_specs=blocks(*args), out_specs=block...  32.2 us
    pallas_call x1, Pallas kernels, local_step(): pl.pallas_call(logits_kernel, grid_spec=pltpu.PrefetchScalarGridSpec(num_...  30.4 us
    ppermute x3, waiting for transfers between devices, local_step(): lists.append(lax.ppermute(give[k], 'dp', swap[k]))  26.3 us
    pallas_call x2, Pallas kernels, lookup(): pl.pallas_call(functools.partial(lookup_kernel, top), grid_spec=pltpu.Pre...  19.9 us
    ppermute x1, waiting for transfers between devices, local_step(): dz_tp = lax.ppermute(dz_half, 'tp', [(0, 1), (1, 0)])  13 us
    pallas_call x1, Pallas kernels, swap_call(): pl.pallas_call(swap_kernel, grid=(4,), in_specs=[pl.BlockSpec((d, seq), l...  9.35 us
  transfers between devices with their start and end apart: 8, of which 5 were waited for; matrix products, arithmetic and copies ran while one was open for 0% of the time, Pallas kernels for 44%

profile of v5, /device:TPU:0, one launch (start us, length us, event | category | flops | bytes accessed | tf_op | source)
XLA Modules:
  0.0 243.4 jit_solution(2547599826837428330)
XLA Ops:
  0.6 14.9 %shard_map.102 = (f32[576,1024]{1,0:T(8,128)}, bf16[576,2048]{1,0:T(8,128)(2,1)}, bf16[2048,576]{1,0:T(8,128)(2,1)}, s32[4,8,1024]{2,1,0:T(8,128)}, s32[8,128]{1...) custom-call(bf16[576,1024]{1,0:T(8,128)(2,1)} %bitcast.14, ...), custom_call_target="tpu_custom_call" | custom-call | flops 268435456 | bytes 1048576 | tf_op jit(solution)/shard_map/pallas_call | solution.py:506
  15.5 1.5 collective-permute-start
  17.0 30.4 %logits.1 = (f32[8,2,256,6144]{3,2,1,0:T(8,128)}, f32[2048,128]{1,0:T(8,128)}, f32[2048,128]{1,0:T(8,128)}) custom-call(s32[8,128]{1,0:T(8,128)} %get-tuple-element.35.sc, bf16[2048,576]{1,0:T(8,128)(2,1)} %get-tuple-element.36.z0.z1, bf16[2048,576]{1,0:T(8,128)(2,1)} %get-tuple-element.36.z0.z1, bf16[576,24576]{1,0:T(8,128)(2,1)} %bitcast.18), custom_call_target="tpu_custom_call" | custom-call | flops 28991029248 | bytes 1048576 | tf_op jit(solution)/shard_map/logits/pallas_call | solution.py:571
  47.4 6.6 %shard_map.103 = (f32[16,128]{1,0:T(8,128)}, s32[16,128]{1,0:T(8,128)}, s32[16,128]{1,0:T(8,128)}, f32[8,128]{1,0:T(8,128)}, s32[8,128]{1,0:T(8,128)}) custom-call(f32[2048,128]{1,0:T(8,128)} %get-tuple-element.39.m_ref, f32[2048,128]{1,0:T(8,128)} %get-tuple-element.40.s_ref, s32[4,8,1024]{2,1,0:T(8,128)} %get-tuple-element.41.all_ref), custom_call_target="tpu_custom_call" | custom-call | flops 268435456 | bytes 1048576 | tf_op jit(solution)/shard_map/pallas_call | solution.py:506
  54.1 6.7 %collective-permute-start.3 = (f32[16,128]{1,0:T(8,128)}, f32[16,128]{1,0:T(8,128)S(1)}, u32[]{:S(2)}, u32[]{:S(2)}) collective-permute-start(f32[16,128]{1,0:T(8,128)} %get-tuple-element.42.k_ref), channel_id=1, source_target_pairs={{0,2},{1,3},{2,0},{3,1},{4,6},{5,7},{6,4},{7,5}} | collective-permute-start | bytes 24584 | tf_op jit(solution)/shard_map/ppermute | solution.py:586
  60.8 8.3 %collective-permute-done.a_ref = f32[576,1024]{1,0:T(8,128)S(1)} collective-permute-done((f32[576,1024]{1,0:T(8,128)}, f32[576,1024]{1,0:T(8,128)S(1)}, u32[]{:S(2)}, u32[]{:S(2)}) %collective-permute-start) | collective-permute-done | bytes 2359328 | tf_op jit(solution)/shard_map/ppermute | solution.py:533
  69.1 39.5 %own.1 = (f32[576,1024]{1,0:T(8,128)}, f32[576,1024]{1,0:T(8,128)}, f32[144,12288]{1,0:T(8,128)}, f32[144,12288]{1,0:T(8,128)}, f32[2048,128]{1,0:T(8,128)}) custom-call(s32[8,128]{1,0:T(8,128)} %get-tuple-element.35.sc, f32[8,2,256,6144]{3,2,1,0:T(8,128)} %get-tuple-element.37.l_ref, bf16[576,24576]{1,0:T(8,128)(2,1)} %bitcast.19, ...), custom_call_target="tpu_custom_call" | custom-call | flops 43486543872 | bytes 1048576 | tf_op jit(solution)/shard_map/own/pallas_call | solution.py:592
  108.7 9.3 %swap.1 = (bf16[576,2048]{1,0:T(8,128)(2,1)}, bf16[2048,576]{1,0:T(8,128)(2,1)}, f32[576,1024]{1,0:T(8,128)}) custom-call(f32[576,1024]{1,0:T(8,128)} %get-tuple-element.45.own_ref, f32[576,1024]{1,0:T(8,128)} %get-tuple-element.46.give_ref, f32[576,1024]{1,0:T(8,128)} %copy-done.1, f32[576,1024]{1,0:T(8,128)} %collective-permute-done.1.b_ref), custom_call_target="tpu_custom_call" | custom-call | flops 268435456 | bytes 1048576 | tf_op jit(solution)/shard_map/swap/pallas_call | solution.py:538
  118.1 0.6 copy-done.7
  118.6 47.5 %other.1 = (f32[144,12288]{1,0:T(8,128)}, f32[144,12288]{1,0:T(8,128)}) custom-call(s32[8,128]{1,0:T(8,128)} %get-tuple-element.35.sc, bf16[2048,576]{1,0:T(8,128)(2,1)} %get-tuple-element.55.z0.z1, bf16[2048,576]{1,0:T(8,128)(2,1)} %get-tuple-element.55.z0.z1, bf16[576,24576]{1,0:T(8,128)(2,1)} %bitcast.20, ...), custom_call_target="tpu_custom_call" | custom-call | flops 43486543872 | bytes 1048576 | tf_op jit(solution)/shard_map/other/pallas_call | solution.py:606
  166.1 0.4 collective-permute-start.4
  166.5 1.6 collective-permute-start.2
  168.1 0.5 collective-permute-start.6
  168.6 1.3 collective-permute-start.7
  169.9 8.5 %collective-permute-done.5.g2 = f32[144,1024]{1,0:T(8,128)S(1)} collective-permute-done((f32[144,1024]{1,0:T(8,128)}, f32[144,1024]{1,0:T(8,128)S(1)}, u32[]{:S(2)}, u32[]{:S(2)}) %collective-permute-start.5) | collective-permute-done | bytes 589856 | tf_op jit(solution)/shard_map/ppermute | solution.py:590
  178.5 6.0 %collective-permute-done.6.g3 = f32[144,1024]{1,0:T(8,128)S(1)} collective-permute-done((f32[144,1024]{1,0:T(8,128)}, f32[144,1024]{1,0:T(8,128)S(1)}, u32[]{:S(2)}, u32[]{:S(2)}) %collective-permute-start.6) | collective-permute-done | bytes 589856 | tf_op jit(solution)/shard_map/ppermute | solution.py:590
  184.5 11.7 %collective-permute-done.7.g4 = f32[144,1024]{1,0:T(8,128)S(1)} collective-permute-done((f32[144,1024]{1,0:T(8,128)}, f32[144,1024]{1,0:T(8,128)S(1)}, u32[]{:S(2)}, u32[]{:S(2)}) %collective-permute-start.7) | collective-permute-done | bytes 589856 | tf_op jit(solution)/shard_map/ppermute | solution.py:590
  196.2 0.8 copy-done.4
  197.0 9.9 %lookup.2.rest_0_ = f32[144,24576]{1,0:T(8,128)} custom-call(s32[8,128]{1,0:T(8,128)} %get-tuple-element.35.sc, s32[8,128]{1,0:T(8,128)} %get-tuple-element.54.look, f32[144,12288]{1,0:T(8,128)} %get-tuple-element.65.from_ref, f32[144,1024]{1,0:T(8,128)} %get-tuple-element.61.g1, f32[144,1024]{1,0:T(8,128)} %copy-done.2, f32[144,1024]{1,0:T(8,128)} %copy-done.3, ...), custom_call_target="tpu_custom_call" | custom-call | flops 3623878656 | bytes 1048576 | tf_op jit(solution)/shard_map/lookup/pallas_call | solution.py:622
  206.9 13.0 %collective-permute-done.2.b_ref = f32[576,1024]{1,0:T(8,128)} collective-permute-done((f32[576,1024]{1,0:T(8,128)S(1)}, f32[576,1024]{1,0:T(8,128)}, u32[]{:S(2)}, u32[]{:S(2)}) %collective-permute-start.2) | collective-permute-done | bytes 2359328 | tf_op jit(solution)/shard_map/ppermute | solution.py:604
  219.9 10.7 %shard_map.104 = (bf16[576,1024]{1,0:T(8,128)(2,1)}, f32[576]{0:T(1024)}, f32[1,128]{1,0:T(1,128)}) custom-call(f32[576,1024]{1,0:T(8,128)} %get-tuple-element.48.a_ref, f32[576,1024]{1,0:T(8,128)} %collective-permute-done.2.b_ref, bf16[576,1024]{1,0:T(8,128)(2,1)} %bitcast.15, bf16[576]{0:T(1024)(128)(2,1)} %g_ref.3, s32[1,1024]{1,0:T(1,128)} %on_ref.1, ...), custom_call_target="tpu_custom_call" | custom-call | flops 268435456 | bytes 1048576 | tf_op jit(solution)/shard_map/pallas_call | solution.py:506
  230.6 10.0 %lookup.3 = f32[144,24576]{1,0:T(8,128)} custom-call(s32[8,128]{1,0:T(8,128)} %get-tuple-element.35.sc, s32[8,128]{1,0:T(8,128)} %get-tuple-element.54.look, f32[144,12288]{1,0:T(8,128)} %collective-permute-done.4.from_ref, f32[144,1024]{1,0:T(8,128)} %get-tuple-element.61.g1, f32[144,1024]{1,0:T(8,128)} %copy-done.2, ...), custom_call_target="tpu_custom_call", output_to_operand_aliasing={{}: (8, {})} | custom-call | flops 3623878656 | bytes 1048576 | tf_op jit(solution)/shard_map/lookup/pallas_call | solution.py:622
  240.7 1.0 copy.17
  241.7 0.6 copy.18
  (21 shorter events, 0.0 us)
Async XLA Ops:
  15.5 53.6 %collective-permute-start = (f32[576,1024]{1,0:T(8,128)}, f32[576,1024]{1,0:T(8,128)S(1)}, u32[]{:S(2)}, u32[]{:S(2)}) collective-permute-start(f32[576,1024]{1,0:T(8,128)} %get-tuple-element.47), channel_id=1, source_target_pairs={{0,2},{1,3},{2,0},{3,1},{4,6},{5,7},{6,4},{7,5}} | collective-permute-start | bytes 7077896 | tf_op jit(solution)/shard_map/ppermute | solution.py:533
  54.1 64.0 %collective-permute-start.3 = (f32[16,128]{1,0:T(8,128)}, f32[16,128]{1,0:T(8,128)S(1)}, u32[]{:S(2)}, u32[]{:S(2)}) collective-permute-start(f32[16,128]{1,0:T(8,128)} %get-tuple-element.42.k_ref), channel_id=1, source_target_pairs={{0,2},{1,3},{2,0},{3,1},{4,6},{5,7},{6,4},{7,5}} | collective-permute-start | bytes 24584 | tf_op jit(solution)/shard_map/ppermute | solution.py:586
  69.1 39.6 %copy-start.1 = (f32[576,1024]{1,0:T(8,128)}, f32[576,1024]{1,0:T(8,128)S(1)}, u32[]{:S(2)}) copy-start(f32[576,1024]{1,0:T(8,128)S(1)} %collective-permute-done.a_ref) | copy-start | bytes 7077892
  69.1 39.6 %collective-permute-start.1 = (f32[576,1024]{1,0:T(8,128)S(1)}, f32[576,1024]{1,0:T(8,128)}, u32[]{:S(2)}, u32[]{:S(2)}) collective-permute-start(f32[576,1024]{1,0:T(8,128)S(1)} %collective-permute-done.a_ref), channel_id=1, source_target_pairs={{0,1},{1,0},{2,3},{3,2},{4,5},{5,4},{6,7},{7,6}} | collective-permute-start | bytes 7077896 | tf_op jit(solution)/shard_map/ppermute | solution.py:534
  118.1 0.6 copy-start.7
  118.6 47.9 %copy-start = (f32[576,1024]{1,0:T(8,128)S(1)}, f32[576,1024]{1,0:T(8,128)}, u32[]{:S(2)}) copy-start(f32[576,1024]{1,0:T(8,128)} %get-tuple-element.48.a_ref) | copy-start | bytes 7077892
  166.1 64.5 %collective-permute-start.4 = (f32[144,12288]{1,0:T(8,128)}, f32[144,12288]{1,0:T(8,128)}, u32[]{:S(2)}, u32[]{:S(2)}) collective-permute-start(f32[144,12288]{1,0:T(8,128)} %get-tuple-element.60), channel_id=1, source_target_pairs={{0,1},{1,0},{2,3},{3,2},{4,5},{5,4},{6,7},{7,6}} | collective-permute-start | bytes 21233672 | tf_op jit(solution)/shard_map/ppermute | solution.py:616
  166.5 53.4 %collective-permute-start.2 = (f32[576,1024]{1,0:T(8,128)S(1)}, f32[576,1024]{1,0:T(8,128)}, u32[]{:S(2)}, u32[]{:S(2)}) collective-permute-start(f32[576,1024]{1,0:T(8,128)S(1)} %copy-done), channel_id=1, source_target_pairs={{0,4},{4,0},{1,5},{5,1},{2,6},{6,2},{3,7},{7,3}} | collective-permute-start | bytes 7077896 | tf_op jit(solution)/shard_map/ppermute | solution.py:604
  168.1 10.4 %collective-permute-start.5 = (f32[144,1024]{1,0:T(8,128)}, f32[144,1024]{1,0:T(8,128)S(1)}, u32[]{:S(2)}, u32[]{:S(2)}) collective-permute-start(f32[144,1024]{1,0:T(8,128)} %get-tuple-element.62), channel_id=1, source_target_pairs={{0,1},{1,0},{2,3},{3,2},{4,5},{5,4},{6,7},{7,6}} | collective-permute-start | bytes 1769480 | tf_op jit(solution)/shard_map/ppermute | solution.py:590
  168.1 16.4 %collective-permute-start.6 = (f32[144,1024]{1,0:T(8,128)}, f32[144,1024]{1,0:T(8,128)S(1)}, u32[]{:S(2)}, u32[]{:S(2)}) collective-permute-start(f32[144,1024]{1,0:T(8,128)} %get-tuple-element.63), channel_id=1, source_target_pairs={{0,2},{1,3},{2,0},{3,1},{4,6},{5,7},{6,4},{7,5}} | collective-permute-start | bytes 1769480 | tf_op jit(solution)/shard_map/ppermute | solution.py:590
  168.6 27.6 %collective-permute-start.7 = (f32[144,1024]{1,0:T(8,128)}, f32[144,1024]{1,0:T(8,128)S(1)}, u32[]{:S(2)}, u32[]{:S(2)}) collective-permute-start(f32[144,1024]{1,0:T(8,128)} %get-tuple-element.64), channel_id=1, source_target_pairs={{0,3},{1,2},{2,1},{3,0},{4,7},{5,6},{6,5},{7,4}} | collective-permute-start | bytes 1769480 | tf_op jit(solution)/shard_map/ppermute | solution.py:590
  178.5 17.7 %copy-start.2 = (f32[144,1024]{1,0:T(8,128)}, f32[144,1024]{1,0:T(8,128)S(1)}, u32[]{:S(2)}) copy-start(f32[144,1024]{1,0:T(8,128)S(1)} %collective-permute-done.5.g2) | copy-start | bytes 1769476
  184.5 11.7 %copy-start.3 = (f32[144,1024]{1,0:T(8,128)}, f32[144,1024]{1,0:T(8,128)S(1)}, u32[]{:S(2)}) copy-start(f32[144,1024]{1,0:T(8,128)S(1)} %collective-permute-done.6.g3) | copy-start | bytes 1769476
  196.2 0.8 copy-start.4
  230.6 10.1 %copy-start.8 = (f32[1,128]{1,0:T(1,128)S(1)}, f32[1,128]{1,0:T(1,128)}, u32[]{:S(2)}) copy-start(f32[1,128]{1,0:T(1,128)} %get-tuple-element.51) | copy-start | bytes 1540
  230.6 10.1 %copy-start.5 = (bf16[576,1024]{1,0:T(8,128)(2,1)S(1)}, bf16[576,1024]{1,0:T(8,128)(2,1)}, u32[]{:S(2)}) copy-start(bf16[576,1024]{1,0:T(8,128)(2,1)} %get-tuple-element.52) | copy-start | bytes 3538948
  240.6 1.1 copy-start.6
